TPU v7x, 512 devices: a whole 4x4x16 slice. The times are simulated.
512 devices in a mesh: seq: 128 (over x, z, core), hid: 4 (over y).
Axes of the slice: x: 4, y: 4, z: 16, core: 2. Of those that a mesh axis runs over, the one named last changes fastest.
Arguments:
- hidden: bfloat16 [131072, 4096], P('seq', 'hid'), may hold values from -40 to 40, as said below
- seg_ids: int32 [131072], P('seq'), may hold values from 0 to 511, as said below
- lengths: int32 [512], replicated, may hold values from 64 to 16384, as said below
- owner_slot: int32 [512], replicated, may hold values from 0 to 511, each once
- pool_bias: float32 [4096], P('hid'), may hold values from -3 to 3
Outputs:
- pooled: bfloat16 [512, 4096], P('seq', 'hid')
Inputs may be any that keep to these rules, and one draw needn't show every extreme that they name: `hidden`: float values; each feature's scale differs. `seg_ids`: never falls along the stream; document d occupies exactly lengths[d] consecutive tokens, documents in order. `lengths`: they sum to 131072; one of them is exactly 16384; the first 16 documents each have 1024 // 16 tokens and so fill the first index's tokens; hence at most 16 documents end within one index's tokens, and the first index has exactly 16. `owner_slot`: each row number once.
All inputs are finite; a program needn't handle non-finite values.
Results may differ from a plain program's by a relative error of at most 0.001.
Values may be sent and summed in bfloat16 or wider, within the bound.
No kernel may reach another device: no remote copies, remote signals or barrier semaphores. Data moves between devices by JAX's collectives and lax.ppermute only.
A program may use at most 64 MiB of HBM per device.

v0:
```python
import jax
import jax.numpy as jnp
from jax import lax
from jax.sharding import Mesh
from jax.sharding import PartitionSpec as P

SEQ = ("seq_0", "seq_1", "seq_2")


def cut_along(array, dim, count):
    dims = array.shape
    pieces = array.reshape(*dims[:dim], count, dims[dim] // count, *dims[dim + 1 :])
    return jnp.moveaxis(pieces, dim, 0)


def summed_on_arrival(array, axis, dim):
    pieces = cut_along(array, dim, lax.axis_size(axis))
    arrived = lax.all_to_all(pieces, axis, split_axis=0, concat_axis=0, tiled=True)
    return arrived.sum(axis=0)


def sum_in_two_steps(array, axes, dim):
    far, near = axes
    pieces = cut_along(array, dim, lax.axis_size(far))
    nearer = summed_on_arrival(pieces, near, dim + 1)
    arrived = lax.all_to_all(nearer, far, split_axis=0, concat_axis=0, tiled=True)
    return arrived.sum(axis=0)


def sent_to_all(array, axis):
    copies = jnp.broadcast_to(array, (lax.axis_size(axis), *array.shape))
    return lax.all_to_all(copies, axis, split_axis=0, concat_axis=0, tiled=True)


def of_everyone(array, axis):
    return sent_to_all(array, axis).sum(axis=0)


def local(hidden, seg_ids, lengths, owner_slot, pool_bias):
    tok_rows, width_part = hidden.shape
    doc_count = lengths.shape[0]
    seq_count = lax.axis_size(SEQ)
    per_owner = doc_count // seq_count
    features = width_part * lax.axis_size("hid")
    doc_iota = lax.broadcasted_iota(jnp.int32, (1, doc_count), 1)
    in_doc = (seg_ids[:, None] == doc_iota).astype(jnp.int32)
    token_row = jnp.sum(in_doc * owner_slot[None, :], axis=1)
    row_iota = lax.broadcasted_iota(jnp.int32, (doc_count, 1), 0)
    routed = (owner_slot[None, :] == row_iota).astype(jnp.int32)
    row_length = jnp.sum(routed * lengths[None, :], axis=1).astype(jnp.float32)
    wanted = lax.broadcasted_iota(jnp.int32, (per_owner * lax.axis_size(SEQ), 1), 0)
    picker = (wanted == token_row[None, :]).astype(jnp.bfloat16)
    totals = sum_in_two_steps(
        jnp.dot(picker, hidden, preferred_element_type=jnp.float32),
        (("seq_0", "seq_1"), "seq_2"),
        0,
    )
    my_length = lax.dynamic_slice_in_dim(row_length, lax.axis_index(SEQ) * per_owner, per_owner)
    averages = totals / my_length[:, None] + pool_bias[None, :]
    energy = of_everyone(jnp.sum(averages * averages, axis=1), "hid")
    return (averages * lax.rsqrt(energy / features + 1e-06)[:, None]).astype(jnp.bfloat16)


def solution(mesh):
    torus = Mesh(
        mesh.devices.reshape(4, 16, 2, mesh.shape["hid"]), ("seq_0", "seq_1", "seq_2", "hid")
    )
    return jax.shard_map(
        local,
        mesh=torus,
        in_specs=(P(SEQ, "hid"), P(SEQ), P(), P(), P("hid")),
        out_specs=P(SEQ, "hid"),
        check_vma=False,
    )
```

profile of v0, /device:TPU:6, one launch (start us, length us, event | category | flops | bytes accessed | tf_op | source)
XLA Modules:
  0.0 102.4 jit_solution(4438978463942110891)
XLA Ops:
  0.0 0.0 copy-start
  0.0 1.3 %select_reduce_fusion = s32[1024]{0:T(1024)S(1)} fusion(s32[512]{0:T(512)} %param.8, s32[1024]{0:T(1024)} %param.6), kind=kLoop, calls=%fused_computation.1 | loop fusion | flops 1571840 | bytes 10240 | tf_op jit(solution)/shard_map/reduce_sum | solution.py:47
  1.3 0.3 copy-done
  1.6 2.6 %fusion = f32[512,1024]{1,0:T(8,128)} fusion(bf16[1024,1024]{1,0:T(8,128)(2,1)S(1)} %copy-done, s32[1024]{0:T(1024)S(1)} %select_reduce_fusion), kind=kOutput, calls=%fused_computation.4 | convolution fusion | flops 1074266112 | bytes 4198400 | tf_op jit(solution)/shard_map/dot_general | solution.py:54
  4.2 2.8 %reshape_reshape.3 = f32[64,2,4,1024]{3,2,1,0:T(4,128)} reshape(f32[512,1024]{1,0:T(8,128)} %fusion) | data formatting | bytes 4194304 | tf_op jit(solution)/shard_map/reshape;reshape | solution.py:12
  7.1 1.8 %copy.13 = f32[64,2,4,1024]{3,2,0,1:T(4,128)S(1)} copy(f32[64,2,4,1024]{3,2,1,0:T(4,128)} %reshape_reshape.3) | data formatting | bytes 4194304 | tf_op jit(solution)/shard_map/reshape;reshape | solution.py:12
  8.8 6.3 %all_to_all.16 = f32[2,64,4,1024]{3,2,1,0:T(4,128)} all-to-all(f32[2,64,4,1024]{3,2,1,0:T(4,128)S(1)} %bitcast.5), channel_id=1, replica_groups=mesh['seq_0'=4,'seq_1'=16,'seq_2'=2,'hid'=4] {'seq_2'}, dimensions={0} | all-to-all | bytes 4194304 | tf_op jit(solution)/shard_map/all_to_all | solution.py:18
  15.1 0.0 copy-start.1
  15.1 0.0 copy-start.3
  15.1 3.5 %reduce_sum.55 = f32[64,4,1024]{2,1,0:T(4,128)} reduce(f32[2,64,4,1024]{3,2,1,0:T(4,128)} %all_to_all.16, f32[]{:T(128)} %constant.10.clone.1), dimensions={0}, to_apply=%region_1.0 | reduce | flops 262144 | bytes 3145732 | tf_op jit(solution)/shard_map/reduce_sum | solution.py:19
  18.7 0.0 copy-start.2
  18.7 18.9 %all-to-all-start.1 = ((f32[64,4,1024]{2,1,0:T(4,128)}), f32[64,4,1024]{2,1,0:T(4,128)S(1)}, u32[]{:S(2)}, u32[]{:S(2)}) async-start(f32[64,4,1024]{2,1,0:T(4,128)} %reduce_sum.55), calls=%async_computation.1 | async-start | bytes 2097152 | tf_op jit(solution)/shard_map/all_to_all | solution.py:26
  37.6 0.0 copy-done.1
  37.6 0.0 copy-done.3
  37.6 0.2 select_reduce_fusion.1
  37.8 0.1 dynamic_slice.3
  37.9 53.8 %all-to-all-done.1 = f32[64,4,1024]{2,1,0:T(4,128)S(1)} async-done(((f32[64,4,1024]{2,1,0:T(4,128)}), f32[64,4,1024]{2,1,0:T(4,128)S(1)}, u32[]{:S(2)}, u32[]{:S(2)}) %all-to-all-start.1) | async-done | bytes 1048608 | tf_op jit(solution)/shard_map/all_to_all | solution.py:26
  91.8 0.2 reduce_sum.56
  92.0 0.0 copy-done.2
  92.0 0.2 multiply_reduce_fusion
  92.2 9.5 %all_to_all.17 = f32[4,1,4]{2,1,0:T(1,128)S(1)} all-to-all(f32[4,1,4]{2,1,0:T(1,128)S(1)} %broadcast_in_dim.2), channel_id=1, replica_groups=mesh['seq_0'=4,'seq_1'=16,'seq_2'=2,'hid'=4] {'hid'}, dimensions={0} | all-to-all | bytes 128 | tf_op jit(solution)/shard_map/all_to_all | solution.py:32
  101.7 0.7 multiply_convert_fusion
  (4 shorter events, 0.0 us)
Async XLA Ops:
  0.0 1.6 %copy-start = (bf16[1024,1024]{1,0:T(8,128)(2,1)S(1)}, bf16[1024,1024]{1,0:T(8,128)(2,1)}, u32[]{:S(2)}) copy-start(bf16[1024,1024]{1,0:T(8,128)(2,1)} %param.5) | copy-start | bytes 6291460
  15.1 22.5 %copy-start.1 = (s32[512]{0:T(512)S(1)}, s32[512]{0:T(512)}, u32[]{:S(2)}) copy-start(s32[512]{0:T(512)} %param.8) | copy-start | bytes 6148
  15.1 22.5 %copy-start.3 = (s32[512]{0:T(512)S(1)}, s32[512]{0:T(512)}, u32[]{:S(2)}) copy-start(s32[512]{0:T(512)} %param.7) | copy-start | bytes 6148
  18.7 73.3 %copy-start.2 = (f32[1024]{0:T(1024)S(1)}, f32[1024]{0:T(1024)}, u32[]{:S(2)}) copy-start(f32[1024]{0:T(1024)} %param.9) | copy-start | bytes 12292
  18.7 73.1 %all-to-all-start.1 = ((f32[64,4,1024]{2,1,0:T(4,128)}), f32[64,4,1024]{2,1,0:T(4,128)S(1)}, u32[]{:S(2)}, u32[]{:S(2)}) async-start(f32[64,4,1024]{2,1,0:T(4,128)} %reduce_sum.55), calls=%async_computation.1 | async-start | bytes 2097152 | tf_op jit(solution)/shard_map/all_to_all | solution.py:26
where the time goes:
time: 103 us; the launch traced here: 102 us
  waiting for transfers between devices  53.8 us (52%)
  starting transfers between devices  18.9 us (18%)
  blocking collectives  15.9 us (15%)
  other arithmetic  6.15 us (6%)
  local copies, waits for them, and re-layouts  4.98 us (5%)
  matrix products  2.6 us (3%)
    all_to_all x1, waiting for transfers between devices, sum_in_two_steps(): lax.all_to_all(nearer, far, split_axis=0, concat_axis=0, tiled=True)  53.8 us
    all_to_all x1, starting transfers between devices, sum_in_two_steps(): lax.all_to_all(nearer, far, split_axis=0, concat_axis=0, tiled=True)  18.9 us
    all_to_all x1, blocking collectives, sent_to_all(): return lax.all_to_all(copies, axis, split_axis=0, concat_axis=0, tiled=True)  9.55 us
    all_to_all x1, blocking collectives, summed_on_arrival(): lax.all_to_all(pieces, axis, split_axis=0, concat_axis=0, tiled=True)  6.31 us
    another operation x2, local copies, waits for them, and re-layouts, cut_along(): array.reshape(*dims[:dim], count, dims[dim] // count, *dims[dim + 1:])  4.59 us
    reduce_sum x1, other arithmetic, summed_on_arrival(): return arrived.sum(axis=0)  3.54 us
    dot_general x1, matrix products, local(): jnp.dot(picker, hidden, preferred_element_type=jnp.float32)  2.6 us
  transfers between devices with their start and end apart: 1, of which 1 were waited for; matrix products, arithmetic and copies ran while one was open for 0% of the time, Pallas kernels for 0%

commit v1 on v0

v1 whole, which is shorter than its diff:
```python
import functools

import jax
import jax.numpy as jnp
from jax import lax
from jax.experimental import pallas as pl
from jax.experimental.pallas import tpu as pltpu
from jax.sharding import Mesh
from jax.sharding import PartitionSpec as P

USED = 17
SLOTS = 24
LANES = 128


def plane_row(owner):
    return ((owner >> 3) & 15) * 32 + (owner >> 7) * 8 + (owner & 7)


def sums_kernel(steps, chunks, seg_ref, owner_ref, hidden_ref, out_ref):
    step = pl.program_id(0)
    first = seg_ref[0:1, 0:1]
    rows = hidden_ref.shape[0]
    seg = seg_ref[:, pl.ds(pl.multiple_of(step * rows, rows), rows)]
    slot = lax.broadcasted_iota(jnp.int32, (SLOTS, rows), 0)
    picker = jnp.where(slot == seg - first, 1.0, 0.0).astype(jnp.bfloat16)
    sums = jnp.dot(picker, hidden_ref[...], preferred_element_type=jnp.float32)

    @pl.when(step == 0)
    def _():
        docs = owner_ref.shape[1]
        source = lax.axis_index("x") * 2 + lax.axis_index("c")
        row = plane_row(owner_ref[...]) + 1
        part = lax.broadcasted_iota(jnp.int32, (8, docs), 0)
        digits = jnp.where(part == 0, row >> 5, jnp.where(part == 1, row & 31, 0))
        lane = lax.broadcasted_iota(jnp.int32, (docs, 2 * LANES), 1) - source * SLOTS
        doc = lax.broadcasted_iota(jnp.int32, (docs, 2 * LANES), 0)
        meets = (doc == first + lane) & (lane >= 0) & (lane < USED)
        found = jnp.dot(
            digits.astype(jnp.float32).astype(jnp.bfloat16),
            jnp.where(meets, 1.0, 0.0).astype(jnp.bfloat16),
            preferred_element_type=jnp.float32,
        )
        where = found[0:1, :] * 32.0 + found[1:2, :]
        line = lax.broadcasted_iota(jnp.int32, (SLOTS, LANES), 0)
        marks = jnp.where(
            line == SLOTS - 2,
            where[:, :LANES],
            jnp.where(line == SLOTS - 1, where[:, LANES:], 0.0),
        )
        for c in range(chunks):
            out_ref[c] = sums[:, c * LANES : (c + 1) * LANES] + marks

    @pl.when(step > 0)
    def _():
        for c in range(chunks):
            out_ref[c] += sums[:, c * LANES : (c + 1) * LANES]


def local_sums(seg_ids, owner_slot, hidden, chunks):
    tokens, width = hidden.shape
    steps = 4
    rows = tokens // steps
    return pl.pallas_call(
        functools.partial(sums_kernel, steps, chunks),
        grid=(steps,),
        in_specs=[
            pl.BlockSpec((1, tokens), lambda i: (0, 0)),
            pl.BlockSpec((1, owner_slot.shape[0]), lambda i: (0, 0)),
            pl.BlockSpec((rows, width), lambda i: (i, 0)),
        ],
        out_specs=pl.BlockSpec((chunks, SLOTS, LANES), lambda i: (0, 0, 0)),
        out_shape=jax.ShapeDtypeStruct((chunks, SLOTS, LANES), jnp.float32),
        name="local_sums",
    )(seg_ids.reshape(1, -1), owner_slot.reshape(1, -1), hidden)


def place_kernel(in_ref, out_ref):
    sources = in_ref.shape[0]
    planes, per_plane, _ = out_ref.shape
    slots = in_ref[...].reshape(sources * SLOTS, LANES)
    where = jnp.sum(in_ref[:, SLOTS - 2 : SLOTS, :], axis=0).astype(jnp.int32)
    row = lax.broadcasted_iota(jnp.int32, (planes * per_plane, LANES), 0) + 1
    rest = sources * SLOTS - LANES
    left = jnp.where(row == where[0:1, :], 1.0, 0.0).astype(jnp.bfloat16)
    right = jnp.where(row == where[1:2, :], 1.0, 0.0).astype(jnp.bfloat16)
    picker = jnp.concatenate([left, right], axis=1)
    total = jnp.concatenate([slots, jnp.zeros((LANES - rest, LANES), jnp.float32)], axis=0)
    high = total.astype(jnp.bfloat16)
    left_over = total - high.astype(jnp.float32)
    middle = left_over.astype(jnp.bfloat16)
    low = (left_over - middle.astype(jnp.float32)).astype(jnp.bfloat16)
    placed = jnp.dot(
        picker, jnp.concatenate([high, middle, low], axis=1), preferred_element_type=jnp.float32
    )
    whole = placed[:, :LANES] + (placed[:, LANES : 2 * LANES] + placed[:, 2 * LANES :])
    out_ref[...] = whole.reshape(out_ref.shape)


def place(slots, planes, per_plane):
    return pl.pallas_call(
        place_kernel,
        out_shape=jax.ShapeDtypeStruct((planes, per_plane, LANES), jnp.float32),
        name="place",
    )(slots)


def average_kernel(owner_ref, length_ref, bias_ref, in_ref, out_ref):
    per_plane = in_ref.shape[1]
    total = jnp.sum(in_ref[...], axis=0)
    mine = lax.axis_index("z") * per_plane
    row = lax.broadcasted_iota(jnp.int32, (per_plane, owner_ref.shape[1]), 0) + mine
    length = jnp.sum(
        jnp.where(row == plane_row(owner_ref[...]), length_ref[...], 0).astype(jnp.float32),
        axis=1,
        keepdims=True,
    )
    chunk = lax.axis_index("x") * 2 + lax.axis_index("c")
    average = total / length + bias_ref[pl.ds(chunk, 1), :]
    owners, copies, rows, _ = out_ref.shape
    for o in range(owners):
        for y in range(copies):
            out_ref[o, y] = average[o * rows : (o + 1) * rows, :]


def averages_for_owners(arrived, owner_slot, lengths, pool_bias, owners, copies):
    rows = arrived.shape[1] // owners
    return pl.pallas_call(
        average_kernel,
        out_shape=jax.ShapeDtypeStruct((owners, copies, rows, LANES), jnp.float32),
        name="average",
    )(owner_slot.reshape(1, -1), lengths.reshape(1, -1), pool_bias.reshape(-1, LANES), arrived)


def norm_kernel(in_ref, out_ref):
    chunks, slices, rows, _ = in_ref.shape
    every = in_ref[...]
    square = jnp.sum(every * every, axis=(0, 1))
    energy = jnp.sum(square, axis=1, keepdims=True) / (chunks * slices * LANES)
    scale = lax.rsqrt(energy + 1e-06)
    mine = lax.axis_index("y")
    for c in range(chunks):
        out_ref[:, c * LANES : (c + 1) * LANES] = (in_ref[c, mine] * scale).astype(jnp.bfloat16)


def normed(arrived):
    chunks, _, rows, _ = arrived.shape
    return pl.pallas_call(
        norm_kernel,
        out_shape=jax.ShapeDtypeStruct((rows, chunks * LANES), jnp.bfloat16),
        name="norm",
    )(arrived)


def swap(array, axes):
    return lax.all_to_all(array, axes, split_axis=0, concat_axis=0, tiled=True)


def local(hidden, seg_ids, lengths, owner_slot, pool_bias):
    chunks = lax.axis_size(("x", "c"))
    planes = lax.axis_size("z")
    slices = lax.axis_size("y")
    docs = lengths.shape[0]
    slots = swap(local_sums(seg_ids, owner_slot, hidden, chunks), ("x", "c"))
    rows = swap(place(slots, planes, docs // planes), "z")
    average = averages_for_owners(rows, owner_slot, lengths, pool_bias, chunks, slices)
    mine = swap(average.reshape(chunks * slices, -1, LANES), ("x", "c", "y"))
    return normed(mine.reshape(average.shape))


def solution(mesh):
    torus = Mesh(mesh.devices.reshape(4, 16, 2, mesh.shape["hid"]), ("x", "z", "c", "y"))
    seq = ("x", "z", "c")
    return jax.shard_map(
        local,
        mesh=torus,
        in_specs=(P(seq, "y"), P(seq), P(), P(), P("y")),
        out_specs=P(seq, "y"),
        check_vma=False,
    )
```

time: 103 us -> 67.3 us (0.65)
  the two profiles are of different devices: /device:TPU:6 before, /device:TPU:1 now
where the time goes in v1:
time: 67.3 us; the launch traced here: 66.9 us
  blocking collectives  58 us (86%)
  Pallas kernels  8.83 us (13%)
    all_to_all x3, blocking collectives, swap(): return lax.all_to_all(array, axes, split_axis=0, concat_axis=0, tiled=True)  58 us
    pallas_call x1, Pallas kernels, local_sums(): pl.pallas_call(functools.partial(sums_kernel, steps, chunks), grid=(steps...  3.67 us
    pallas_call x1, Pallas kernels, place(): pl.pallas_call(place_kernel, out_shape=jax.ShapeDtypeStruct((planes, per_...  1.89 us
    pallas_call x1, Pallas kernels, averages_for_owners(): pl.pallas_call(average_kernel, out_shape=jax.ShapeDtypeStruct((owners, co...  1.72 us
    pallas_call x1, Pallas kernels, normed(): pl.pallas_call(norm_kernel, out_shape=jax.ShapeDtypeStruct((rows, chunks...  1.56 us

profile of v1, /device:TPU:1, one launch (start us, length us, event | category | flops | bytes accessed | tf_op | source)
XLA Modules:
  0.0 66.9 jit_solution(15477344991184466340)
XLA Ops:
  0.0 3.7 %local_sums.1 = f32[8,24,128]{2,1,0:T(8,128)} custom-call(s32[1,1024]{1,0:T(1,128)} %bitcast.10, s32[1,512]{1,0:T(1,128)} %bitcast.8, bf16[1024,1024]{1,0:T(8,128)(2,1)} %hidden_ref.1), custom_call_target="tpu_custom_call" | custom-call | tf_op jit(solution)/shard_map/local_sums/pallas_call | solution.py:64
  3.7 15.8 %all_to_all.15.in_ref = f32[8,24,128]{2,1,0:T(8,128)} all-to-all(f32[8,24,128]{2,1,0:T(8,128)} %local_sums.1), channel_id=1, replica_groups=mesh['x'=4,'z'=16,'c'=2,'y'=4] {'x','c'}, dimensions={0} | all-to-all | bytes 196608 | tf_op jit(solution)/shard_map/all_to_all | solution.py:156
  19.4 1.9 %place.1 = f32[16,32,128]{2,1,0:T(8,128)} custom-call(f32[8,24,128]{2,1,0:T(8,128)} %all_to_all.15.in_ref), custom_call_target="tpu_custom_call" | custom-call | tf_op jit(solution)/shard_map/place/pallas_call | solution.py:101
  21.3 23.6 %all_to_all.16.in_ref = f32[16,32,128]{2,1,0:T(8,128)} all-to-all(f32[16,32,128]{2,1,0:T(8,128)} %place.1), channel_id=1, replica_groups=mesh['x'=4,'z'=16,'c'=2,'y'=4] {'z'}, dimensions={0} | all-to-all | bytes 524288 | tf_op jit(solution)/shard_map/all_to_all | solution.py:156
  44.9 1.7 %average.1 = f32[8,4,4,128]{3,2,1,0:T(4,128)} custom-call(s32[1,512]{1,0:T(1,128)} %bitcast.9, s32[1,512]{1,0:T(1,128)} %bitcast.12, f32[8,128]{1,0:T(8,128)} %bitcast.11, f32[16,32,128]{2,1,0:T(8,128)} %all_to_all.16.in_ref), custom_call_target="tpu_custom_call" | custom-call | tf_op jit(solution)/shard_map/average/pallas_call | solution.py:128
  46.6 18.7 %all_to_all.17 = f32[32,4,128]{2,1,0:T(4,128)} all-to-all(f32[32,4,128]{2,1,0:T(4,128)} %bitcast.7), channel_id=1, replica_groups=mesh['x'=4,'z'=16,'c'=2,'y'=4] {'x','c','y'}, dimensions={0} | all-to-all | bytes 131072 | tf_op jit(solution)/shard_map/all_to_all | solution.py:156
  65.3 1.6 %norm.1 = bf16[4,1024]{1,0:T(4,128)(2,1)} custom-call(f32[8,4,4,128]{3,2,1,0:T(4,128)} %bitcast.6), custom_call_target="tpu_custom_call" | custom-call | tf_op jit(solution)/shard_map/norm/pallas_call | solution.py:148

commit v2 on v1

--- a/solution.py
+++ b/solution.py
@@ -11,6 +11,7 @@
 USED = 17
 SLOTS = 24
 LANES = 128
+GRANT = 16 * 1024 * 1024
 
 
 def plane_row(owner):
@@ -71,6 +72,7 @@
         ],
         out_specs=pl.BlockSpec((chunks, SLOTS, LANES), lambda i: (0, 0, 0)),
         out_shape=jax.ShapeDtypeStruct((chunks, SLOTS, LANES), jnp.float32),
+        compiler_params=pltpu.CompilerParams(vmem_limit_bytes=GRANT),
         name="local_sums",
     )(seg_ids.reshape(1, -1), owner_slot.reshape(1, -1), hidden)
 
@@ -101,6 +103,7 @@
     return pl.pallas_call(
         place_kernel,
         out_shape=jax.ShapeDtypeStruct((planes, per_plane, LANES), jnp.float32),
+        compiler_params=pltpu.CompilerParams(vmem_limit_bytes=GRANT),
         name="place",
     )(slots)
 
@@ -128,6 +131,7 @@
     return pl.pallas_call(
         average_kernel,
         out_shape=jax.ShapeDtypeStruct((owners, copies, rows, LANES), jnp.float32),
+        compiler_params=pltpu.CompilerParams(vmem_limit_bytes=GRANT),
         name="average",
     )(owner_slot.reshape(1, -1), lengths.reshape(1, -1), pool_bias.reshape(-1, LANES), arrived)
 
@@ -148,6 +152,7 @@
     return pl.pallas_call(
         norm_kernel,
         out_shape=jax.ShapeDtypeStruct((rows, chunks * LANES), jnp.bfloat16),
+        compiler_params=pltpu.CompilerParams(vmem_limit_bytes=GRANT),
         name="norm",
     )(arrived)
 

time: 67.3 us -> 62.7 us (0.932)
  Pallas kernels: 8.83 us -> 2.3 us
  local copies, waits for them, and re-layouts: 0 us -> 2.98 us
  blocking collectives: 58 us -> 57.1 us
    unnamed x0 -> x12, local copies, waits for them, and re-layouts: none -> 2.98 us
    pallas_call x1, Pallas kernels: 3.67 us -> 1.17 us  [local_sums(): pl.pallas_call(functools.partial(sums_kernel, steps, chunks), grid=(steps...]
    pallas_call x1, Pallas kernels: 1.72 us -> 0.11 us  [averages_for_owners(): pl.pallas_call(average_kernel, out_shape=jax.ShapeDtypeStruct((owners, co...]
    pallas_call x1, Pallas kernels: 1.89 us -> 0.3 us  [place(): pl.pallas_call(place_kernel, out_shape=jax.ShapeDtypeStruct((planes, per_...]
    all_to_all x3, blocking collectives: 58 us -> 57.1 us  [swap(): return lax.all_to_all(array, axes, split_axis=0, concat_axis=0, tiled=True)]
    pallas_call x1, Pallas kernels: 1.56 us -> 0.72 us  [normed(): pl.pallas_call(norm_kernel, out_shape=jax.ShapeDtypeStruct((rows, chunks...]
where the time goes in v2:
time: 62.7 us; the launch traced here: 62.4 us
  blocking collectives  57.1 us (91%)
  local copies, waits for them, and re-layouts  2.98 us (5%)
  Pallas kernels  2.3 us (4%)
    all_to_all x3, blocking collectives, swap(): return lax.all_to_all(array, axes, split_axis=0, concat_axis=0, tiled=True)  57.1 us
    unnamed x12, local copies, waits for them, and re-layouts  2.98 us

profile of v2, /device:TPU:1, one launch (start us, length us, event | category | flops | bytes accessed | tf_op | source)
XLA Modules:
  0.0 62.4 jit_solution(3180466110039501303)
XLA Ops:
  0.0 0.0 copy-start.2
  0.0 0.0 copy-start
  0.0 1.6 %copy-done = bf16[1024,1024]{1,0:T(8,128)(2,1)S(1)} copy-done((bf16[1024,1024]{1,0:T(8,128)(2,1)S(1)}, bf16[1024,1024]{1,0:T(8,128)(2,1)}, u32[]{:S(2)}) %copy-start) | copy-done | bytes 2097176
  1.6 0.0 copy-start.1
  1.6 0.7 %copy-done.1 = s32[512]{0:T(512)S(1)} copy-done((s32[512]{0:T(512)S(1)}, s32[512]{0:T(512)}, u32[]{:S(2)}) %copy-start.1) | copy-done | bytes 2072
  2.3 0.0 copy-start.3
  2.3 0.7 %copy-done.3 = s32[1024]{0:T(1024)S(1)} copy-done((s32[1024]{0:T(1024)S(1)}, s32[1024]{0:T(1024)}, u32[]{:S(2)}) %copy-start.3) | copy-done | bytes 4120
  3.0 0.0 copy-start.4
  3.0 0.0 copy-start.5
  3.0 1.2 %local_sums.1 = f32[8,24,128]{2,1,0:T(8,128)S(1)} custom-call(s32[1,1024]{1,0:T(1,128)S(1)} %bitcast.10, s32[1,512]{1,0:T(1,128)S(1)} %bitcast.8, bf16[1024,1024]{1,0:T(8,128)(2,1)S(1)} %copy-done), custom_call_target="tpu_custom_call" | custom-call | tf_op jit(solution)/shard_map/local_sums/pallas_call | solution.py:65
  4.2 14.2 %all_to_all.15.in_ref = f32[8,24,128]{2,1,0:T(8,128)S(1)} all-to-all(f32[8,24,128]{2,1,0:T(8,128)S(1)} %local_sums.1), channel_id=1, replica_groups=mesh['x'=4,'z'=16,'c'=2,'y'=4] {'x','c'}, dimensions={0} | all-to-all | bytes 196608 | tf_op jit(solution)/shard_map/all_to_all | solution.py:161
  18.4 0.3 place.1
  18.7 24.5 %all_to_all.16.in_ref = f32[16,32,128]{2,1,0:T(8,128)S(1)} all-to-all(f32[16,32,128]{2,1,0:T(8,128)S(1)} %place.1), channel_id=1, replica_groups=mesh['x'=4,'z'=16,'c'=2,'y'=4] {'z'}, dimensions={0} | all-to-all | bytes 524288 | tf_op jit(solution)/shard_map/all_to_all | solution.py:161
  43.2 0.0 copy-done.2
  43.2 0.0 copy-done.4
  43.2 0.0 copy-done.5
  43.2 0.1 average.1
  43.3 18.4 %all_to_all.17 = f32[32,4,128]{2,1,0:T(4,128)S(1)} all-to-all(f32[32,4,128]{2,1,0:T(4,128)S(1)} %bitcast.7), channel_id=1, replica_groups=mesh['x'=4,'z'=16,'c'=2,'y'=4] {'x','c','y'}, dimensions={0} | all-to-all | bytes 131072 | tf_op jit(solution)/shard_map/all_to_all | solution.py:161
  61.7 0.7 %norm.1 = bf16[4,1024]{1,0:T(4,128)(2,1)} custom-call(f32[8,4,4,128]{3,2,1,0:T(4,128)S(1)} %bitcast.6), custom_call_target="tpu_custom_call" | custom-call | tf_op jit(solution)/shard_map/norm/pallas_call | solution.py:152
Async XLA Ops:
  0.0 43.2 %copy-start.2 = (s32[512]{0:T(512)S(1)}, s32[512]{0:T(512)}, u32[]{:S(2)}) copy-start(s32[512]{0:T(512)} %param.8) | copy-start | bytes 6148
  0.0 1.6 %copy-start = (bf16[1024,1024]{1,0:T(8,128)(2,1)S(1)}, bf16[1024,1024]{1,0:T(8,128)(2,1)}, u32[]{:S(2)}) copy-start(bf16[1024,1024]{1,0:T(8,128)(2,1)} %hidden_ref.1) | copy-start | bytes 6291460
  1.6 0.7 %copy-start.1 = (s32[512]{0:T(512)S(1)}, s32[512]{0:T(512)}, u32[]{:S(2)}) copy-start(s32[512]{0:T(512)} %param.8) | copy-start | bytes 6148
  2.3 0.7 %copy-start.3 = (s32[1024]{0:T(1024)S(1)}, s32[1024]{0:T(1024)}, u32[]{:S(2)}) copy-start(s32[1024]{0:T(1024)} %param.6) | copy-start | bytes 12292
  3.0 40.2 %copy-start.4 = (f32[1024]{0:T(1024)S(1)}, f32[1024]{0:T(1024)}, u32[]{:S(2)}) copy-start(f32[1024]{0:T(1024)} %param.9) | copy-start | bytes 12292
  3.0 40.2 %copy-start.5 = (s32[512]{0:T(512)S(1)}, s32[512]{0:T(512)}, u32[]{:S(2)}) copy-start(s32[512]{0:T(512)} %param.7) | copy-start | bytes 6148

commit v3 on v2

--- a/solution.py
+++ b/solution.py
@@ -12,67 +12,80 @@
 SLOTS = 24
 LANES = 128
 GRANT = 16 * 1024 * 1024
+WIDE = 53 * 1024 * 1024
 
 
 def plane_row(owner):
     return ((owner >> 3) & 15) * 32 + (owner >> 7) * 8 + (owner & 7)
 
 
-def sums_kernel(steps, chunks, seg_ref, owner_ref, hidden_ref, out_ref):
-    step = pl.program_id(0)
-    first = seg_ref[0:1, 0:1]
-    rows = hidden_ref.shape[0]
-    seg = seg_ref[:, pl.ds(pl.multiple_of(step * rows, rows), rows)]
-    slot = lax.broadcasted_iota(jnp.int32, (SLOTS, rows), 0)
-    picker = jnp.where(slot == seg - first, 1.0, 0.0).astype(jnp.bfloat16)
-    sums = jnp.dot(picker, hidden_ref[...], preferred_element_type=jnp.float32)
+def marks_of(first, owner):
+    docs = owner.shape[1]
+    source = lax.axis_index("x") * 2 + lax.axis_index("c")
+    row = plane_row(owner) + 1
+    part = lax.broadcasted_iota(jnp.int32, (8, docs), 0)
+    digits = jnp.where(part == 0, row >> 5, jnp.where(part == 1, row & 31, 0))
+    lane = lax.broadcasted_iota(jnp.int32, (docs, 2 * LANES), 1) - source * SLOTS
+    doc = lax.broadcasted_iota(jnp.int32, (docs, 2 * LANES), 0)
+    meets = (doc == first + lane) & (lane >= 0) & (lane < USED)
+    found = jnp.dot(
+        digits.astype(jnp.float32).astype(jnp.bfloat16),
+        jnp.where(meets, 1.0, 0.0).astype(jnp.bfloat16),
+        preferred_element_type=jnp.float32,
+    )
+    where = found[0:1, :] * 32.0 + found[1:2, :]
+    line = lax.broadcasted_iota(jnp.int32, (SLOTS, LANES), 0)
+    second = jnp.where(line == SLOTS - 1, where[:, LANES:], 0.0)
+    return jnp.where(line == SLOTS - 2, where[:, :LANES], second)
 
-    @pl.when(step == 0)
-    def _():
-        docs = owner_ref.shape[1]
-        source = lax.axis_index("x") * 2 + lax.axis_index("c")
-        row = plane_row(owner_ref[...]) + 1
-        part = lax.broadcasted_iota(jnp.int32, (8, docs), 0)
-        digits = jnp.where(part == 0, row >> 5, jnp.where(part == 1, row & 31, 0))
-        lane = lax.broadcasted_iota(jnp.int32, (docs, 2 * LANES), 1) - source * SLOTS
-        doc = lax.broadcasted_iota(jnp.int32, (docs, 2 * LANES), 0)
-        meets = (doc == first + lane) & (lane >= 0) & (lane < USED)
-        found = jnp.dot(
-            digits.astype(jnp.float32).astype(jnp.bfloat16),
-            jnp.where(meets, 1.0, 0.0).astype(jnp.bfloat16),
+
+def sums_kernel(pieces, seg_hbm, owner_hbm, hidden_hbm, out_ref, seg, owner, hidden, sems):
+    tokens = hidden.shape[0]
+    rows = tokens // pieces
+    copies = [
+        pltpu.make_async_copy(seg_hbm, seg, sems.at[pieces]),
+        pltpu.make_async_copy(owner_hbm, owner, sems.at[pieces + 1]),
+    ]
+    for p in range(pieces):
+        here = pl.ds(p * rows, rows)
+        copies.append(pltpu.make_async_copy(hidden_hbm.at[here], hidden.at[here], sems.at[p]))
+    for copy in copies:
+        copy.start()
+    copies[0].wait()
+    first = seg[0:1, 0:1]
+    copies[1].wait()
+    marks = marks_of(first, owner[...])
+    slot = lax.broadcasted_iota(jnp.int32, (SLOTS, rows), 0) + first
+    sums = None
+    for p in range(pieces):
+        picker = jnp.where(slot == seg[:, p * rows : (p + 1) * rows], 1.0, 0.0)
+        copies[2 + p].wait()
+        term = jnp.dot(
+            picker.astype(jnp.bfloat16),
+            hidden[p * rows : (p + 1) * rows, :],
             preferred_element_type=jnp.float32,
         )
-        where = found[0:1, :] * 32.0 + found[1:2, :]
-        line = lax.broadcasted_iota(jnp.int32, (SLOTS, LANES), 0)
-        marks = jnp.where(
-            line == SLOTS - 2,
-            where[:, :LANES],
-            jnp.where(line == SLOTS - 1, where[:, LANES:], 0.0),
-        )
-        for c in range(chunks):
-            out_ref[c] = sums[:, c * LANES : (c + 1) * LANES] + marks
-
-    @pl.when(step > 0)
-    def _():
-        for c in range(chunks):
-            out_ref[c] += sums[:, c * LANES : (c + 1) * LANES]
+        sums = term if sums is None else sums + term
+    for c in range(out_ref.shape[0]):
+        out_ref[c] = sums[:, c * LANES : (c + 1) * LANES] + marks
 
 
 def local_sums(seg_ids, owner_slot, hidden, chunks):
     tokens, width = hidden.shape
-    steps = 4
-    rows = tokens // steps
+    docs = owner_slot.shape[0]
+    pieces = 4
     return pl.pallas_call(
-        functools.partial(sums_kernel, steps, chunks),
-        grid=(steps,),
-        in_specs=[
-            pl.BlockSpec((1, tokens), lambda i: (0, 0)),
-            pl.BlockSpec((1, owner_slot.shape[0]), lambda i: (0, 0)),
-            pl.BlockSpec((rows, width), lambda i: (i, 0)),
+        functools.partial(sums_kernel, pieces),
+        in_specs=[pl.BlockSpec(memory_space=pltpu.HBM)] * 3,
+        out_specs=pl.BlockSpec(memory_space=pltpu.VMEM),
+        out_shape=jax.ShapeDtypeStruct((chunks, SLOTS, LANES), jnp.float32),
+        scratch_shapes=[
+            pltpu.VMEM((1, tokens), jnp.int32),
+            pltpu.VMEM((1, docs), jnp.int32),
+            pltpu.VMEM((tokens, width), hidden.dtype),
+            pltpu.SemaphoreType.DMA((pieces + 2,)),
         ],
-        out_specs=pl.BlockSpec((chunks, SLOTS, LANES), lambda i: (0, 0, 0)),
-        out_shape=jax.ShapeDtypeStruct((chunks, SLOTS, LANES), jnp.float32),
-        compiler_params=pltpu.CompilerParams(vmem_limit_bytes=GRANT),
+        compiler_params=pltpu.CompilerParams(vmem_limit_bytes=WIDE),
         name="local_sums",
     )(seg_ids.reshape(1, -1), owner_slot.reshape(1, -1), hidden)
 

time: 62.7 us -> 62 us (0.989)
  local copies, waits for them, and re-layouts: 2.98 us -> 1.39 us
  Pallas kernels: 2.3 us -> 3.17 us
    unnamed x12 -> x8, local copies, waits for them, and re-layouts: 2.98 us -> 1.39 us
    pallas_call x1, Pallas kernels: 1.17 us -> 2.04 us  [local_sums(): pl.pallas_call(functools.partial(sums_kernel, pieces), in_specs=[pl.Block...]
where the time goes in v3:
time: 62 us; the launch traced here: 61.7 us
  blocking collectives  57.1 us (92%)
  Pallas kernels  3.17 us (5%)
  local copies, waits for them, and re-layouts  1.39 us (2%)
    all_to_all x3, blocking collectives, swap(): return lax.all_to_all(array, axes, split_axis=0, concat_axis=0, tiled=True)  57.1 us
    pallas_call x1, Pallas kernels, local_sums(): pl.pallas_call(functools.partial(sums_kernel, pieces), in_specs=[pl.Block...  2.04 us
    unnamed x8, local copies, waits for them, and re-layouts  1.39 us

profile of v3, /device:TPU:1, one launch (start us, length us, event | category | flops | bytes accessed | tf_op | source)
XLA Modules:
  0.0 61.7 jit_solution(434638679056032743)
XLA Ops:
  0.0 0.0 copy-start.3
  0.0 0.0 copy-start
  0.0 0.7 %copy-done = s32[512]{0:T(512)S(1)} copy-done((s32[512]{0:T(512)S(1)}, s32[512]{0:T(512)}, u32[]{:S(2)}) %copy-start) | copy-done | bytes 2072
  0.7 0.0 copy-start.1
  0.7 0.7 %copy-done.1 = s32[1024]{0:T(1024)S(1)} copy-done((s32[1024]{0:T(1024)S(1)}, s32[1024]{0:T(1024)}, u32[]{:S(2)}) %copy-start.1) | copy-done | bytes 4120
  1.4 0.0 copy-start.2
  1.4 2.0 %local_sums.1 = f32[8,24,128]{2,1,0:T(8,128)S(1)} custom-call(s32[1,1024]{1,0:T(1,128)S(1)} %bitcast.10, s32[1,512]{1,0:T(1,128)S(1)} %bitcast.8, bf16[1024,1024]{1,0:T(8,128)(2,1)} %hidden_hbm.1), custom_call_target="tpu_custom_call" | custom-call | tf_op jit(solution)/shard_map/local_sums/pallas_call | solution.py:77
  3.4 14.2 %all_to_all.15.in_ref = f32[8,24,128]{2,1,0:T(8,128)S(1)} all-to-all(f32[8,24,128]{2,1,0:T(8,128)S(1)} %local_sums.1), channel_id=1, replica_groups=mesh['x'=4,'z'=16,'c'=2,'y'=4] {'x','c'}, dimensions={0} | all-to-all | bytes 196608 | tf_op jit(solution)/shard_map/all_to_all | solution.py:174
  17.6 0.3 place.1
  17.9 24.5 %all_to_all.16.in_ref = f32[16,32,128]{2,1,0:T(8,128)S(1)} all-to-all(f32[16,32,128]{2,1,0:T(8,128)S(1)} %place.1), channel_id=1, replica_groups=mesh['x'=4,'z'=16,'c'=2,'y'=4] {'z'}, dimensions={0} | all-to-all | bytes 524288 | tf_op jit(solution)/shard_map/all_to_all | solution.py:174
  42.5 0.0 copy-done.3
  42.5 0.0 copy-done.2
  42.5 0.1 average.1
  42.6 18.4 %all_to_all.17 = f32[32,4,128]{2,1,0:T(4,128)S(1)} all-to-all(f32[32,4,128]{2,1,0:T(4,128)S(1)} %bitcast.7), channel_id=1, replica_groups=mesh['x'=4,'z'=16,'c'=2,'y'=4] {'x','c','y'}, dimensions={0} | all-to-all | bytes 131072 | tf_op jit(solution)/shard_map/all_to_all | solution.py:174
  61.0 0.7 %norm.1 = bf16[4,1024]{1,0:T(4,128)(2,1)} custom-call(f32[8,4,4,128]{3,2,1,0:T(4,128)S(1)} %bitcast.6), custom_call_target="tpu_custom_call" | custom-call | tf_op jit(solution)/shard_map/norm/pallas_call | solution.py:165
Async XLA Ops:
  0.0 42.5 %copy-start.3 = (s32[512]{0:T(512)S(1)}, s32[512]{0:T(512)}, u32[]{:S(2)}) copy-start(s32[512]{0:T(512)} %param.7) | copy-start | bytes 6148
  0.0 0.7 %copy-start = (s32[512]{0:T(512)S(1)}, s32[512]{0:T(512)}, u32[]{:S(2)}) copy-start(s32[512]{0:T(512)} %param.8) | copy-start | bytes 6148
  0.7 0.7 %copy-start.1 = (s32[1024]{0:T(1024)S(1)}, s32[1024]{0:T(1024)}, u32[]{:S(2)}) copy-start(s32[1024]{0:T(1024)} %param.6) | copy-start | bytes 12292
  1.4 41.1 %copy-start.2 = (f32[1024]{0:T(1024)S(1)}, f32[1024]{0:T(1024)}, u32[]{:S(2)}) copy-start(f32[1024]{0:T(1024)} %param.9) | copy-start | bytes 12292

commit v4 on v3

--- a/solution.py
+++ b/solution.py
@@ -12,7 +12,7 @@
 SLOTS = 24
 LANES = 128
 GRANT = 16 * 1024 * 1024
-WIDE = 53 * 1024 * 1024
+WIDE = 56 * 1024 * 1024
 
 
 def plane_row(owner):
@@ -78,7 +78,7 @@
         functools.partial(sums_kernel, pieces),
         in_specs=[pl.BlockSpec(memory_space=pltpu.HBM)] * 3,
         out_specs=pl.BlockSpec(memory_space=pltpu.VMEM),
-        out_shape=jax.ShapeDtypeStruct((chunks, SLOTS, LANES), jnp.float32),
+        out_shape=pltpu.VMEM((chunks, SLOTS, LANES), jnp.float32),
         scratch_shapes=[
             pltpu.VMEM((1, tokens), jnp.int32),
             pltpu.VMEM((1, docs), jnp.int32),

time: 62 us -> 60.6 us (0.977)
  local copies, waits for them, and re-layouts: 1.39 us -> 0.01 us
    unnamed x8 -> x6, local copies, waits for them, and re-layouts: 1.39 us -> 0.01 us
where the time goes in v4:
time: 60.6 us; the launch traced here: 60.4 us
  blocking collectives  57.1 us (94%)
  Pallas kernels  3.23 us (5%)
    all_to_all x3, blocking collectives, swap(): return lax.all_to_all(array, axes, split_axis=0, concat_axis=0, tiled=True)  57.1 us
    pallas_call x1, Pallas kernels, local_sums(): pl.pallas_call(functools.partial(sums_kernel, pieces), in_specs=[pl.Block...  2.1 us

profile of v4, /device:TPU:1, one launch (start us, length us, event | category | flops | bytes accessed | tf_op | source)
XLA Modules:
  0.0 60.4 jit_solution(9343223756958252233)
XLA Ops:
  0.0 0.0 copy-start
  0.0 0.0 copy-start.1
  0.0 0.0 copy-start.2
  0.0 2.1 %local_sums.1 = f32[8,24,128]{2,1,0:T(8,128)S(1)} custom-call(s32[1,1024]{1,0:T(1,128)} %bitcast.12, s32[1,512]{1,0:T(1,128)} %bitcast.8, bf16[1024,1024]{1,0:T(8,128)(2,1)} %hidden_hbm.1), custom_call_target="tpu_custom_call" | custom-call | tf_op jit(solution)/shard_map/local_sums/pallas_call | solution.py:77
  2.1 14.2 %all_to_all.15.in_ref = f32[8,24,128]{2,1,0:T(8,128)S(1)} all-to-all(f32[8,24,128]{2,1,0:T(8,128)S(1)} %local_sums.1), channel_id=1, replica_groups=mesh['x'=4,'z'=16,'c'=2,'y'=4] {'x','c'}, dimensions={0} | all-to-all | bytes 196608 | tf_op jit(solution)/shard_map/all_to_all | solution.py:174
  16.3 0.3 place.1
  16.6 24.5 %all_to_all.16.in_ref = f32[16,32,128]{2,1,0:T(8,128)S(1)} all-to-all(f32[16,32,128]{2,1,0:T(8,128)S(1)} %place.1), channel_id=1, replica_groups=mesh['x'=4,'z'=16,'c'=2,'y'=4] {'z'}, dimensions={0} | all-to-all | bytes 524288 | tf_op jit(solution)/shard_map/all_to_all | solution.py:174
  41.2 0.0 copy-done
  41.2 0.0 copy-done.1
  41.2 0.0 copy-done.2
  41.2 0.1 average.1
  41.3 18.4 %all_to_all.17 = f32[32,4,128]{2,1,0:T(4,128)S(1)} all-to-all(f32[32,4,128]{2,1,0:T(4,128)S(1)} %bitcast.7), channel_id=1, replica_groups=mesh['x'=4,'z'=16,'c'=2,'y'=4] {'x','c','y'}, dimensions={0} | all-to-all | bytes 131072 | tf_op jit(solution)/shard_map/all_to_all | solution.py:174
  59.7 0.7 %norm.1 = bf16[4,1024]{1,0:T(4,128)(2,1)} custom-call(f32[8,4,4,128]{3,2,1,0:T(4,128)S(1)} %bitcast.6), custom_call_target="tpu_custom_call" | custom-call | tf_op jit(solution)/shard_map/norm/pallas_call | solution.py:165
Async XLA Ops:
  0.0 41.2 %copy-start = (s32[512]{0:T(512)S(1)}, s32[512]{0:T(512)}, u32[]{:S(2)}) copy-start(s32[512]{0:T(512)} %param.8) | copy-start | bytes 6148
  0.0 41.2 %copy-start.1 = (f32[1024]{0:T(1024)S(1)}, f32[1024]{0:T(1024)}, u32[]{:S(2)}) copy-start(f32[1024]{0:T(1024)} %param.9) | copy-start | bytes 12292
  0.0 41.2 %copy-start.2 = (s32[512]{0:T(512)S(1)}, s32[512]{0:T(512)}, u32[]{:S(2)}) copy-start(s32[512]{0:T(512)} %param.7) | copy-start | bytes 6148

commit v5 on v4

v5 whole, which is shorter than its diff:
```python
import functools

import jax
import jax.numpy as jnp
from jax import lax
from jax.experimental import pallas as pl
from jax.experimental.pallas import tpu as pltpu
from jax.sharding import Mesh
from jax.sharding import PartitionSpec as P

USED = 17
SLOTS = 24
LANES = 128
FIT = 14
ROWS = 16
GRANT = 16 * 1024 * 1024
WIDE = 56 * 1024 * 1024


def plane_row(owner):
    return ((owner >> 3) & 15) * 32 + (owner >> 7) * 8 + (owner & 7)


def ones(mask):
    return jnp.where(mask, 1.0, 0.0).astype(jnp.bfloat16)


def iota(shape, dim):
    return lax.broadcasted_iota(jnp.int32, shape, dim)


def small(array):
    return array.astype(jnp.float32).astype(jnp.bfloat16)


def dot(left, right):
    return jnp.dot(left, right, preferred_element_type=jnp.float32)


def dot_rows(left, right):
    return lax.dot_general(
        left, right, (((1,), (1,)), ((), ())), preferred_element_type=jnp.float32
    )


def picked(picker, values):
    high = values.astype(jnp.bfloat16)
    left_over = values - high.astype(jnp.float32)
    middle = left_over.astype(jnp.bfloat16)
    low = (left_over - middle.astype(jnp.float32)).astype(jnp.bfloat16)
    parts = dot(picker, jnp.concatenate([high, middle, low], axis=1))
    return parts[:, :LANES] + (parts[:, LANES : 2 * LANES] + parts[:, 2 * LANES :])


def marks_of(first, last, owner):
    docs = owner.shape[1]
    source = lax.axis_index("x") * 2 + lax.axis_index("c")
    row = plane_row(owner) + 1
    part = iota((8, docs), 0)
    digits = jnp.where(part == 0, row >> 5, jnp.where(part == 1, row & 31, 0))
    lane = iota((docs, 2 * LANES), 1) - source * SLOTS
    doc = iota((docs, 2 * LANES), 0)
    meets = (doc == first + lane) & (doc <= last) & (lane >= 0) & (lane < USED)
    found = dot(small(digits), ones(meets))
    where = found[0:1, :] * 32.0 + found[1:2, :]
    line = iota((SLOTS, LANES), 0)
    second = jnp.where(line == SLOTS - 1, where[:, LANES:], 0.0)
    return jnp.where(line == SLOTS - 2, where[:, :LANES], second)


def most_rows(lengths, owner, tokens):
    docs = owner.shape[1]
    part = iota((8, docs), 0)
    digits = jnp.where(part == 0, lengths >> 7, jnp.where(part == 1, lengths & 127, 0))
    until = ones(iota((docs, docs), 0) <= iota((docs, docs), 1))
    sums = dot(small(digits), until)
    end = (sums[0:1, :] * 128.0 + sums[1:2, :]).astype(jnp.int32)
    start = end - lengths
    line = iota((LANES, docs), 0)
    device = (line >> 5) * 32 + (line & 15) * 2 + ((line >> 4) & 1)
    touches = (start < (device + 1) * tokens) & (end > device * tokens)
    owned = ((owner >> 3) & 15) == line
    counts = dot_rows(ones(touches), ones(owned))
    return jnp.max(jnp.sum(counts.reshape(8, 16, LANES), axis=0))


def sums_kernel(
    pieces, seg_hbm, owner_hbm, length_hbm, hidden_hbm, out_ref, seg, owner, length, hidden, sems
):
    tokens = hidden.shape[0]
    rows = tokens // pieces
    copies = [
        pltpu.make_async_copy(seg_hbm, seg, sems.at[pieces]),
        pltpu.make_async_copy(owner_hbm, owner, sems.at[pieces + 1]),
        pltpu.make_async_copy(length_hbm, length, sems.at[pieces + 2]),
    ]
    for p in range(pieces):
        here = pl.ds(p * rows, rows)
        copies.append(pltpu.make_async_copy(hidden_hbm.at[here], hidden.at[here], sems.at[p]))
    for copy in copies:
        copy.start()
    copies[0].wait()
    first = seg[0:1, 0:1]
    last = seg[0:1, tokens - 1 : tokens]
    copies[1].wait()
    marks = marks_of(first, last, owner[...])
    copies[2].wait()
    over = jnp.where(most_rows(length[...], owner[...], tokens) > FIT, 1.0, 0.0)
    marks = jnp.where((iota((SLOTS, LANES), 0) == SLOTS - 1) & (iota((SLOTS, LANES), 1) == LANES - 1), over, marks)
    slot = iota((SLOTS, rows), 0) + first
    sums = None
    for p in range(pieces):
        picker = ones(slot == seg[:, p * rows : (p + 1) * rows])
        copies[3 + p].wait()
        term = dot(picker, hidden[p * rows : (p + 1) * rows, :])
        sums = term if sums is None else sums + term
    for c in range(out_ref.shape[0]):
        out_ref[c] = sums[:, c * LANES : (c + 1) * LANES] + marks


def local_sums(seg_ids, owner_slot, lengths, hidden, chunks):
    tokens, width = hidden.shape
    docs = owner_slot.shape[0]
    pieces = 4
    return pl.pallas_call(
        functools.partial(sums_kernel, pieces),
        in_specs=[pl.BlockSpec(memory_space=pltpu.HBM)] * 4,
        out_specs=pl.BlockSpec(memory_space=pltpu.VMEM),
        out_shape=pltpu.VMEM((chunks, SLOTS, LANES), jnp.float32),
        scratch_shapes=[
            pltpu.VMEM((1, tokens), jnp.int32),
            pltpu.VMEM((1, docs), jnp.int32),
            pltpu.VMEM((1, docs), jnp.int32),
            pltpu.VMEM((tokens, width), hidden.dtype),
            pltpu.SemaphoreType.DMA((pieces + 3,)),
        ],
        compiler_params=pltpu.CompilerParams(vmem_limit_bytes=WIDE),
        name="local_sums",
    )(seg_ids.reshape(1, -1), owner_slot.reshape(1, -1), lengths.reshape(1, -1), hidden)


def slots_of(in_ref):
    sources = in_ref.shape[0]
    values = in_ref[...].reshape(sources * SLOTS, LANES)
    empty = jnp.zeros((2 * LANES - sources * SLOTS, LANES), jnp.float32)
    marks = jnp.sum(in_ref[:, SLOTS - 2 : SLOTS, :], axis=0).astype(jnp.int32)
    where = jnp.concatenate([marks[0:1, :], marks[1:2, :]], axis=1)
    where = jnp.where(iota(where.shape, 1) < sources * SLOTS, where, 0)
    plane = jnp.where(where > 0, (where - 1) >> 5, -1)
    bound = iota((16, 2 * LANES), 0) == plane
    ahead = iota((2 * LANES, 2 * LANES), 0) < iota((2 * LANES, 2 * LANES), 1)
    seen = dot(ones(bound), ones(ahead))
    rank = jnp.sum(jnp.where(bound, seen, 0.0), axis=0, keepdims=True).astype(jnp.int32)
    return jnp.concatenate([values, empty], axis=0), where, plane, bound, rank


def place_kernel(in_ref, out_ref, kept_ref, none_ref, over_ref):
    planes = out_ref.shape[0]
    kept_ref[...] = in_ref[...]
    none_ref[...] = jnp.zeros_like(none_ref)
    over_ref[0] = jnp.max(in_ref[0, SLOTS - 1 : SLOTS, LANES - 1 : LANES]).astype(jnp.int32)
    values, where, plane, bound, rank = slots_of(in_ref)
    target = jnp.where((where > 0) & (rank < FIT), plane * ROWS + rank, -1)
    placed = picked(ones(iota((planes * ROWS, 2 * LANES), 0) == target), values)
    number = jnp.where(bound, ((where - 1) & 31) + 1, 0)
    lane = iota((2 * LANES, 2 * LANES), 0) - lax.axis_index("z") * ROWS
    numbers = dot_rows(small(number), ones((lane == rank) & (rank < FIT)))
    placed = placed.reshape(out_ref.shape)
    line = iota(out_ref.shape, 1)
    near = numbers[:, :LANES].reshape(planes, 1, LANES)
    far = numbers[:, LANES:].reshape(planes, 1, LANES)
    out_ref[...] = jnp.where(line == FIT, near, jnp.where(line == FIT + 1, far, placed))


def place(slots, planes, per_plane):
    return pl.pallas_call(
        place_kernel,
        out_specs=[
            pl.BlockSpec(memory_space=pltpu.VMEM),
            pl.BlockSpec(memory_space=pltpu.VMEM),
            pl.BlockSpec(memory_space=pltpu.VMEM),
            pl.BlockSpec(memory_space=pltpu.SMEM),
        ],
        out_shape=[
            pltpu.VMEM((planes, ROWS, LANES), jnp.float32),
            pltpu.VMEM(slots.shape, slots.dtype),
            pltpu.VMEM((per_plane, LANES), jnp.float32),
            jax.ShapeDtypeStruct((1,), jnp.int32),
        ],
        compiler_params=pltpu.CompilerParams(vmem_limit_bytes=GRANT),
        name="place",
    )(slots)


def place_rest_kernel(in_ref, out_ref):
    planes, per_plane, _ = out_ref.shape
    values, where, _, _, rank = slots_of(in_ref)
    row = iota((planes * per_plane, 2 * LANES), 0) + 1
    out_ref[...] = picked(ones((row == where) & (rank >= FIT)), values).reshape(out_ref.shape)


def place_rest(slots, planes, per_plane):
    return pl.pallas_call(
        place_rest_kernel,
        out_shape=jax.ShapeDtypeStruct((planes, per_plane, LANES), jnp.float32),
        compiler_params=pltpu.CompilerParams(vmem_limit_bytes=GRANT),
        name="place_rest",
    )(slots)


def average_kernel(owner_ref, length_ref, bias_ref, in_ref, rest_ref, out_ref):
    planes = in_ref.shape[0]
    per_plane = rest_ref.shape[0]
    marks = jnp.sum(in_ref[:, FIT : FIT + 2, :], axis=0).astype(jnp.int32)
    where = jnp.concatenate([marks[0:1, :], marks[1:2, :]], axis=1)
    picker = ones(iota((per_plane, planes * ROWS), 0) + 1 == where)
    total = picked(picker, in_ref[...].reshape(planes * ROWS, LANES)) + rest_ref[...]
    mine = lax.axis_index("z") * per_plane
    row = iota((per_plane, owner_ref.shape[1]), 0) + mine
    length = jnp.sum(
        jnp.where(row == plane_row(owner_ref[...]), length_ref[...], 0).astype(jnp.float32),
        axis=1,
        keepdims=True,
    )
    chunk = lax.axis_index("x") * 2 + lax.axis_index("c")
    average = total / length + bias_ref[pl.ds(chunk, 1), :]
    owners, copies, rows, _ = out_ref.shape
    for o in range(owners):
        for y in range(copies):
            out_ref[o, y] = average[o * rows : (o + 1) * rows, :]


def averages_for_owners(arrived, rest, owner_slot, lengths, pool_bias, owners, copies):
    rows = rest.shape[0] // owners
    return pl.pallas_call(
        average_kernel,
        out_shape=jax.ShapeDtypeStruct((owners, copies, rows, LANES), jnp.float32),
        compiler_params=pltpu.CompilerParams(vmem_limit_bytes=GRANT),
        name="average",
    )(owner_slot.reshape(1, -1), lengths.reshape(1, -1), pool_bias.reshape(-1, LANES), arrived, rest)


def norm_kernel(in_ref, out_ref):
    chunks, slices, rows, _ = in_ref.shape
    every = in_ref[...]
    square = jnp.sum(every * every, axis=(0, 1))
    energy = jnp.sum(square, axis=1, keepdims=True) / (chunks * slices * LANES)
    scale = lax.rsqrt(energy + 1e-06)
    mine = lax.axis_index("y")
    for c in range(chunks):
        out_ref[:, c * LANES : (c + 1) * LANES] = (in_ref[c, mine] * scale).astype(jnp.bfloat16)


def normed(arrived):
    chunks, _, rows, _ = arrived.shape
    return pl.pallas_call(
        norm_kernel,
        out_shape=jax.ShapeDtypeStruct((rows, chunks * LANES), jnp.bfloat16),
        compiler_params=pltpu.CompilerParams(vmem_limit_bytes=GRANT),
        name="norm",
    )(arrived)


def swap(array, axes):
    return lax.all_to_all(array, axes, split_axis=0, concat_axis=0, tiled=True)


def local(hidden, seg_ids, lengths, owner_slot, pool_bias):
    chunks = lax.axis_size(("x", "c"))
    planes = lax.axis_size("z")
    slices = lax.axis_size("y")
    per_plane = lengths.shape[0] // planes
    slots = swap(local_sums(seg_ids, owner_slot, lengths, hidden, chunks), ("x", "c"))
    placed, kept, none, over = place(slots, planes, per_plane)
    rows = swap(placed, "z")
    rest = lax.cond(
        over[0] > 0,
        lambda slots, none: jnp.sum(swap(place_rest(slots, planes, per_plane), "z"), axis=0),
        lambda slots, none: none,
        kept,
        none,
    )
    average = averages_for_owners(rows, rest, owner_slot, lengths, pool_bias, chunks, slices)
    mine = swap(average.reshape(chunks * slices, -1, LANES), ("x", "c", "y"))
    return normed(mine.reshape(average.shape))


def solution(mesh):
    torus = Mesh(mesh.devices.reshape(4, 16, 2, mesh.shape["hid"]), ("x", "z", "c", "y"))
    seq = ("x", "z", "c")
    return jax.shard_map(
        local,
        mesh=torus,
        in_specs=(P(seq, "y"), P(seq), P(), P(), P("y")),
        out_specs=P(seq, "y"),
        check_vma=False,
    )
```

time: 60.6 us -> 58.2 us (0.960)
  blocking collectives: 57.1 us -> 53.3 us
  Pallas kernels: 3.23 us -> 4.02 us
  between operations: 0.03 us -> 0.69 us
    all_to_all x3, blocking collectives: 57.1 us -> 53.3 us  [swap(): return lax.all_to_all(array, axes, split_axis=0, concat_axis=0, tiled=True)]
where the time goes in v5:
time: 58.2 us; the launch traced here: 58 us
  blocking collectives  53.3 us (92%)
  Pallas kernels  4.02 us (7%)
  between operations  0.69 us (1%)
    all_to_all x3, blocking collectives, swap(): return lax.all_to_all(array, axes, split_axis=0, concat_axis=0, tiled=True)  53.3 us
    pallas_call x1, Pallas kernels, local_sums(): pl.pallas_call(functools.partial(sums_kernel, pieces), in_specs=[pl.Block...  2.32 us

profile of v5, /device:TPU:1, one launch (start us, length us, event | category | flops | bytes accessed | tf_op | source)
XLA Modules:
  0.0 58.0 jit_solution(15536451802688239674)
XLA Ops:
  0.0 0.0 copy-start
  0.0 0.0 copy-start.1
  0.0 0.0 copy-start.2
  0.0 2.3 %local_sums.1 = f32[8,24,128]{2,1,0:T(8,128)S(1)} custom-call(s32[1,1024]{1,0:T(1,128)} %bitcast.14, s32[1,512]{1,0:T(1,128)} %bitcast.9, s32[1,512]{1,0:T(1,128)} %bitcast.11, bf16[1024,1024]{1,0:T(8,128)(2,1)} %hidden_hbm.1), custom_call_target="tpu_custom_call" | custom-call | tf_op jit(solution)/shard_map/local_sums/pallas_call | solution.py:125
  2.3 14.2 %all_to_all.20.in_ref = f32[8,24,128]{2,1,0:T(8,128)S(1)} all-to-all(f32[8,24,128]{2,1,0:T(8,128)S(1)} %local_sums.1), channel_id=1, replica_groups=mesh['x'=4,'z'=16,'c'=2,'y'=4] {'x','c'}, dimensions={0} | all-to-all | bytes 196608 | tf_op jit(solution)/shard_map/all_to_all | solution.py:265
  16.5 0.8 %place.1 = (f32[16,16,128]{2,1,0:T(8,128)S(1)}, f32[8,24,128]{2,1,0:T(8,128)S(1)}, f32[32,128]{1,0:T(8,128)S(1)}, s32[1]{0:T(128)}) custom-call(f32[8,24,128]{2,1,0:T(8,128)S(1)} %all_to_all.20.in_ref), custom_call_target="tpu_custom_call" | custom-call | tf_op jit(solution)/shard_map/place/pallas_call | solution.py:176
  18.0 23.0 %all_to_all.21.in_ref = f32[16,16,128]{2,1,0:T(8,128)S(1)} all-to-all(f32[16,16,128]{2,1,0:T(8,128)S(1)} %get-tuple-element.14), channel_id=1, replica_groups=mesh['x'=4,'z'=16,'c'=2,'y'=4] {'z'}, dimensions={0} | all-to-all | bytes 262144 | tf_op jit(solution)/shard_map/all_to_all | solution.py:265
  41.1 0.0 copy-done
  41.1 0.0 copy-done.1
  41.1 0.0 copy-done.2
  41.1 0.2 average.1
  41.3 16.1 %all_to_all.22 = f32[32,4,128]{2,1,0:T(4,128)S(1)} all-to-all(f32[32,4,128]{2,1,0:T(4,128)S(1)} %bitcast.7), channel_id=1, replica_groups=mesh['x'=4,'z'=16,'c'=2,'y'=4] {'x','c','y'}, dimensions={0} | all-to-all | bytes 131072 | tf_op jit(solution)/shard_map/all_to_all | solution.py:265
  57.3 0.7 %norm.1 = bf16[4,1024]{1,0:T(4,128)(2,1)} custom-call(f32[8,4,4,128]{3,2,1,0:T(4,128)S(1)} %bitcast.8), custom_call_target="tpu_custom_call" | custom-call | tf_op jit(solution)/shard_map/norm/pallas_call | solution.py:256
  (1 shorter events, 0.0 us)
Async XLA Ops:
  0.0 41.1 %copy-start = (s32[512]{0:T(512)S(1)}, s32[512]{0:T(512)}, u32[]{:S(2)}) copy-start(s32[512]{0:T(512)} %param.10) | copy-start | bytes 6148
  0.0 41.1 %copy-start.1 = (s32[512]{0:T(512)S(1)}, s32[512]{0:T(512)}, u32[]{:S(2)}) copy-start(s32[512]{0:T(512)} %param.9) | copy-start | bytes 6148
  0.0 41.1 %copy-start.2 = (f32[1024]{0:T(1024)S(1)}, f32[1024]{0:T(1024)}, u32[]{:S(2)}) copy-start(f32[1024]{0:T(1024)} %param.11) | copy-start | bytes 12292

commit v6 on v5

--- a/solution.py
+++ b/solution.py
@@ -154,10 +154,9 @@
     return jnp.concatenate([values, empty], axis=0), where, plane, bound, rank
 
 
-def place_kernel(in_ref, out_ref, kept_ref, none_ref, over_ref):
+def place_kernel(in_ref, out_ref, kept_ref, over_ref):
     planes = out_ref.shape[0]
     kept_ref[...] = in_ref[...]
-    none_ref[...] = jnp.zeros_like(none_ref)
     over_ref[0] = jnp.max(in_ref[0, SLOTS - 1 : SLOTS, LANES - 1 : LANES]).astype(jnp.int32)
     values, where, plane, bound, rank = slots_of(in_ref)
     target = jnp.where((where > 0) & (rank < FIT), plane * ROWS + rank, -1)
@@ -172,11 +171,10 @@
     out_ref[...] = jnp.where(line == FIT, near, jnp.where(line == FIT + 1, far, placed))
 
 
-def place(slots, planes, per_plane):
+def place(slots, planes):
     return pl.pallas_call(
         place_kernel,
         out_specs=[
-            pl.BlockSpec(memory_space=pltpu.VMEM),
             pl.BlockSpec(memory_space=pltpu.VMEM),
             pl.BlockSpec(memory_space=pltpu.VMEM),
             pl.BlockSpec(memory_space=pltpu.SMEM),
@@ -184,7 +182,6 @@
         out_shape=[
             pltpu.VMEM((planes, ROWS, LANES), jnp.float32),
             pltpu.VMEM(slots.shape, slots.dtype),
-            pltpu.VMEM((per_plane, LANES), jnp.float32),
             jax.ShapeDtypeStruct((1,), jnp.int32),
         ],
         compiler_params=pltpu.CompilerParams(vmem_limit_bytes=GRANT),
@@ -208,13 +205,16 @@
     )(slots)
 
 
-def average_kernel(owner_ref, length_ref, bias_ref, in_ref, rest_ref, out_ref):
+def average_kernel(owner_ref, length_ref, bias_ref, in_ref, *rest_and_out):
+    out_ref = rest_and_out[-1]
     planes = in_ref.shape[0]
-    per_plane = rest_ref.shape[0]
+    per_plane = owner_ref.shape[1] // planes
     marks = jnp.sum(in_ref[:, FIT : FIT + 2, :], axis=0).astype(jnp.int32)
     where = jnp.concatenate([marks[0:1, :], marks[1:2, :]], axis=1)
     picker = ones(iota((per_plane, planes * ROWS), 0) + 1 == where)
-    total = picked(picker, in_ref[...].reshape(planes * ROWS, LANES)) + rest_ref[...]
+    total = picked(picker, in_ref[...].reshape(planes * ROWS, LANES))
+    for rest_ref in rest_and_out[:-1]:
+        total = total + jnp.sum(rest_ref[...], axis=0)
     mine = lax.axis_index("z") * per_plane
     row = iota((per_plane, owner_ref.shape[1]), 0) + mine
     length = jnp.sum(
@@ -230,14 +230,14 @@
             out_ref[o, y] = average[o * rows : (o + 1) * rows, :]
 
 
-def averages_for_owners(arrived, rest, owner_slot, lengths, pool_bias, owners, copies):
-    rows = rest.shape[0] // owners
+def averages_for_owners(arrived, owner_slot, lengths, pool_bias, owners, copies, *rest):
+    rows = owner_slot.shape[0] // (arrived.shape[0] * owners)
     return pl.pallas_call(
         average_kernel,
         out_shape=jax.ShapeDtypeStruct((owners, copies, rows, LANES), jnp.float32),
         compiler_params=pltpu.CompilerParams(vmem_limit_bytes=GRANT),
         name="average",
-    )(owner_slot.reshape(1, -1), lengths.reshape(1, -1), pool_bias.reshape(-1, LANES), arrived, rest)
+    )(owner_slot.reshape(1, -1), lengths.reshape(1, -1), pool_bias.reshape(-1, LANES), arrived, *rest)
 
 
 def norm_kernel(in_ref, out_ref):
@@ -271,16 +271,18 @@
     slices = lax.axis_size("y")
     per_plane = lengths.shape[0] // planes
     slots = swap(local_sums(seg_ids, owner_slot, lengths, hidden, chunks), ("x", "c"))
-    placed, kept, none, over = place(slots, planes, per_plane)
+    placed, kept, over = place(slots, planes)
     rows = swap(placed, "z")
-    rest = lax.cond(
-        over[0] > 0,
-        lambda slots, none: jnp.sum(swap(place_rest(slots, planes, per_plane), "z"), axis=0),
-        lambda slots, none: none,
-        kept,
-        none,
-    )
-    average = averages_for_owners(rows, rest, owner_slot, lengths, pool_bias, chunks, slices)
+    args = (owner_slot, lengths, pool_bias, chunks, slices)
+
+    def with_rest(rows, kept):
+        rest = swap(place_rest(kept, planes, per_plane), "z")
+        return averages_for_owners(rows, *args, rest)
+
+    def alone(rows, kept):
+        return averages_for_owners(rows, *args)
+
+    average = lax.cond(over[0] > 0, with_rest, alone, rows, kept)
     mine = swap(average.reshape(chunks * slices, -1, LANES), ("x", "c", "y"))
     return normed(mine.reshape(average.shape))
 

time: 58.2 us -> 58.1 us (level)
  blocking collectives: 53.3 us -> 30.2 us
  starting transfers between devices: 0 us -> 11.3 us
  waiting for transfers between devices: 0 us -> 11.3 us
    all_to_all x3 -> x2, blocking collectives: 53.3 us -> 30.2 us  [swap(): return lax.all_to_all(array, axes, split_axis=0, concat_axis=0, tiled=True)]
    all_to_all x0 -> x1, waiting for transfers between devices: none -> 11.3 us  [swap(): return lax.all_to_all(array, axes, split_axis=0, concat_axis=0, tiled=True)]
    all_to_all x0 -> x1, starting transfers between devices: none -> 11.3 us  [swap(): return lax.all_to_all(array, axes, split_axis=0, concat_axis=0, tiled=True)]
  transfers between devices with their start and end apart: 0 -> 1, of which waited for: 0 -> 1; matrix products, arithmetic and copies ran while one was open for 0% -> 0% of each run, Pallas kernels for 0% -> 0%
where the time goes in v6:
time: 58.1 us; the launch traced here: 57.8 us
  blocking collectives  30.2 us (52%)
  starting transfers between devices  11.3 us (19%)
  waiting for transfers between devices  11.3 us (19%)
  Pallas kernels  4.26 us (7%)
  between operations  0.69 us (1%)
    all_to_all x2, blocking collectives, swap(): return lax.all_to_all(array, axes, split_axis=0, concat_axis=0, tiled=True)  30.2 us
    all_to_all x1, waiting for transfers between devices, swap(): return lax.all_to_all(array, axes, split_axis=0, concat_axis=0, tiled=True)  11.3 us
    all_to_all x1, starting transfers between devices, swap(): return lax.all_to_all(array, axes, split_axis=0, concat_axis=0, tiled=True)  11.3 us
    pallas_call x1, Pallas kernels, local_sums(): pl.pallas_call(functools.partial(sums_kernel, pieces), in_specs=[pl.Block...  2.33 us
  transfers between devices with their start and end apart: 1, of which 1 were waited for; matrix products, arithmetic and copies ran while one was open for 0% of the time, Pallas kernels for 0%

profile of v6, /device:TPU:1, one launch (start us, length us, event | category | flops | bytes accessed | tf_op | source)
XLA Modules:
  0.0 57.8 jit_solution(8037150540689835291)
XLA Ops:
  0.0 0.0 copy-start.1
  0.0 0.0 copy-start
  0.0 0.0 copy-start.2
  0.0 2.3 %local_sums.1 = f32[8,24,128]{2,1,0:T(8,128)S(1)} custom-call(s32[1,1024]{1,0:T(1,128)} %bitcast.22, s32[1,512]{1,0:T(1,128)} %bitcast.14, s32[1,512]{1,0:T(1,128)} %bitcast.17, bf16[1024,1024]{1,0:T(8,128)(2,1)} %hidden_hbm.1), custom_call_target="tpu_custom_call" | custom-call | tf_op jit(solution)/shard_map/local_sums/pallas_call | solution.py:125
  2.3 14.2 %all_to_all.20.in_ref = f32[8,24,128]{2,1,0:T(8,128)S(1)} all-to-all(f32[8,24,128]{2,1,0:T(8,128)S(1)} %local_sums.1), channel_id=1, replica_groups=mesh['x'=4,'z'=16,'c'=2,'y'=4] {'x','c'}, dimensions={0} | all-to-all | bytes 196608 | tf_op jit(solution)/shard_map/all_to_all | solution.py:265
  16.5 1.0 %place.1 = (f32[16,16,128]{2,1,0:T(8,128)}, f32[8,24,128]{2,1,0:T(8,128)S(1)}, s32[1]{0:T(128)}) custom-call(f32[8,24,128]{2,1,0:T(8,128)S(1)} %all_to_all.20.in_ref), custom_call_target="tpu_custom_call" | custom-call | tf_op jit(solution)/shard_map/place/pallas_call | solution.py:175
  17.6 11.3 %all-to-all-start.2 = ((f32[16,16,128]{2,1,0:T(8,128)}), f32[16,16,128]{2,1,0:T(8,128)S(1)}, u32[]{:S(2)}, u32[]{:S(2)}) async-start(f32[16,16,128]{2,1,0:T(8,128)} %get-tuple-element.39), calls=%async_computation.2 | async-start | bytes 262144 | tf_op jit(solution)/shard_map/all_to_all | solution.py:265
  29.6 11.3 %all-to-all-done.2 = f32[16,16,128]{2,1,0:T(8,128)S(1)} async-done(((f32[16,16,128]{2,1,0:T(8,128)}), f32[16,16,128]{2,1,0:T(8,128)S(1)}, u32[]{:S(2)}, u32[]{:S(2)}) %all-to-all-start.2) | async-done | bytes 131104 | tf_op jit(solution)/shard_map/all_to_all | solution.py:265
  40.9 0.0 copy-done.1
  40.9 0.0 copy-done
  40.9 0.0 copy-done.2
  40.9 0.2 conditional.1
  40.9 0.2 average.2
  41.1 16.0 %all_to_all.21 = f32[32,4,128]{2,1,0:T(4,128)S(1)} all-to-all(f32[32,4,128]{2,1,0:T(4,128)S(1)} %bitcast.13), channel_id=1, replica_groups=mesh['x'=4,'z'=16,'c'=2,'y'=4] {'x','c','y'}, dimensions={0} | all-to-all | bytes 131072 | tf_op jit(solution)/shard_map/all_to_all | solution.py:265
  57.1 0.7 %norm.1 = bf16[4,1024]{1,0:T(4,128)(2,1)} custom-call(f32[8,4,4,128]{3,2,1,0:T(4,128)S(1)} %bitcast.12), custom_call_target="tpu_custom_call" | custom-call | tf_op jit(solution)/shard_map/norm/pallas_call | solution.py:256
Async XLA Ops:
  0.0 40.9 %copy-start.1 = (s32[512]{0:T(512)S(1)}, s32[512]{0:T(512)}, u32[]{:S(2)}) copy-start(s32[512]{0:T(512)} %param.9) | copy-start | bytes 6148
  0.0 40.9 %copy-start = (s32[512]{0:T(512)S(1)}, s32[512]{0:T(512)}, u32[]{:S(2)}) copy-start(s32[512]{0:T(512)} %param.10) | copy-start | bytes 6148
  0.0 40.9 %copy-start.2 = (f32[1024]{0:T(1024)S(1)}, f32[1024]{0:T(1024)}, u32[]{:S(2)}) copy-start(f32[1024]{0:T(1024)} %param.11) | copy-start | bytes 12292
  17.6 23.3 %all-to-all-start.2 = ((f32[16,16,128]{2,1,0:T(8,128)}), f32[16,16,128]{2,1,0:T(8,128)S(1)}, u32[]{:S(2)}, u32[]{:S(2)}) async-start(f32[16,16,128]{2,1,0:T(8,128)} %get-tuple-element.39), calls=%async_computation.2 | async-start | bytes 262144 | tf_op jit(solution)/shard_map/all_to_all | solution.py:265

commit v7 on v6

--- a/solution.py
+++ b/solution.py
@@ -17,8 +17,25 @@
 WIDE = 56 * 1024 * 1024
 
 
+def chunk_place():
+    return (((lax.axis_index("x") + 2) & 3) * 2 + lax.axis_index("c")) ^ 1
+
+
+def plane_place(z):
+    return (z + 8) & 15
+
+
+def slice_place():
+    return (lax.axis_index("y") + 2) & 3
+
+
+CHUNK_GROUP = [[(((j >> 1) + 2) & 3) * 2 + (j & 1) ^ 1 for j in range(8)]]
+PLANE_GROUP = [[(j + 8) & 15 for j in range(16)]]
+OWNER_GROUP = [[(j & ~3) + ((j + 2) & 3) for j in range(32)]]
+
+
 def plane_row(owner):
-    return ((owner >> 3) & 15) * 32 + (owner >> 7) * 8 + (owner & 7)
+    return plane_place(owner >> 3) * 32 + (owner >> 7) * 8 + (owner & 7)
 
 
 def ones(mask):
@@ -54,7 +71,7 @@
 
 def marks_of(first, last, owner):
     docs = owner.shape[1]
-    source = lax.axis_index("x") * 2 + lax.axis_index("c")
+    source = chunk_place()
     row = plane_row(owner) + 1
     part = iota((8, docs), 0)
     digits = jnp.where(part == 0, row >> 5, jnp.where(part == 1, row & 31, 0))
@@ -162,7 +179,7 @@
     target = jnp.where((where > 0) & (rank < FIT), plane * ROWS + rank, -1)
     placed = picked(ones(iota((planes * ROWS, 2 * LANES), 0) == target), values)
     number = jnp.where(bound, ((where - 1) & 31) + 1, 0)
-    lane = iota((2 * LANES, 2 * LANES), 0) - lax.axis_index("z") * ROWS
+    lane = iota((2 * LANES, 2 * LANES), 0) - plane_place(lax.axis_index("z")) * ROWS
     numbers = dot_rows(small(number), ones((lane == rank) & (rank < FIT)))
     placed = placed.reshape(out_ref.shape)
     line = iota(out_ref.shape, 1)
@@ -215,14 +232,14 @@
     total = picked(picker, in_ref[...].reshape(planes * ROWS, LANES))
     for rest_ref in rest_and_out[:-1]:
         total = total + jnp.sum(rest_ref[...], axis=0)
-    mine = lax.axis_index("z") * per_plane
+    mine = plane_place(lax.axis_index("z")) * per_plane
     row = iota((per_plane, owner_ref.shape[1]), 0) + mine
     length = jnp.sum(
         jnp.where(row == plane_row(owner_ref[...]), length_ref[...], 0).astype(jnp.float32),
         axis=1,
         keepdims=True,
     )
-    chunk = lax.axis_index("x") * 2 + lax.axis_index("c")
+    chunk = chunk_place()
     average = total / length + bias_ref[pl.ds(chunk, 1), :]
     owners, copies, rows, _ = out_ref.shape
     for o in range(owners):
@@ -246,9 +263,10 @@
     square = jnp.sum(every * every, axis=(0, 1))
     energy = jnp.sum(square, axis=1, keepdims=True) / (chunks * slices * LANES)
     scale = lax.rsqrt(energy + 1e-06)
-    mine = lax.axis_index("y")
-    for c in range(chunks):
-        out_ref[:, c * LANES : (c + 1) * LANES] = (in_ref[c, mine] * scale).astype(jnp.bfloat16)
+    mine = slice_place()
+    for c, device in enumerate(CHUNK_GROUP[0]):
+        values = in_ref[device, mine] * scale
+        out_ref[:, c * LANES : (c + 1) * LANES] = values.astype(jnp.bfloat16)
 
 
 def normed(arrived):
@@ -261,8 +279,10 @@
     )(arrived)
 
 
-def swap(array, axes):
-    return lax.all_to_all(array, axes, split_axis=0, concat_axis=0, tiled=True)
+def swap(array, axes, group):
+    return lax.all_to_all(
+        array, axes, split_axis=0, concat_axis=0, tiled=True, axis_index_groups=group
+    )
 
 
 def local(hidden, seg_ids, lengths, owner_slot, pool_bias):
@@ -270,20 +290,20 @@
     planes = lax.axis_size("z")
     slices = lax.axis_size("y")
     per_plane = lengths.shape[0] // planes
-    slots = swap(local_sums(seg_ids, owner_slot, lengths, hidden, chunks), ("x", "c"))
+    slots = swap(local_sums(seg_ids, owner_slot, lengths, hidden, chunks), ("x", "c"), CHUNK_GROUP)
     placed, kept, over = place(slots, planes)
-    rows = swap(placed, "z")
+    rows = swap(placed, "z", PLANE_GROUP)
     args = (owner_slot, lengths, pool_bias, chunks, slices)
 
     def with_rest(rows, kept):
-        rest = swap(place_rest(kept, planes, per_plane), "z")
+        rest = swap(place_rest(kept, planes, per_plane), "z", PLANE_GROUP)
         return averages_for_owners(rows, *args, rest)
 
     def alone(rows, kept):
         return averages_for_owners(rows, *args)
 
     average = lax.cond(over[0] > 0, with_rest, alone, rows, kept)
-    mine = swap(average.reshape(chunks * slices, -1, LANES), ("x", "c", "y"))
+    mine = swap(average.reshape(chunks * slices, -1, LANES), ("x", "c", "y"), OWNER_GROUP)
     return normed(mine.reshape(average.shape))
 
 

time: 58.1 us -> 51.5 us (0.89)
  waiting for transfers between devices: 11.3 us -> 6.14 us
  blocking collectives: 30.2 us -> 26.4 us
  starting transfers between devices: 11.3 us -> 13.7 us
    all_to_all x1, waiting for transfers between devices: 11.3 us -> 6.14 us  [swap(): lax.all_to_all(array, axes, split_axis=0, concat_axis=0, tiled=True, axis...]
    all_to_all x2, blocking collectives: 30.2 us -> 26.4 us  [swap(): lax.all_to_all(array, axes, split_axis=0, concat_axis=0, tiled=True, axis...]
    all_to_all x1, starting transfers between devices: 11.3 us -> 13.7 us  [swap(): lax.all_to_all(array, axes, split_axis=0, concat_axis=0, tiled=True, axis...]
where the time goes in v7:
time: 51.5 us; the launch traced here: 51.2 us
  blocking collectives  26.4 us (51%)
  starting transfers between devices  13.7 us (27%)
  waiting for transfers between devices  6.14 us (12%)
  Pallas kernels  4.26 us (8%)
  between operations  0.69 us (1%)
    all_to_all x2, blocking collectives, swap(): lax.all_to_all(array, axes, split_axis=0, concat_axis=0, tiled=True, axis...  26.4 us
    all_to_all x1, starting transfers between devices, swap(): lax.all_to_all(array, axes, split_axis=0, concat_axis=0, tiled=True, axis...  13.7 us
    all_to_all x1, waiting for transfers between devices, swap(): lax.all_to_all(array, axes, split_axis=0, concat_axis=0, tiled=True, axis...  6.14 us
    pallas_call x1, Pallas kernels, local_sums(): pl.pallas_call(functools.partial(sums_kernel, pieces), in_specs=[pl.Block...  2.33 us
    pallas_call x1, Pallas kernels, place(): pl.pallas_call(place_kernel, out_specs=[pl.BlockSpec(memory_space=pltpu.V...  1.05 us
  transfers between devices with their start and end apart: 1, of which 1 were waited for; matrix products, arithmetic and copies ran while one was open for 0% of the time, Pallas kernels for 0%

profile of v7, /device:TPU:1, one launch (start us, length us, event | category | flops | bytes accessed | tf_op | source)
XLA Modules:
  0.0 51.2 jit_solution(12110522877897254969)
XLA Ops:
  0.0 0.0 copy-start.1
  0.0 0.0 copy-start
  0.0 0.0 copy-start.2
  0.0 2.3 %local_sums.1 = f32[8,24,128]{2,1,0:T(8,128)S(1)} custom-call(s32[1,1024]{1,0:T(1,128)} %bitcast.22, s32[1,512]{1,0:T(1,128)} %bitcast.14, s32[1,512]{1,0:T(1,128)} %bitcast.17, bf16[1024,1024]{1,0:T(8,128)(2,1)} %hidden_hbm.1), custom_call_target="tpu_custom_call" | custom-call | tf_op jit(solution)/shard_map/local_sums/pallas_call | solution.py:142
  2.3 13.4 %all_to_all.20.in_ref = f32[8,24,128]{2,1,0:T(8,128)S(1)} all-to-all(f32[8,24,128]{2,1,0:T(8,128)S(1)} %local_sums.1), channel_id=1, replica_groups={{260,256,388,384,4,0,132,128},{261,257,389,385,5,1,133,129},{262,258,39..., dimensions={0} | all-to-all | bytes 196608 | tf_op jit(solution)/shard_map/all_to_all | solution.py:283
  15.8 1.0 %place.1 = (f32[16,16,128]{2,1,0:T(8,128)}, f32[8,24,128]{2,1,0:T(8,128)S(1)}, s32[1]{0:T(128)}) custom-call(f32[8,24,128]{2,1,0:T(8,128)S(1)} %all_to_all.20.in_ref), custom_call_target="tpu_custom_call" | custom-call | tf_op jit(solution)/shard_map/place/pallas_call | solution.py:192
  16.8 13.7 %all-to-all-start.2 = ((f32[16,16,128]{2,1,0:T(8,128)}), f32[16,16,128]{2,1,0:T(8,128)S(1)}, u32[]{:S(2)}, u32[]{:S(2)}) async-start(f32[16,16,128]{2,1,0:T(8,128)} %get-tuple-element.39), calls=%async_computation.2 | async-start | bytes 262144 | tf_op jit(solution)/shard_map/all_to_all | solution.py:283
  31.1 6.1 %all-to-all-done.2 = f32[16,16,128]{2,1,0:T(8,128)S(1)} async-done(((f32[16,16,128]{2,1,0:T(8,128)}), f32[16,16,128]{2,1,0:T(8,128)S(1)}, u32[]{:S(2)}, u32[]{:S(2)}) %all-to-all-start.2) | async-done | bytes 131104 | tf_op jit(solution)/shard_map/all_to_all | solution.py:283
  37.3 0.0 copy-done.1
  37.3 0.0 copy-done
  37.3 0.0 copy-done.2
  37.3 0.2 conditional.1
  37.3 0.2 average.2
  37.5 13.0 %all_to_all.21 = f32[32,4,128]{2,1,0:T(4,128)S(1)} all-to-all(f32[32,4,128]{2,1,0:T(4,128)S(1)} %bitcast.13), channel_id=1, replica_groups={{2,3,0,1,6,7,4,5,130,131,128,129,134,135,132,133,258,259,256,257,262,26..., dimensions={0} | all-to-all | bytes 131072 | tf_op jit(solution)/shard_map/all_to_all | solution.py:283
  50.5 0.7 %norm.1 = bf16[4,1024]{1,0:T(4,128)(2,1)} custom-call(f32[8,4,4,128]{3,2,1,0:T(4,128)S(1)} %bitcast.12), custom_call_target="tpu_custom_call" | custom-call | tf_op jit(solution)/shard_map/norm/pallas_call | solution.py:274
Async XLA Ops:
  0.0 37.3 %copy-start.1 = (s32[512]{0:T(512)S(1)}, s32[512]{0:T(512)}, u32[]{:S(2)}) copy-start(s32[512]{0:T(512)} %param.9) | copy-start | bytes 6148
  0.0 37.3 %copy-start = (s32[512]{0:T(512)S(1)}, s32[512]{0:T(512)}, u32[]{:S(2)}) copy-start(s32[512]{0:T(512)} %param.10) | copy-start | bytes 6148
  0.0 37.3 %copy-start.2 = (f32[1024]{0:T(1024)S(1)}, f32[1024]{0:T(1024)}, u32[]{:S(2)}) copy-start(f32[1024]{0:T(1024)} %param.11) | copy-start | bytes 12292
  16.8 20.5 %all-to-all-start.2 = ((f32[16,16,128]{2,1,0:T(8,128)}), f32[16,16,128]{2,1,0:T(8,128)S(1)}, u32[]{:S(2)}, u32[]{:S(2)}) async-start(f32[16,16,128]{2,1,0:T(8,128)} %get-tuple-element.39), calls=%async_computation.2 | async-start | bytes 262144 | tf_op jit(solution)/shard_map/all_to_all | solution.py:283

commit v8 on v7

--- a/solution.py
+++ b/solution.py
@@ -22,7 +22,7 @@
 
 
 def plane_place(z):
-    return (z + 8) & 15
+    return (z + 4) & 15
 
 
 def slice_place():
@@ -30,7 +30,7 @@
 
 
 CHUNK_GROUP = [[(((j >> 1) + 2) & 3) * 2 + (j & 1) ^ 1 for j in range(8)]]
-PLANE_GROUP = [[(j + 8) & 15 for j in range(16)]]
+PLANE_GROUP = [[(j + 12) & 15 for j in range(16)]]
 OWNER_GROUP = [[(j & ~3) + ((j + 2) & 3) for j in range(32)]]
 
 

time: 51.5 us -> 52.9 us (1.027)
  starting transfers between devices: 13.7 us -> 10.5 us
  blocking collectives: 26.4 us -> 28.7 us
  waiting for transfers between devices: 6.14 us -> 8.39 us
    all_to_all x1, starting transfers between devices: 13.7 us -> 10.5 us  [swap(): lax.all_to_all(array, axes, split_axis=0, concat_axis=0, tiled=True, axis...]
    all_to_all x2, blocking collectives: 26.4 us -> 28.7 us  [swap(): lax.all_to_all(array, axes, split_axis=0, concat_axis=0, tiled=True, axis...]
    all_to_all x1, waiting for transfers between devices: 6.14 us -> 8.39 us  [swap(): lax.all_to_all(array, axes, split_axis=0, concat_axis=0, tiled=True, axis...]
where the time goes in v8:
time: 52.9 us; the launch traced here: 52.6 us
  blocking collectives  28.7 us (54%)
  starting transfers between devices  10.5 us (20%)
  waiting for transfers between devices  8.39 us (16%)
  Pallas kernels  4.26 us (8%)
  between operations  0.69 us (1%)
    all_to_all x2, blocking collectives, swap(): lax.all_to_all(array, axes, split_axis=0, concat_axis=0, tiled=True, axis...  28.7 us
    all_to_all x1, starting transfers between devices, swap(): lax.all_to_all(array, axes, split_axis=0, concat_axis=0, tiled=True, axis...  10.5 us
    all_to_all x1, waiting for transfers between devices, swap(): lax.all_to_all(array, axes, split_axis=0, concat_axis=0, tiled=True, axis...  8.39 us
    pallas_call x1, Pallas kernels, local_sums(): pl.pallas_call(functools.partial(sums_kernel, pieces), in_specs=[pl.Block...  2.33 us
  transfers between devices with their start and end apart: 1, of which 1 were waited for; matrix products, arithmetic and copies ran while one was open for 0% of the time, Pallas kernels for 0%

profile of v8, /device:TPU:1, one launch (start us, length us, event | category | flops | bytes accessed | tf_op | source)
XLA Modules:
  0.0 52.6 jit_solution(14553685628271814905)
XLA Ops:
  0.0 0.0 copy-start.1
  0.0 0.0 copy-start
  0.0 0.0 copy-start.2
  0.0 2.3 %local_sums.1 = f32[8,24,128]{2,1,0:T(8,128)S(1)} custom-call(s32[1,1024]{1,0:T(1,128)} %bitcast.22, s32[1,512]{1,0:T(1,128)} %bitcast.14, s32[1,512]{1,0:T(1,128)} %bitcast.17, bf16[1024,1024]{1,0:T(8,128)(2,1)} %hidden_hbm.1), custom_call_target="tpu_custom_call" | custom-call | tf_op jit(solution)/shard_map/local_sums/pallas_call | solution.py:142
  2.3 13.4 %all_to_all.20.in_ref = f32[8,24,128]{2,1,0:T(8,128)S(1)} all-to-all(f32[8,24,128]{2,1,0:T(8,128)S(1)} %local_sums.1), channel_id=1, replica_groups={{260,256,388,384,4,0,132,128},{261,257,389,385,5,1,133,129},{262,258,39..., dimensions={0} | all-to-all | bytes 196608 | tf_op jit(solution)/shard_map/all_to_all | solution.py:283
  15.8 1.0 %place.1 = (f32[16,16,128]{2,1,0:T(8,128)}, f32[8,24,128]{2,1,0:T(8,128)S(1)}, s32[1]{0:T(128)}) custom-call(f32[8,24,128]{2,1,0:T(8,128)S(1)} %all_to_all.20.in_ref), custom_call_target="tpu_custom_call" | custom-call | tf_op jit(solution)/shard_map/place/pallas_call | solution.py:192
  16.8 10.5 %all-to-all-start.2 = ((f32[16,16,128]{2,1,0:T(8,128)}), f32[16,16,128]{2,1,0:T(8,128)S(1)}, u32[]{:S(2)}, u32[]{:S(2)}) async-start(f32[16,16,128]{2,1,0:T(8,128)} %get-tuple-element.39), calls=%async_computation.2 | async-start | bytes 262144 | tf_op jit(solution)/shard_map/all_to_all | solution.py:283
  28.0 8.4 %all-to-all-done.2 = f32[16,16,128]{2,1,0:T(8,128)S(1)} async-done(((f32[16,16,128]{2,1,0:T(8,128)}), f32[16,16,128]{2,1,0:T(8,128)S(1)}, u32[]{:S(2)}, u32[]{:S(2)}) %all-to-all-start.2) | async-done | bytes 131104 | tf_op jit(solution)/shard_map/all_to_all | solution.py:283
  36.3 0.0 copy-done.1
  36.3 0.0 copy-done
  36.3 0.0 copy-done.2
  36.4 0.2 conditional.1
  36.4 0.2 average.2
  36.5 15.3 %all_to_all.21 = f32[32,4,128]{2,1,0:T(4,128)S(1)} all-to-all(f32[32,4,128]{2,1,0:T(4,128)S(1)} %bitcast.13), channel_id=1, replica_groups={{2,3,0,1,6,7,4,5,130,131,128,129,134,135,132,133,258,259,256,257,262,26..., dimensions={0} | all-to-all | bytes 131072 | tf_op jit(solution)/shard_map/all_to_all | solution.py:283
  51.9 0.7 %norm.1 = bf16[4,1024]{1,0:T(4,128)(2,1)} custom-call(f32[8,4,4,128]{3,2,1,0:T(4,128)S(1)} %bitcast.12), custom_call_target="tpu_custom_call" | custom-call | tf_op jit(solution)/shard_map/norm/pallas_call | solution.py:274
Async XLA Ops:
  0.0 36.3 %copy-start.1 = (s32[512]{0:T(512)S(1)}, s32[512]{0:T(512)}, u32[]{:S(2)}) copy-start(s32[512]{0:T(512)} %param.9) | copy-start | bytes 6148
  0.0 36.3 %copy-start = (s32[512]{0:T(512)S(1)}, s32[512]{0:T(512)}, u32[]{:S(2)}) copy-start(s32[512]{0:T(512)} %param.10) | copy-start | bytes 6148
  0.0 36.3 %copy-start.2 = (f32[1024]{0:T(1024)S(1)}, f32[1024]{0:T(1024)}, u32[]{:S(2)}) copy-start(f32[1024]{0:T(1024)} %param.11) | copy-start | bytes 12292
  16.8 19.5 %all-to-all-start.2 = ((f32[16,16,128]{2,1,0:T(8,128)}), f32[16,16,128]{2,1,0:T(8,128)S(1)}, u32[]{:S(2)}, u32[]{:S(2)}) async-start(f32[16,16,128]{2,1,0:T(8,128)} %get-tuple-element.39), calls=%async_computation.2 | async-start | bytes 262144 | tf_op jit(solution)/shard_map/all_to_all | solution.py:283

commit v9 on v7

--- a/solution.py
+++ b/solution.py
@@ -98,18 +98,17 @@
     touches = (start < (device + 1) * tokens) & (end > device * tokens)
     owned = ((owner >> 3) & 15) == line
     counts = dot_rows(ones(touches), ones(owned))
-    return jnp.max(jnp.sum(counts.reshape(8, 16, LANES), axis=0))
+    return jnp.max(jnp.sum(counts.reshape(8, 16, LANES), axis=0)).astype(jnp.int32)
 
 
 def sums_kernel(
-    pieces, seg_hbm, owner_hbm, length_hbm, hidden_hbm, out_ref, seg, owner, length, hidden, sems
+    pieces, seg_hbm, owner_hbm, hidden_hbm, out_ref, seg, owner, hidden, sems
 ):
     tokens = hidden.shape[0]
     rows = tokens // pieces
     copies = [
         pltpu.make_async_copy(seg_hbm, seg, sems.at[pieces]),
         pltpu.make_async_copy(owner_hbm, owner, sems.at[pieces + 1]),
-        pltpu.make_async_copy(length_hbm, length, sems.at[pieces + 2]),
     ]
     for p in range(pieces):
         here = pl.ds(p * rows, rows)
@@ -121,39 +120,35 @@
     last = seg[0:1, tokens - 1 : tokens]
     copies[1].wait()
     marks = marks_of(first, last, owner[...])
-    copies[2].wait()
-    over = jnp.where(most_rows(length[...], owner[...], tokens) > FIT, 1.0, 0.0)
-    marks = jnp.where((iota((SLOTS, LANES), 0) == SLOTS - 1) & (iota((SLOTS, LANES), 1) == LANES - 1), over, marks)
     slot = iota((SLOTS, rows), 0) + first
     sums = None
     for p in range(pieces):
         picker = ones(slot == seg[:, p * rows : (p + 1) * rows])
-        copies[3 + p].wait()
+        copies[2 + p].wait()
         term = dot(picker, hidden[p * rows : (p + 1) * rows, :])
         sums = term if sums is None else sums + term
     for c in range(out_ref.shape[0]):
         out_ref[c] = sums[:, c * LANES : (c + 1) * LANES] + marks
 
 
-def local_sums(seg_ids, owner_slot, lengths, hidden, chunks):
+def local_sums(seg_ids, owner_slot, hidden, chunks):
     tokens, width = hidden.shape
     docs = owner_slot.shape[0]
     pieces = 4
     return pl.pallas_call(
         functools.partial(sums_kernel, pieces),
-        in_specs=[pl.BlockSpec(memory_space=pltpu.HBM)] * 4,
+        in_specs=[pl.BlockSpec(memory_space=pltpu.HBM)] * 3,
         out_specs=pl.BlockSpec(memory_space=pltpu.VMEM),
         out_shape=pltpu.VMEM((chunks, SLOTS, LANES), jnp.float32),
         scratch_shapes=[
             pltpu.VMEM((1, tokens), jnp.int32),
             pltpu.VMEM((1, docs), jnp.int32),
-            pltpu.VMEM((1, docs), jnp.int32),
             pltpu.VMEM((tokens, width), hidden.dtype),
-            pltpu.SemaphoreType.DMA((pieces + 3,)),
+            pltpu.SemaphoreType.DMA((pieces + 2,)),
         ],
         compiler_params=pltpu.CompilerParams(vmem_limit_bytes=WIDE),
         name="local_sums",
-    )(seg_ids.reshape(1, -1), owner_slot.reshape(1, -1), lengths.reshape(1, -1), hidden)
+    )(seg_ids.reshape(1, -1), owner_slot.reshape(1, -1), hidden)
 
 
 def slots_of(in_ref):
@@ -162,7 +157,6 @@
     empty = jnp.zeros((2 * LANES - sources * SLOTS, LANES), jnp.float32)
     marks = jnp.sum(in_ref[:, SLOTS - 2 : SLOTS, :], axis=0).astype(jnp.int32)
     where = jnp.concatenate([marks[0:1, :], marks[1:2, :]], axis=1)
-    where = jnp.where(iota(where.shape, 1) < sources * SLOTS, where, 0)
     plane = jnp.where(where > 0, (where - 1) >> 5, -1)
     bound = iota((16, 2 * LANES), 0) == plane
     ahead = iota((2 * LANES, 2 * LANES), 0) < iota((2 * LANES, 2 * LANES), 1)
@@ -171,10 +165,9 @@
     return jnp.concatenate([values, empty], axis=0), where, plane, bound, rank
 
 
-def place_kernel(in_ref, out_ref, kept_ref, over_ref):
+def place_kernel(in_ref, out_ref, ready_ref):
     planes = out_ref.shape[0]
-    kept_ref[...] = in_ref[...]
-    over_ref[0] = jnp.max(in_ref[0, SLOTS - 1 : SLOTS, LANES - 1 : LANES]).astype(jnp.int32)
+    ready_ref[...] = jnp.zeros_like(ready_ref)
     values, where, plane, bound, rank = slots_of(in_ref)
     target = jnp.where((where > 0) & (rank < FIT), plane * ROWS + rank, -1)
     placed = picked(ones(iota((planes * ROWS, 2 * LANES), 0) == target), values)
@@ -194,16 +187,33 @@
         out_specs=[
             pl.BlockSpec(memory_space=pltpu.VMEM),
             pl.BlockSpec(memory_space=pltpu.VMEM),
-            pl.BlockSpec(memory_space=pltpu.SMEM),
         ],
         out_shape=[
             pltpu.VMEM((planes, ROWS, LANES), jnp.float32),
-            pltpu.VMEM(slots.shape, slots.dtype),
-            jax.ShapeDtypeStruct((1,), jnp.int32),
+            pltpu.VMEM((8, LANES), jnp.int32),
         ],
         compiler_params=pltpu.CompilerParams(vmem_limit_bytes=GRANT),
         name="place",
     )(slots)
+
+
+def crowded_kernel(tokens, ready_ref, owner_ref, length_ref, over_ref):
+    most = most_rows(length_ref[...], owner_ref[...], tokens)
+    over_ref[0] = (most + jnp.max(ready_ref[...]) > FIT).astype(jnp.int32)
+
+
+def crowded(ready, owner_slot, lengths, tokens):
+    docs = owner_slot.shape[0]
+    return pl.pallas_call(
+        functools.partial(crowded_kernel, tokens),
+        out_specs=pl.BlockSpec(memory_space=pltpu.SMEM),
+        out_shape=jax.ShapeDtypeStruct((1,), jnp.int32),
+        cost_estimate=pl.CostEstimate(
+            flops=64 * docs * docs, bytes_accessed=8 * docs, transcendentals=0
+        ),
+        compiler_params=pltpu.CompilerParams(vmem_limit_bytes=GRANT),
+        name="crowded",
+    )(ready, owner_slot.reshape(1, -1), lengths.reshape(1, -1))
 
 
 def place_rest_kernel(in_ref, out_ref):
@@ -290,8 +300,9 @@
     planes = lax.axis_size("z")
     slices = lax.axis_size("y")
     per_plane = lengths.shape[0] // planes
-    slots = swap(local_sums(seg_ids, owner_slot, lengths, hidden, chunks), ("x", "c"), CHUNK_GROUP)
-    placed, kept, over = place(slots, planes)
+    slots = swap(local_sums(seg_ids, owner_slot, hidden, chunks), ("x", "c"), CHUNK_GROUP)
+    placed, ready = place(slots, planes)
+    over = crowded(ready, owner_slot, lengths, hidden.shape[0])
     rows = swap(placed, "z", PLANE_GROUP)
     args = (owner_slot, lengths, pool_bias, chunks, slices)
 
@@ -302,7 +313,7 @@
     def alone(rows, kept):
         return averages_for_owners(rows, *args)
 
-    average = lax.cond(over[0] > 0, with_rest, alone, rows, kept)
+    average = lax.cond(over[0] > 0, with_rest, alone, rows, slots)
     mine = swap(average.reshape(chunks * slices, -1, LANES), ("x", "c", "y"), OWNER_GROUP)
     return normed(mine.reshape(average.shape))
 

time: 51.5 us -> 51.2 us (level)
  waiting for transfers between devices: 6.14 us -> 5.1 us
  Pallas kernels: 4.26 us -> 5.04 us
    all_to_all x1, waiting for transfers between devices: 6.14 us -> 5.1 us  [swap(): lax.all_to_all(array, axes, split_axis=0, concat_axis=0, tiled=True, axis...]
    pallas_call x0 -> x1, Pallas kernels: none -> 1.02 us  [crowded(): pl.pallas_call(functools.partial(crowded_kernel, tokens), out_specs=pl.Bl...]
  transfers between devices with their start and end apart: 1 -> 1, of which waited for: 1 -> 1; matrix products, arithmetic and copies ran while one was open for 0% -> 0% of each run, Pallas kernels for 0% -> 2%
where the time goes in v9:
time: 51.2 us; the launch traced here: 50.9 us
  blocking collectives  26.4 us (52%)
  starting transfers between devices  13.6 us (27%)
  waiting for transfers between devices  5.1 us (10%)
  Pallas kernels  5.04 us (10%)
  between operations  0.69 us (1%)
    all_to_all x2, blocking collectives, swap(): lax.all_to_all(array, axes, split_axis=0, concat_axis=0, tiled=True, axis...  26.4 us
    all_to_all x1, starting transfers between devices, swap(): lax.all_to_all(array, axes, split_axis=0, concat_axis=0, tiled=True, axis...  13.6 us
    all_to_all x1, waiting for transfers between devices, swap(): lax.all_to_all(array, axes, split_axis=0, concat_axis=0, tiled=True, axis...  5.1 us
    pallas_call x1, Pallas kernels, local_sums(): pl.pallas_call(functools.partial(sums_kernel, pieces), in_specs=[pl.Block...  2.1 us
    pallas_call x1, Pallas kernels, place(): pl.pallas_call(place_kernel, out_specs=[pl.BlockSpec(memory_space=pltpu.V...  1.04 us
    pallas_call x1, Pallas kernels, crowded(): pl.pallas_call(functools.partial(crowded_kernel, tokens), out_specs=pl.Bl...  1.02 us
  transfers between devices with their start and end apart: 1, of which 1 were waited for; matrix products, arithmetic and copies ran while one was open for 0% of the time, Pallas kernels for 2%

profile of v9, /device:TPU:1, one launch (start us, length us, event | category | flops | bytes accessed | tf_op | source)
XLA Modules:
  0.0 50.9 jit_solution(2676904837172922475)
XLA Ops:
  0.0 0.0 copy-start
  0.0 0.0 copy-start.2
  0.0 0.0 copy-start.1
  0.0 2.1 %local_sums.1 = f32[8,24,128]{2,1,0:T(8,128)S(1)} custom-call(s32[1,1024]{1,0:T(1,128)} %bitcast.23, s32[1,512]{1,0:T(1,128)} %bitcast.14, bf16[1024,1024]{1,0:T(8,128)(2,1)} %hidden_hbm.1), custom_call_target="tpu_custom_call" | custom-call | tf_op jit(solution)/shard_map/local_sums/pallas_call | solution.py:138
  2.1 13.4 %all_to_all.20.in_ref = f32[8,24,128]{2,1,0:T(8,128)S(1)} all-to-all(f32[8,24,128]{2,1,0:T(8,128)S(1)} %local_sums.1), channel_id=1, replica_groups={{260,256,388,384,4,0,132,128},{261,257,389,385,5,1,133,129},{262,258,39..., dimensions={0} | all-to-all | bytes 196608 | tf_op jit(solution)/shard_map/all_to_all | solution.py:293
  15.5 1.0 %place.1 = (f32[16,16,128]{2,1,0:T(8,128)}, s32[8,128]{1,0:T(8,128)S(1)}) custom-call(f32[8,24,128]{2,1,0:T(8,128)S(1)} %all_to_all.20.in_ref), custom_call_target="tpu_custom_call" | custom-call | tf_op jit(solution)/shard_map/place/pallas_call | solution.py:185
  16.6 13.6 %all-to-all-start.2 = ((f32[16,16,128]{2,1,0:T(8,128)}), f32[16,16,128]{2,1,0:T(8,128)S(1)}, u32[]{:S(2)}, u32[]{:S(2)}) async-start(f32[16,16,128]{2,1,0:T(8,128)} %get-tuple-element.38), calls=%async_computation.2 | async-start | bytes 262144 | tf_op jit(solution)/shard_map/all_to_all | solution.py:293
  30.2 0.0 copy-done
  30.2 0.0 copy-done.2
  30.2 1.0 %crowded.1 = s32[1]{0:T(128)} custom-call(s32[8,128]{1,0:T(8,128)S(1)} %get-tuple-element.37.ready_ref, s32[1,512]{1,0:T(1,128)S(1)} %bitcast.15, s32[1,512]{1,0:T(1,128)S(1)} %bitcast.20), custom_call_target="tpu_custom_call" | custom-call | flops 16777216 | bytes 4096 | tf_op jit(solution)/shard_map/crowded/pallas_call | solution.py:207
  31.9 5.1 %all-to-all-done.2 = f32[16,16,128]{2,1,0:T(8,128)S(1)} async-done(((f32[16,16,128]{2,1,0:T(8,128)}), f32[16,16,128]{2,1,0:T(8,128)S(1)}, u32[]{:S(2)}, u32[]{:S(2)}) %all-to-all-start.2) | async-done | bytes 131104 | tf_op jit(solution)/shard_map/all_to_all | solution.py:293
  37.0 0.0 copy-done.1
  37.0 0.2 conditional.1
  37.0 0.2 average.2
  37.2 13.0 %all_to_all.21 = f32[32,4,128]{2,1,0:T(4,128)S(1)} all-to-all(f32[32,4,128]{2,1,0:T(4,128)S(1)} %bitcast.13), channel_id=1, replica_groups={{2,3,0,1,6,7,4,5,130,131,128,129,134,135,132,133,258,259,256,257,262,26..., dimensions={0} | all-to-all | bytes 131072 | tf_op jit(solution)/shard_map/all_to_all | solution.py:293
  50.2 0.7 %norm.1 = bf16[4,1024]{1,0:T(4,128)(2,1)} custom-call(f32[8,4,4,128]{3,2,1,0:T(4,128)S(1)} %bitcast.12), custom_call_target="tpu_custom_call" | custom-call | tf_op jit(solution)/shard_map/norm/pallas_call | solution.py:284
Async XLA Ops:
  0.0 30.2 %copy-start = (s32[512]{0:T(512)S(1)}, s32[512]{0:T(512)}, u32[]{:S(2)}) copy-start(s32[512]{0:T(512)} %param.10) | copy-start | bytes 6148
  0.0 30.2 %copy-start.2 = (s32[512]{0:T(512)S(1)}, s32[512]{0:T(512)}, u32[]{:S(2)}) copy-start(s32[512]{0:T(512)} %param.9) | copy-start | bytes 6148
  0.0 37.0 %copy-start.1 = (f32[1024]{0:T(1024)S(1)}, f32[1024]{0:T(1024)}, u32[]{:S(2)}) copy-start(f32[1024]{0:T(1024)} %param.11) | copy-start | bytes 12292
  16.6 20.4 %all-to-all-start.2 = ((f32[16,16,128]{2,1,0:T(8,128)}), f32[16,16,128]{2,1,0:T(8,128)S(1)}, u32[]{:S(2)}, u32[]{:S(2)}) async-start(f32[16,16,128]{2,1,0:T(8,128)} %get-tuple-element.38), calls=%async_computation.2 | async-start | bytes 262144 | tf_op jit(solution)/shard_map/all_to_all | solution.py:293

commit v10 on v9

--- a/solution.py
+++ b/solution.py
@@ -11,8 +11,9 @@
 USED = 17
 SLOTS = 24
 LANES = 128
-FIT = 14
-ROWS = 16
+FIT = 11
+ROWS = 12
+PAIRS = 8
 GRANT = 16 * 1024 * 1024
 WIDE = 56 * 1024 * 1024
 
@@ -22,7 +23,7 @@
 
 
 def plane_place(z):
-    return (z + 8) & 15
+    return (z + 6) & 15
 
 
 def slice_place():
@@ -30,8 +31,8 @@
 
 
 CHUNK_GROUP = [[(((j >> 1) + 2) & 3) * 2 + (j & 1) ^ 1 for j in range(8)]]
-PLANE_GROUP = [[(j + 8) & 15 for j in range(16)]]
-OWNER_GROUP = [[(j & ~3) + ((j + 2) & 3) for j in range(32)]]
+PLANE_GROUP = [[(j + 10) & 15 for j in range(16)]]
+OWNER_GROUP = [[((j & ~3) ^ 4) + ((j + 2) & 3) for j in range(32)]]
 
 
 def plane_row(owner):
@@ -166,19 +167,16 @@
 
 
 def place_kernel(in_ref, out_ref, ready_ref):
-    planes = out_ref.shape[0]
+    planes = out_ref.shape[0] // ROWS
     ready_ref[...] = jnp.zeros_like(ready_ref)
     values, where, plane, bound, rank = slots_of(in_ref)
     target = jnp.where((where > 0) & (rank < FIT), plane * ROWS + rank, -1)
-    placed = picked(ones(iota((planes * ROWS, 2 * LANES), 0) == target), values)
-    number = jnp.where(bound, ((where - 1) & 31) + 1, 0)
-    lane = iota((2 * LANES, 2 * LANES), 0) - plane_place(lax.axis_index("z")) * ROWS
-    numbers = dot_rows(small(number), ones((lane == rank) & (rank < FIT)))
-    placed = placed.reshape(out_ref.shape)
-    line = iota(out_ref.shape, 1)
-    near = numbers[:, :LANES].reshape(planes, 1, LANES)
-    far = numbers[:, LANES:].reshape(planes, 1, LANES)
-    out_ref[...] = jnp.where(line == FIT, near, jnp.where(line == FIT + 1, far, placed))
+    out_ref[...] = picked(ones(iota((planes * ROWS, 2 * LANES), 0) == target), values)
+    number = (((where - 1) & 31) + 1) * jnp.where((rank & 1) == 1, 64, 1)
+    lane = iota((LANES, 2 * LANES), 0) - plane_place(lax.axis_index("z")) * PAIRS
+    numbers = dot_rows(small(jnp.where(bound, number, 0)), ones((lane == rank >> 1) & (rank < FIT)))
+    for p in range(planes):
+        out_ref[p * ROWS + FIT : (p + 1) * ROWS, :] = numbers[p : p + 1, :]
 
 
 def place(slots, planes):
@@ -189,7 +187,7 @@
             pl.BlockSpec(memory_space=pltpu.VMEM),
         ],
         out_shape=[
-            pltpu.VMEM((planes, ROWS, LANES), jnp.float32),
+            pltpu.VMEM((planes * ROWS, LANES), jnp.float32),
             pltpu.VMEM((8, LANES), jnp.int32),
         ],
         compiler_params=pltpu.CompilerParams(vmem_limit_bytes=GRANT),
@@ -234,12 +232,24 @@
 
 def average_kernel(owner_ref, length_ref, bias_ref, in_ref, *rest_and_out):
     out_ref = rest_and_out[-1]
-    planes = in_ref.shape[0]
+    count = in_ref.shape[0]
+    planes = count // ROWS
     per_plane = owner_ref.shape[1] // planes
-    marks = jnp.sum(in_ref[:, FIT : FIT + 2, :], axis=0).astype(jnp.int32)
-    where = jnp.concatenate([marks[0:1, :], marks[1:2, :]], axis=1)
-    picker = ones(iota((per_plane, planes * ROWS), 0) + 1 == where)
-    total = picked(picker, in_ref[...].reshape(planes * ROWS, LANES))
+    marks = in_ref[FIT:ROWS, :]
+    for p in range(1, planes):
+        marks = marks + in_ref[p * ROWS + FIT : (p + 1) * ROWS, :]
+    marks = marks.astype(jnp.int32)
+    part = iota((8, LANES), 0)
+    halves = jnp.where(part == 0, marks & 63, jnp.where(part == 1, marks >> 6, 0))
+    line = iota((LANES, count), 1)
+    source = (line * 171) >> 11
+    spread = dot(small(halves), ones(iota((LANES, count), 0) == source * PAIRS + ((line - source * ROWS) >> 1)))
+    line = line[0:1, :]
+    line = line - ((line * 171) >> 11) * ROWS
+    where = jnp.where((line & 1) == 1, spread[1:2, :], spread[0:1, :]).astype(jnp.int32)
+    where = jnp.where(line < FIT, where, 0)
+    picker = ones(iota((per_plane, count), 0) + 1 == where)
+    total = picked(picker, in_ref[...])
     for rest_ref in rest_and_out[:-1]:
         total = total + jnp.sum(rest_ref[...], axis=0)
     mine = plane_place(lax.axis_index("z")) * per_plane
@@ -254,11 +264,11 @@
     owners, copies, rows, _ = out_ref.shape
     for o in range(owners):
         for y in range(copies):
-            out_ref[o, y] = average[o * rows : (o + 1) * rows, :]
+            out_ref[o ^ 1, y] = average[o * rows : (o + 1) * rows, :]
 
 
 def averages_for_owners(arrived, owner_slot, lengths, pool_bias, owners, copies, *rest):
-    rows = owner_slot.shape[0] // (arrived.shape[0] * owners)
+    rows = owner_slot.shape[0] // (arrived.shape[0] // ROWS * owners)
     return pl.pallas_call(
         average_kernel,
         out_shape=jax.ShapeDtypeStruct((owners, copies, rows, LANES), jnp.float32),
@@ -275,7 +285,7 @@
     scale = lax.rsqrt(energy + 1e-06)
     mine = slice_place()
     for c, device in enumerate(CHUNK_GROUP[0]):
-        values = in_ref[device, mine] * scale
+        values = in_ref[device ^ 1, mine] * scale
         out_ref[:, c * LANES : (c + 1) * LANES] = values.astype(jnp.bfloat16)
 
 
@@ -303,7 +313,7 @@
     slots = swap(local_sums(seg_ids, owner_slot, hidden, chunks), ("x", "c"), CHUNK_GROUP)
     placed, ready = place(slots, planes)
     over = crowded(ready, owner_slot, lengths, hidden.shape[0])
-    rows = swap(placed, "z", PLANE_GROUP)
+    rows = swap(placed.reshape(-1, 4, LANES), "z", PLANE_GROUP).reshape(placed.shape)
     args = (owner_slot, lengths, pool_bias, chunks, slices)
 
     def with_rest(rows, kept):

time: 51.2 us -> 49.5 us (0.967)
  starting transfers between devices: 13.6 us -> 11.8 us
    all_to_all x1, starting transfers between devices: 13.6 us -> 11.8 us  [swap(): lax.all_to_all(array, axes, split_axis=0, concat_axis=0, tiled=True, axis...]
where the time goes in v10:
time: 49.5 us; the launch traced here: 49.3 us
  blocking collectives  26.8 us (54%)
  starting transfers between devices  11.8 us (24%)
  Pallas kernels  5.08 us (10%)
  waiting for transfers between devices  4.8 us (10%)
  between operations  0.69 us (1%)
    all_to_all x2, blocking collectives, swap(): lax.all_to_all(array, axes, split_axis=0, concat_axis=0, tiled=True, axis...  26.8 us
    all_to_all x1, starting transfers between devices, swap(): lax.all_to_all(array, axes, split_axis=0, concat_axis=0, tiled=True, axis...  11.8 us
    all_to_all x1, waiting for transfers between devices, swap(): lax.all_to_all(array, axes, split_axis=0, concat_axis=0, tiled=True, axis...  4.8 us
    pallas_call x1, Pallas kernels, local_sums(): pl.pallas_call(functools.partial(sums_kernel, pieces), in_specs=[pl.Block...  2.1 us
    pallas_call x1, Pallas kernels, crowded(): pl.pallas_call(functools.partial(crowded_kernel, tokens), out_specs=pl.Bl...  1.02 us
  transfers between devices with their start and end apart: 1, of which 1 were waited for; matrix products, arithmetic and copies ran while one was open for 0% of the time, Pallas kernels for 2%

profile of v10, /device:TPU:1, one launch (start us, length us, event | category | flops | bytes accessed | tf_op | source)
XLA Modules:
  0.0 49.3 jit_solution(3700299715938921152)
XLA Ops:
  0.0 0.0 copy-start
  0.0 0.0 copy-start.2
  0.0 0.0 copy-start.1
  0.0 2.1 %local_sums.1 = f32[8,24,128]{2,1,0:T(8,128)S(1)} custom-call(s32[1,1024]{1,0:T(1,128)} %bitcast.27, s32[1,512]{1,0:T(1,128)} %bitcast.18, bf16[1024,1024]{1,0:T(8,128)(2,1)} %hidden_hbm.1), custom_call_target="tpu_custom_call" | custom-call | tf_op jit(solution)/shard_map/local_sums/pallas_call | solution.py:139
  2.1 13.4 %all_to_all.20.in_ref = f32[8,24,128]{2,1,0:T(8,128)S(1)} all-to-all(f32[8,24,128]{2,1,0:T(8,128)S(1)} %local_sums.1), channel_id=1, replica_groups={{260,256,388,384,4,0,132,128},{261,257,389,385,5,1,133,129},{262,258,39..., dimensions={0} | all-to-all | bytes 196608 | tf_op jit(solution)/shard_map/all_to_all | solution.py:303
  15.5 1.0 %place.1 = (f32[192,128]{1,0:T(8,128)}, s32[8,128]{1,0:T(8,128)S(1)}) custom-call(f32[8,24,128]{2,1,0:T(8,128)S(1)} %all_to_all.20.in_ref), custom_call_target="tpu_custom_call" | custom-call | tf_op jit(solution)/shard_map/place/pallas_call | solution.py:183
  16.5 11.8 %all-to-all-start.2 = ((f32[48,4,128]{2,1,0:T(4,128)}), f32[48,4,128]{2,1,0:T(4,128)S(1)}, u32[]{:S(2)}, u32[]{:S(2)}) async-start(f32[48,4,128]{2,1,0:T(4,128)} %bitcast.10), calls=%async_computation.2 | async-start | bytes 196608 | tf_op jit(solution)/shard_map/all_to_all | solution.py:303
  28.4 0.0 copy-done
  28.4 0.0 copy-done.2
  28.4 1.0 %crowded.1 = s32[1]{0:T(128)} custom-call(s32[8,128]{1,0:T(8,128)S(1)} %get-tuple-element.37.ready_ref, s32[1,512]{1,0:T(1,128)S(1)} %bitcast.19, s32[1,512]{1,0:T(1,128)S(1)} %bitcast.24), custom_call_target="tpu_custom_call" | custom-call | flops 16777216 | bytes 4096 | tf_op jit(solution)/shard_map/crowded/pallas_call | solution.py:205
  30.1 4.8 %all-to-all-done.2 = f32[48,4,128]{2,1,0:T(4,128)S(1)} async-done(((f32[48,4,128]{2,1,0:T(4,128)}), f32[48,4,128]{2,1,0:T(4,128)S(1)}, u32[]{:S(2)}, u32[]{:S(2)}) %all-to-all-start.2) | async-done | bytes 98336 | tf_op jit(solution)/shard_map/all_to_all | solution.py:303
  34.9 0.0 copy-done.1
  34.9 0.3 conditional.1
  34.9 0.3 average.2
  35.1 13.4 %all_to_all.21 = f32[32,4,128]{2,1,0:T(4,128)S(1)} all-to-all(f32[32,4,128]{2,1,0:T(4,128)S(1)} %bitcast.17), channel_id=1, replica_groups={{6,7,4,5,2,3,0,1,134,135,132,133,130,131,128,129,262,263,260,261,258,25..., dimensions={0} | all-to-all | bytes 131072 | tf_op jit(solution)/shard_map/all_to_all | solution.py:303
  48.5 0.7 %norm.1 = bf16[4,1024]{1,0:T(4,128)(2,1)} custom-call(f32[8,4,4,128]{3,2,1,0:T(4,128)S(1)} %bitcast.14), custom_call_target="tpu_custom_call" | custom-call | tf_op jit(solution)/shard_map/norm/pallas_call | solution.py:294
Async XLA Ops:
  0.0 28.4 %copy-start = (s32[512]{0:T(512)S(1)}, s32[512]{0:T(512)}, u32[]{:S(2)}) copy-start(s32[512]{0:T(512)} %param.10) | copy-start | bytes 6148
  0.0 28.4 %copy-start.2 = (s32[512]{0:T(512)S(1)}, s32[512]{0:T(512)}, u32[]{:S(2)}) copy-start(s32[512]{0:T(512)} %param.9) | copy-start | bytes 6148
  0.0 34.9 %copy-start.1 = (f32[1024]{0:T(1024)S(1)}, f32[1024]{0:T(1024)}, u32[]{:S(2)}) copy-start(f32[1024]{0:T(1024)} %param.11) | copy-start | bytes 12292
  16.5 18.3 %all-to-all-start.2 = ((f32[48,4,128]{2,1,0:T(4,128)}), f32[48,4,128]{2,1,0:T(4,128)S(1)}, u32[]{:S(2)}, u32[]{:S(2)}) async-start(f32[48,4,128]{2,1,0:T(4,128)} %bitcast.10), calls=%async_computation.2 | async-start | bytes 196608 | tf_op jit(solution)/shard_map/all_to_all | solution.py:303

commit v11 on v10

--- a/solution.py
+++ b/solution.py
@@ -23,7 +23,7 @@
 
 
 def plane_place(z):
-    return (z + 6) & 15
+    return (z + 4) & 15
 
 
 def slice_place():
@@ -31,7 +31,7 @@
 
 
 CHUNK_GROUP = [[(((j >> 1) + 2) & 3) * 2 + (j & 1) ^ 1 for j in range(8)]]
-PLANE_GROUP = [[(j + 10) & 15 for j in range(16)]]
+PLANE_GROUP = [[(j + 12) & 15 for j in range(16)]]
 OWNER_GROUP = [[((j & ~3) ^ 4) + ((j + 2) & 3) for j in range(32)]]
 
 
@@ -135,7 +135,7 @@
 def local_sums(seg_ids, owner_slot, hidden, chunks):
     tokens, width = hidden.shape
     docs = owner_slot.shape[0]
-    pieces = 4
+    pieces = 8
     return pl.pallas_call(
         functools.partial(sums_kernel, pieces),
         in_specs=[pl.BlockSpec(memory_space=pltpu.HBM)] * 3,

time: 49.5 us -> 51.5 us (1.040)
  waiting for transfers between devices: 4.8 us -> 7.55 us
  starting transfers between devices: 11.8 us -> 10.5 us
    all_to_all x1, waiting for transfers between devices: 4.8 us -> 7.55 us  [swap(): lax.all_to_all(array, axes, split_axis=0, concat_axis=0, tiled=True, axis...]
    all_to_all x1, starting transfers between devices: 11.8 us -> 10.5 us  [swap(): lax.all_to_all(array, axes, split_axis=0, concat_axis=0, tiled=True, axis...]
where the time goes in v11:
time: 51.5 us; the launch traced here: 51.2 us
  blocking collectives  26.9 us (52%)
  starting transfers between devices  10.5 us (20%)
  waiting for transfers between devices  7.55 us (15%)
  Pallas kernels  5.54 us (11%)
  between operations  0.69 us (1%)
    all_to_all x2, blocking collectives, swap(): lax.all_to_all(array, axes, split_axis=0, concat_axis=0, tiled=True, axis...  26.9 us
    all_to_all x1, starting transfers between devices, swap(): lax.all_to_all(array, axes, split_axis=0, concat_axis=0, tiled=True, axis...  10.5 us
    all_to_all x1, waiting for transfers between devices, swap(): lax.all_to_all(array, axes, split_axis=0, concat_axis=0, tiled=True, axis...  7.55 us
    pallas_call x1, Pallas kernels, local_sums(): pl.pallas_call(functools.partial(sums_kernel, pieces), in_specs=[pl.Block...  2.56 us
  transfers between devices with their start and end apart: 1, of which 1 were waited for; matrix products, arithmetic and copies ran while one was open for 0% of the time, Pallas kernels for 2%

profile of v11, /device:TPU:1, one launch (start us, length us, event | category | flops | bytes accessed | tf_op | source)
XLA Modules:
  0.0 51.2 jit_solution(13630735551235013278)
XLA Ops:
  0.0 0.0 copy-start
  0.0 0.0 copy-start.2
  0.0 0.0 copy-start.1
  0.0 2.6 %local_sums.1 = f32[8,24,128]{2,1,0:T(8,128)S(1)} custom-call(s32[1,1024]{1,0:T(1,128)} %bitcast.27, s32[1,512]{1,0:T(1,128)} %bitcast.18, bf16[1024,1024]{1,0:T(8,128)(2,1)} %hidden_hbm.1), custom_call_target="tpu_custom_call" | custom-call | tf_op jit(solution)/shard_map/local_sums/pallas_call | solution.py:139
  2.6 13.4 %all_to_all.20.in_ref = f32[8,24,128]{2,1,0:T(8,128)S(1)} all-to-all(f32[8,24,128]{2,1,0:T(8,128)S(1)} %local_sums.1), channel_id=1, replica_groups={{260,256,388,384,4,0,132,128},{261,257,389,385,5,1,133,129},{262,258,39..., dimensions={0} | all-to-all | bytes 196608 | tf_op jit(solution)/shard_map/all_to_all | solution.py:303
  16.0 1.0 %place.1 = (f32[192,128]{1,0:T(8,128)}, s32[8,128]{1,0:T(8,128)S(1)}) custom-call(f32[8,24,128]{2,1,0:T(8,128)S(1)} %all_to_all.20.in_ref), custom_call_target="tpu_custom_call" | custom-call | tf_op jit(solution)/shard_map/place/pallas_call | solution.py:183
  17.0 10.5 %all-to-all-start.2 = ((f32[48,4,128]{2,1,0:T(4,128)}), f32[48,4,128]{2,1,0:T(4,128)S(1)}, u32[]{:S(2)}, u32[]{:S(2)}) async-start(f32[48,4,128]{2,1,0:T(4,128)} %bitcast.10), calls=%async_computation.2 | async-start | bytes 196608 | tf_op jit(solution)/shard_map/all_to_all | solution.py:303
  27.4 0.0 copy-done
  27.5 0.0 copy-done.2
  27.5 1.0 %crowded.1 = s32[1]{0:T(128)} custom-call(s32[8,128]{1,0:T(8,128)S(1)} %get-tuple-element.37.ready_ref, s32[1,512]{1,0:T(1,128)S(1)} %bitcast.19, s32[1,512]{1,0:T(1,128)S(1)} %bitcast.24), custom_call_target="tpu_custom_call" | custom-call | flops 16777216 | bytes 4096 | tf_op jit(solution)/shard_map/crowded/pallas_call | solution.py:205
  29.1 7.5 %all-to-all-done.2 = f32[48,4,128]{2,1,0:T(4,128)S(1)} async-done(((f32[48,4,128]{2,1,0:T(4,128)}), f32[48,4,128]{2,1,0:T(4,128)S(1)}, u32[]{:S(2)}, u32[]{:S(2)}) %all-to-all-start.2) | async-done | bytes 98336 | tf_op jit(solution)/shard_map/all_to_all | solution.py:303
  36.7 0.0 copy-done.1
  36.7 0.3 conditional.1
  36.7 0.3 average.2
  37.0 13.5 %all_to_all.21 = f32[32,4,128]{2,1,0:T(4,128)S(1)} all-to-all(f32[32,4,128]{2,1,0:T(4,128)S(1)} %bitcast.17), channel_id=1, replica_groups={{6,7,4,5,2,3,0,1,134,135,132,133,130,131,128,129,262,263,260,261,258,25..., dimensions={0} | all-to-all | bytes 131072 | tf_op jit(solution)/shard_map/all_to_all | solution.py:303
  50.5 0.7 %norm.1 = bf16[4,1024]{1,0:T(4,128)(2,1)} custom-call(f32[8,4,4,128]{3,2,1,0:T(4,128)S(1)} %bitcast.14), custom_call_target="tpu_custom_call" | custom-call | tf_op jit(solution)/shard_map/norm/pallas_call | solution.py:294
Async XLA Ops:
  0.0 27.5 %copy-start = (s32[512]{0:T(512)S(1)}, s32[512]{0:T(512)}, u32[]{:S(2)}) copy-start(s32[512]{0:T(512)} %param.10) | copy-start | bytes 6148
  0.0 27.5 %copy-start.2 = (s32[512]{0:T(512)S(1)}, s32[512]{0:T(512)}, u32[]{:S(2)}) copy-start(s32[512]{0:T(512)} %param.9) | copy-start | bytes 6148
  0.0 36.7 %copy-start.1 = (f32[1024]{0:T(1024)S(1)}, f32[1024]{0:T(1024)}, u32[]{:S(2)}) copy-start(f32[1024]{0:T(1024)} %param.11) | copy-start | bytes 12292
  17.0 19.7 %all-to-all-start.2 = ((f32[48,4,128]{2,1,0:T(4,128)}), f32[48,4,128]{2,1,0:T(4,128)S(1)}, u32[]{:S(2)}, u32[]{:S(2)}) async-start(f32[48,4,128]{2,1,0:T(4,128)} %bitcast.10), calls=%async_computation.2 | async-start | bytes 196608 | tf_op jit(solution)/shard_map/all_to_all | solution.py:303

commit v12 on v10

--- a/solution.py
+++ b/solution.py
@@ -135,7 +135,7 @@
 def local_sums(seg_ids, owner_slot, hidden, chunks):
     tokens, width = hidden.shape
     docs = owner_slot.shape[0]
-    pieces = 4
+    pieces = 2
     return pl.pallas_call(
         functools.partial(sums_kernel, pieces),
         in_specs=[pl.BlockSpec(memory_space=pltpu.HBM)] * 3,

time: 49.5 us -> 49.6 us (level)
  no operation moved by 1% of the time
where the time goes in v12:
time: 49.6 us; the launch traced here: 49.3 us
  blocking collectives  26.8 us (54%)
  starting transfers between devices  11.8 us (24%)
  Pallas kernels  5.1 us (10%)
  waiting for transfers between devices  4.8 us (10%)
  between operations  0.69 us (1%)
    all_to_all x2, blocking collectives, swap(): lax.all_to_all(array, axes, split_axis=0, concat_axis=0, tiled=True, axis...  26.8 us
    all_to_all x1, starting transfers between devices, swap(): lax.all_to_all(array, axes, split_axis=0, concat_axis=0, tiled=True, axis...  11.8 us
    all_to_all x1, waiting for transfers between devices, swap(): lax.all_to_all(array, axes, split_axis=0, concat_axis=0, tiled=True, axis...  4.8 us
    pallas_call x1, Pallas kernels, local_sums(): pl.pallas_call(functools.partial(sums_kernel, pieces), in_specs=[pl.Block...  2.12 us
    pallas_call x1, Pallas kernels, crowded(): pl.pallas_call(functools.partial(crowded_kernel, tokens), out_specs=pl.Bl...  1.02 us
  transfers between devices with their start and end apart: 1, of which 1 were waited for; matrix products, arithmetic and copies ran while one was open for 0% of the time, Pallas kernels for 2%

profile of v12, /device:TPU:1, one launch (start us, length us, event | category | flops | bytes accessed | tf_op | source)
XLA Modules:
  0.0 49.3 jit_solution(18423569511064923834)
XLA Ops:
  0.0 0.0 copy-start
  0.0 0.0 copy-start.2
  0.0 0.0 copy-start.1
  0.0 2.1 %local_sums.1 = f32[8,24,128]{2,1,0:T(8,128)S(1)} custom-call(s32[1,1024]{1,0:T(1,128)} %bitcast.27, s32[1,512]{1,0:T(1,128)} %bitcast.18, bf16[1024,1024]{1,0:T(8,128)(2,1)} %hidden_hbm.1), custom_call_target="tpu_custom_call" | custom-call | tf_op jit(solution)/shard_map/local_sums/pallas_call | solution.py:139
  2.1 13.4 %all_to_all.20.in_ref = f32[8,24,128]{2,1,0:T(8,128)S(1)} all-to-all(f32[8,24,128]{2,1,0:T(8,128)S(1)} %local_sums.1), channel_id=1, replica_groups={{260,256,388,384,4,0,132,128},{261,257,389,385,5,1,133,129},{262,258,39..., dimensions={0} | all-to-all | bytes 196608 | tf_op jit(solution)/shard_map/all_to_all | solution.py:303
  15.6 1.0 %place.1 = (f32[192,128]{1,0:T(8,128)}, s32[8,128]{1,0:T(8,128)S(1)}) custom-call(f32[8,24,128]{2,1,0:T(8,128)S(1)} %all_to_all.20.in_ref), custom_call_target="tpu_custom_call" | custom-call | tf_op jit(solution)/shard_map/place/pallas_call | solution.py:183
  16.5 11.8 %all-to-all-start.2 = ((f32[48,4,128]{2,1,0:T(4,128)}), f32[48,4,128]{2,1,0:T(4,128)S(1)}, u32[]{:S(2)}, u32[]{:S(2)}) async-start(f32[48,4,128]{2,1,0:T(4,128)} %bitcast.10), calls=%async_computation.2 | async-start | bytes 196608 | tf_op jit(solution)/shard_map/all_to_all | solution.py:303
  28.4 0.0 copy-done
  28.4 0.0 copy-done.2
  28.4 1.0 %crowded.1 = s32[1]{0:T(128)} custom-call(s32[8,128]{1,0:T(8,128)S(1)} %get-tuple-element.37.ready_ref, s32[1,512]{1,0:T(1,128)S(1)} %bitcast.19, s32[1,512]{1,0:T(1,128)S(1)} %bitcast.24), custom_call_target="tpu_custom_call" | custom-call | flops 16777216 | bytes 4096 | tf_op jit(solution)/shard_map/crowded/pallas_call | solution.py:205
  30.1 4.8 %all-to-all-done.2 = f32[48,4,128]{2,1,0:T(4,128)S(1)} async-done(((f32[48,4,128]{2,1,0:T(4,128)}), f32[48,4,128]{2,1,0:T(4,128)S(1)}, u32[]{:S(2)}, u32[]{:S(2)}) %all-to-all-start.2) | async-done | bytes 98336 | tf_op jit(solution)/shard_map/all_to_all | solution.py:303
  34.9 0.0 copy-done.1
  34.9 0.3 conditional.1
  34.9 0.3 average.2
  35.2 13.4 %all_to_all.21 = f32[32,4,128]{2,1,0:T(4,128)S(1)} all-to-all(f32[32,4,128]{2,1,0:T(4,128)S(1)} %bitcast.17), channel_id=1, replica_groups={{6,7,4,5,2,3,0,1,134,135,132,133,130,131,128,129,262,263,260,261,258,25..., dimensions={0} | all-to-all | bytes 131072 | tf_op jit(solution)/shard_map/all_to_all | solution.py:303
  48.6 0.7 %norm.1 = bf16[4,1024]{1,0:T(4,128)(2,1)} custom-call(f32[8,4,4,128]{3,2,1,0:T(4,128)S(1)} %bitcast.14), custom_call_target="tpu_custom_call" | custom-call | tf_op jit(solution)/shard_map/norm/pallas_call | solution.py:294
Async XLA Ops:
  0.0 28.4 %copy-start = (s32[512]{0:T(512)S(1)}, s32[512]{0:T(512)}, u32[]{:S(2)}) copy-start(s32[512]{0:T(512)} %param.10) | copy-start | bytes 6148
  0.0 28.4 %copy-start.2 = (s32[512]{0:T(512)S(1)}, s32[512]{0:T(512)}, u32[]{:S(2)}) copy-start(s32[512]{0:T(512)} %param.9) | copy-start | bytes 6148
  0.0 34.9 %copy-start.1 = (f32[1024]{0:T(1024)S(1)}, f32[1024]{0:T(1024)}, u32[]{:S(2)}) copy-start(f32[1024]{0:T(1024)} %param.11) | copy-start | bytes 12292
  16.5 18.3 %all-to-all-start.2 = ((f32[48,4,128]{2,1,0:T(4,128)}), f32[48,4,128]{2,1,0:T(4,128)S(1)}, u32[]{:S(2)}, u32[]{:S(2)}) async-start(f32[48,4,128]{2,1,0:T(4,128)} %bitcast.10), calls=%async_computation.2 | async-start | bytes 196608 | tf_op jit(solution)/shard_map/all_to_all | solution.py:303

commit v13 on v10

--- a/solution.py
+++ b/solution.py
@@ -14,6 +14,7 @@
 FIT = 11
 ROWS = 12
 PAIRS = 8
+SPLIT = 4
 GRANT = 16 * 1024 * 1024
 WIDE = 56 * 1024 * 1024
 
@@ -23,7 +24,7 @@
 
 
 def plane_place(z):
-    return (z + 6) & 15
+    return (z + 7) & 15
 
 
 def slice_place():
@@ -31,7 +32,7 @@
 
 
 CHUNK_GROUP = [[(((j >> 1) + 2) & 3) * 2 + (j & 1) ^ 1 for j in range(8)]]
-PLANE_GROUP = [[(j + 10) & 15 for j in range(16)]]
+PLANE_GROUP = [[(j + 9) & 15 for j in range(16)]]
 OWNER_GROUP = [[((j & ~3) ^ 4) + ((j + 2) & 3) for j in range(32)]]
 
 
@@ -108,11 +109,12 @@
     tokens = hidden.shape[0]
     rows = tokens // pieces
     copies = [
-        pltpu.make_async_copy(seg_hbm, seg, sems.at[pieces]),
-        pltpu.make_async_copy(owner_hbm, owner, sems.at[pieces + 1]),
+        pltpu.make_async_copy(seg_hbm, seg, sems.at[pieces * SPLIT]),
+        pltpu.make_async_copy(owner_hbm, owner, sems.at[pieces * SPLIT + 1]),
     ]
-    for p in range(pieces):
-        here = pl.ds(p * rows, rows)
+    few = rows // SPLIT
+    for p in range(pieces * SPLIT):
+        here = pl.ds(p * few, few)
         copies.append(pltpu.make_async_copy(hidden_hbm.at[here], hidden.at[here], sems.at[p]))
     for copy in copies:
         copy.start()
@@ -125,7 +127,8 @@
     sums = None
     for p in range(pieces):
         picker = ones(slot == seg[:, p * rows : (p + 1) * rows])
-        copies[2 + p].wait()
+        for copy in copies[2 + p * SPLIT : 2 + (p + 1) * SPLIT]:
+            copy.wait()
         term = dot(picker, hidden[p * rows : (p + 1) * rows, :])
         sums = term if sums is None else sums + term
     for c in range(out_ref.shape[0]):
@@ -145,7 +148,7 @@
             pltpu.VMEM((1, tokens), jnp.int32),
             pltpu.VMEM((1, docs), jnp.int32),
             pltpu.VMEM((tokens, width), hidden.dtype),
-            pltpu.SemaphoreType.DMA((pieces + 2,)),
+            pltpu.SemaphoreType.DMA((pieces * SPLIT + 2,)),
         ],
         compiler_params=pltpu.CompilerParams(vmem_limit_bytes=WIDE),
         name="local_sums",

time: 49.5 us -> 49.8 us (level)
  starting transfers between devices: 11.8 us -> 12.7 us
  blocking collectives: 26.8 us -> 26 us
    all_to_all x1, starting transfers between devices: 11.8 us -> 12.7 us  [swap(): lax.all_to_all(array, axes, split_axis=0, concat_axis=0, tiled=True, axis...]
    all_to_all x2, blocking collectives: 26.8 us -> 26 us  [swap(): lax.all_to_all(array, axes, split_axis=0, concat_axis=0, tiled=True, axis...]
where the time goes in v13:
time: 49.8 us; the launch traced here: 49.5 us
  blocking collectives  26 us (52%)
  starting transfers between devices  12.7 us (26%)
  Pallas kernels  5.27 us (11%)
  waiting for transfers between devices  4.79 us (10%)
  between operations  0.69 us (1%)
    all_to_all x2, blocking collectives, swap(): lax.all_to_all(array, axes, split_axis=0, concat_axis=0, tiled=True, axis...  26 us
    all_to_all x1, starting transfers between devices, swap(): lax.all_to_all(array, axes, split_axis=0, concat_axis=0, tiled=True, axis...  12.7 us
    all_to_all x1, waiting for transfers between devices, swap(): lax.all_to_all(array, axes, split_axis=0, concat_axis=0, tiled=True, axis...  4.79 us
    pallas_call x1, Pallas kernels, local_sums(): pl.pallas_call(functools.partial(sums_kernel, pieces), in_specs=[pl.Block...  2.29 us
    pallas_call x1, Pallas kernels, crowded(): pl.pallas_call(functools.partial(crowded_kernel, tokens), out_specs=pl.Bl...  1.02 us
  transfers between devices with their start and end apart: 1, of which 1 were waited for; matrix products, arithmetic and copies ran while one was open for 0% of the time, Pallas kernels for 2%

profile of v13, /device:TPU:1, one launch (start us, length us, event | category | flops | bytes accessed | tf_op | source)
XLA Modules:
  0.0 49.5 jit_solution(4868581387753203664)
XLA Ops:
  0.0 0.0 copy-start
  0.0 0.0 copy-start.2
  0.0 0.0 copy-start.1
  0.0 2.3 %local_sums.1 = f32[8,24,128]{2,1,0:T(8,128)S(1)} custom-call(s32[1,1024]{1,0:T(1,128)} %bitcast.27, s32[1,512]{1,0:T(1,128)} %bitcast.18, bf16[1024,1024]{1,0:T(8,128)(2,1)} %hidden_hbm.1), custom_call_target="tpu_custom_call" | custom-call | tf_op jit(solution)/shard_map/local_sums/pallas_call | solution.py:142
  2.3 13.4 %all_to_all.20.in_ref = f32[8,24,128]{2,1,0:T(8,128)S(1)} all-to-all(f32[8,24,128]{2,1,0:T(8,128)S(1)} %local_sums.1), channel_id=1, replica_groups={{260,256,388,384,4,0,132,128},{261,257,389,385,5,1,133,129},{262,258,39..., dimensions={0} | all-to-all | bytes 196608 | tf_op jit(solution)/shard_map/all_to_all | solution.py:306
  15.7 1.0 %place.1 = (f32[192,128]{1,0:T(8,128)}, s32[8,128]{1,0:T(8,128)S(1)}) custom-call(f32[8,24,128]{2,1,0:T(8,128)S(1)} %all_to_all.20.in_ref), custom_call_target="tpu_custom_call" | custom-call | tf_op jit(solution)/shard_map/place/pallas_call | solution.py:186
  16.7 12.7 %all-to-all-start.2 = ((f32[48,4,128]{2,1,0:T(4,128)}), f32[48,4,128]{2,1,0:T(4,128)S(1)}, u32[]{:S(2)}, u32[]{:S(2)}) async-start(f32[48,4,128]{2,1,0:T(4,128)} %bitcast.10), calls=%async_computation.2 | async-start | bytes 196608 | tf_op jit(solution)/shard_map/all_to_all | solution.py:306
  29.5 0.0 copy-done
  29.5 0.0 copy-done.2
  29.5 1.0 %crowded.1 = s32[1]{0:T(128)} custom-call(s32[8,128]{1,0:T(8,128)S(1)} %get-tuple-element.37.ready_ref, s32[1,512]{1,0:T(1,128)S(1)} %bitcast.19, s32[1,512]{1,0:T(1,128)S(1)} %bitcast.24), custom_call_target="tpu_custom_call" | custom-call | flops 16777216 | bytes 4096 | tf_op jit(solution)/shard_map/crowded/pallas_call | solution.py:208
  31.2 4.8 %all-to-all-done.2 = f32[48,4,128]{2,1,0:T(4,128)S(1)} async-done(((f32[48,4,128]{2,1,0:T(4,128)}), f32[48,4,128]{2,1,0:T(4,128)S(1)}, u32[]{:S(2)}, u32[]{:S(2)}) %all-to-all-start.2) | async-done | bytes 98336 | tf_op jit(solution)/shard_map/all_to_all | solution.py:306
  35.9 0.0 copy-done.1
  35.9 0.3 conditional.1
  35.9 0.3 average.2
  36.2 12.6 %all_to_all.21 = f32[32,4,128]{2,1,0:T(4,128)S(1)} all-to-all(f32[32,4,128]{2,1,0:T(4,128)S(1)} %bitcast.17), channel_id=1, replica_groups={{6,7,4,5,2,3,0,1,134,135,132,133,130,131,128,129,262,263,260,261,258,25..., dimensions={0} | all-to-all | bytes 131072 | tf_op jit(solution)/shard_map/all_to_all | solution.py:306
  48.8 0.7 %norm.1 = bf16[4,1024]{1,0:T(4,128)(2,1)} custom-call(f32[8,4,4,128]{3,2,1,0:T(4,128)S(1)} %bitcast.14), custom_call_target="tpu_custom_call" | custom-call | tf_op jit(solution)/shard_map/norm/pallas_call | solution.py:297
Async XLA Ops:
  0.0 29.5 %copy-start = (s32[512]{0:T(512)S(1)}, s32[512]{0:T(512)}, u32[]{:S(2)}) copy-start(s32[512]{0:T(512)} %param.10) | copy-start | bytes 6148
  0.0 29.5 %copy-start.2 = (s32[512]{0:T(512)S(1)}, s32[512]{0:T(512)}, u32[]{:S(2)}) copy-start(s32[512]{0:T(512)} %param.9) | copy-start | bytes 6148
  0.0 35.9 %copy-start.1 = (f32[1024]{0:T(1024)S(1)}, f32[1024]{0:T(1024)}, u32[]{:S(2)}) copy-start(f32[1024]{0:T(1024)} %param.11) | copy-start | bytes 12292
  16.7 19.2 %all-to-all-start.2 = ((f32[48,4,128]{2,1,0:T(4,128)}), f32[48,4,128]{2,1,0:T(4,128)S(1)}, u32[]{:S(2)}, u32[]{:S(2)}) async-start(f32[48,4,128]{2,1,0:T(4,128)} %bitcast.10), calls=%async_computation.2 | async-start | bytes 196608 | tf_op jit(solution)/shard_map/all_to_all | solution.py:306

commit v14 on v10

--- a/solution.py
+++ b/solution.py
@@ -9,7 +9,7 @@
 from jax.sharding import PartitionSpec as P
 
 USED = 17
-SLOTS = 24
+SLOTS = 20
 LANES = 128
 FIT = 11
 ROWS = 12
@@ -128,8 +128,8 @@
         copies[2 + p].wait()
         term = dot(picker, hidden[p * rows : (p + 1) * rows, :])
         sums = term if sums is None else sums + term
-    for c in range(out_ref.shape[0]):
-        out_ref[c] = sums[:, c * LANES : (c + 1) * LANES] + marks
+    for c in range(out_ref.shape[0] // SLOTS):
+        out_ref[c * SLOTS : (c + 1) * SLOTS, :] = sums[:, c * LANES : (c + 1) * LANES] + marks
 
 
 def local_sums(seg_ids, owner_slot, hidden, chunks):
@@ -140,7 +140,7 @@
         functools.partial(sums_kernel, pieces),
         in_specs=[pl.BlockSpec(memory_space=pltpu.HBM)] * 3,
         out_specs=pl.BlockSpec(memory_space=pltpu.VMEM),
-        out_shape=pltpu.VMEM((chunks, SLOTS, LANES), jnp.float32),
+        out_shape=pltpu.VMEM((chunks * SLOTS, LANES), jnp.float32),
         scratch_shapes=[
             pltpu.VMEM((1, tokens), jnp.int32),
             pltpu.VMEM((1, docs), jnp.int32),
@@ -153,10 +153,13 @@
 
 
 def slots_of(in_ref):
-    sources = in_ref.shape[0]
-    values = in_ref[...].reshape(sources * SLOTS, LANES)
-    empty = jnp.zeros((2 * LANES - sources * SLOTS, LANES), jnp.float32)
-    marks = jnp.sum(in_ref[:, SLOTS - 2 : SLOTS, :], axis=0).astype(jnp.int32)
+    count = in_ref.shape[0]
+    values = in_ref[...]
+    empty = jnp.zeros((2 * LANES - count, LANES), jnp.float32)
+    marks = in_ref[SLOTS - 2 : SLOTS, :]
+    for row in range(2 * SLOTS, count + SLOTS, SLOTS):
+        marks = marks + in_ref[row - 2 : row, :]
+    marks = marks.astype(jnp.int32)
     where = jnp.concatenate([marks[0:1, :], marks[1:2, :]], axis=1)
     plane = jnp.where(where > 0, (where - 1) >> 5, -1)
     bound = iota((16, 2 * LANES), 0) == plane
@@ -310,7 +313,8 @@
     planes = lax.axis_size("z")
     slices = lax.axis_size("y")
     per_plane = lengths.shape[0] // planes
-    slots = swap(local_sums(seg_ids, owner_slot, hidden, chunks), ("x", "c"), CHUNK_GROUP)
+    sums = local_sums(seg_ids, owner_slot, hidden, chunks)
+    slots = swap(sums.reshape(-1, 4, LANES), ("x", "c"), CHUNK_GROUP).reshape(sums.shape)
     placed, ready = place(slots, planes)
     over = crowded(ready, owner_slot, lengths, hidden.shape[0])
     rows = swap(placed.reshape(-1, 4, LANES), "z", PLANE_GROUP).reshape(placed.shape)

time: 49.5 us -> 49.5 us (level)
  no operation moved by 1% of the time
where the time goes in v14:
time: 49.5 us; the launch traced here: 49.2 us
  blocking collectives  26.8 us (54%)
  starting transfers between devices  11.8 us (24%)
  Pallas kernels  5.08 us (10%)
  waiting for transfers between devices  4.81 us (10%)
  between operations  0.69 us (1%)
    all_to_all x2, blocking collectives, swap(): lax.all_to_all(array, axes, split_axis=0, concat_axis=0, tiled=True, axis...  26.8 us
    all_to_all x1, starting transfers between devices, swap(): lax.all_to_all(array, axes, split_axis=0, concat_axis=0, tiled=True, axis...  11.8 us
    all_to_all x1, waiting for transfers between devices, swap(): lax.all_to_all(array, axes, split_axis=0, concat_axis=0, tiled=True, axis...  4.81 us
    pallas_call x1, Pallas kernels, local_sums(): pl.pallas_call(functools.partial(sums_kernel, pieces), in_specs=[pl.Block...  2.1 us
    pallas_call x1, Pallas kernels, crowded(): pl.pallas_call(functools.partial(crowded_kernel, tokens), out_specs=pl.Bl...  1.02 us
  transfers between devices with their start and end apart: 1, of which 1 were waited for; matrix products, arithmetic and copies ran while one was open for 0% of the time, Pallas kernels for 2%

profile of v14, /device:TPU:1, one launch (start us, length us, event | category | flops | bytes accessed | tf_op | source)
XLA Modules:
  0.0 49.2 jit_solution(13800181105786032363)
XLA Ops:
  0.0 0.0 copy-start
  0.0 0.0 copy-start.2
  0.0 0.0 copy-start.1
  0.0 2.1 %local_sums.1 = f32[160,128]{1,0:T(8,128)S(1)} custom-call(s32[1,1024]{1,0:T(1,128)} %bitcast.32, s32[1,512]{1,0:T(1,128)} %bitcast.23, bf16[1024,1024]{1,0:T(8,128)(2,1)} %hidden_hbm.1), custom_call_target="tpu_custom_call" | custom-call | tf_op jit(solution)/shard_map/local_sums/pallas_call | solution.py:139
  2.1 13.3 %all_to_all.20 = f32[40,4,128]{2,1,0:T(4,128)S(1)} all-to-all(f32[40,4,128]{2,1,0:T(4,128)S(1)} %bitcast.16), channel_id=1, replica_groups={{260,256,388,384,4,0,132,128},{261,257,389,385,5,1,133,129},{262,258,39..., dimensions={0} | all-to-all | bytes 163840 | tf_op jit(solution)/shard_map/all_to_all | solution.py:306
  15.5 1.0 %place.1 = (f32[192,128]{1,0:T(8,128)}, s32[8,128]{1,0:T(8,128)S(1)}) custom-call(f32[160,128]{1,0:T(8,128)S(1)} %bitcast.20), custom_call_target="tpu_custom_call" | custom-call | tf_op jit(solution)/shard_map/place/pallas_call | solution.py:186
  16.4 11.8 %all-to-all-start.2 = ((f32[48,4,128]{2,1,0:T(4,128)}), f32[48,4,128]{2,1,0:T(4,128)S(1)}, u32[]{:S(2)}, u32[]{:S(2)}) async-start(f32[48,4,128]{2,1,0:T(4,128)} %bitcast.12), calls=%async_computation.2 | async-start | bytes 196608 | tf_op jit(solution)/shard_map/all_to_all | solution.py:306
  28.3 0.0 copy-done
  28.3 0.0 copy-done.2
  28.3 1.0 %crowded.1 = s32[1]{0:T(128)} custom-call(s32[8,128]{1,0:T(8,128)S(1)} %get-tuple-element.37.ready_ref, s32[1,512]{1,0:T(1,128)S(1)} %bitcast.24, s32[1,512]{1,0:T(1,128)S(1)} %bitcast.29), custom_call_target="tpu_custom_call" | custom-call | flops 16777216 | bytes 4096 | tf_op jit(solution)/shard_map/crowded/pallas_call | solution.py:208
  30.0 4.8 %all-to-all-done.2 = f32[48,4,128]{2,1,0:T(4,128)S(1)} async-done(((f32[48,4,128]{2,1,0:T(4,128)}), f32[48,4,128]{2,1,0:T(4,128)S(1)}, u32[]{:S(2)}, u32[]{:S(2)}) %all-to-all-start.2) | async-done | bytes 98336 | tf_op jit(solution)/shard_map/all_to_all | solution.py:306
  34.8 0.0 copy-done.1
  34.8 0.3 conditional.1
  34.8 0.3 average.2
  35.1 13.5 %all_to_all.21 = f32[32,4,128]{2,1,0:T(4,128)S(1)} all-to-all(f32[32,4,128]{2,1,0:T(4,128)S(1)} %bitcast.22), channel_id=1, replica_groups={{6,7,4,5,2,3,0,1,134,135,132,133,130,131,128,129,262,263,260,261,258,25..., dimensions={0} | all-to-all | bytes 131072 | tf_op jit(solution)/shard_map/all_to_all | solution.py:306
  48.5 0.7 %norm.1 = bf16[4,1024]{1,0:T(4,128)(2,1)} custom-call(f32[8,4,4,128]{3,2,1,0:T(4,128)S(1)} %bitcast.17), custom_call_target="tpu_custom_call" | custom-call | tf_op jit(solution)/shard_map/norm/pallas_call | solution.py:297
Async XLA Ops:
  0.0 28.3 %copy-start = (s32[512]{0:T(512)S(1)}, s32[512]{0:T(512)}, u32[]{:S(2)}) copy-start(s32[512]{0:T(512)} %param.10) | copy-start | bytes 6148
  0.0 28.3 %copy-start.2 = (s32[512]{0:T(512)S(1)}, s32[512]{0:T(512)}, u32[]{:S(2)}) copy-start(s32[512]{0:T(512)} %param.9) | copy-start | bytes 6148
  0.0 34.8 %copy-start.1 = (f32[1024]{0:T(1024)S(1)}, f32[1024]{0:T(1024)}, u32[]{:S(2)}) copy-start(f32[1024]{0:T(1024)} %param.11) | copy-start | bytes 12292
  16.4 18.3 %all-to-all-start.2 = ((f32[48,4,128]{2,1,0:T(4,128)}), f32[48,4,128]{2,1,0:T(4,128)S(1)}, u32[]{:S(2)}, u32[]{:S(2)}) async-start(f32[48,4,128]{2,1,0:T(4,128)} %bitcast.12), calls=%async_computation.2 | async-start | bytes 196608 | tf_op jit(solution)/shard_map/all_to_all | solution.py:306

commit v15 on v14

--- a/solution.py
+++ b/solution.py
@@ -23,7 +23,7 @@
 
 
 def plane_place(z):
-    return (z + 6) & 15
+    return (z + 6 + lax.axis_index("c")) & 15
 
 
 def slice_place():
@@ -31,12 +31,12 @@
 
 
 CHUNK_GROUP = [[(((j >> 1) + 2) & 3) * 2 + (j & 1) ^ 1 for j in range(8)]]
-PLANE_GROUP = [[(j + 10) & 15 for j in range(16)]]
+PLANE_GROUP = [[((j + 10 - c) & 15) * 2 + c for j in range(16)] for c in range(2)]
 OWNER_GROUP = [[((j & ~3) ^ 4) + ((j + 2) & 3) for j in range(32)]]
 
 
 def plane_row(owner):
-    return plane_place(owner >> 3) * 32 + (owner >> 7) * 8 + (owner & 7)
+    return ((owner >> 3) & 15) * 32 + (owner >> 7) * 8 + (owner & 7)
 
 
 def ones(mask):
@@ -161,7 +161,8 @@
         marks = marks + in_ref[row - 2 : row, :]
     marks = marks.astype(jnp.int32)
     where = jnp.concatenate([marks[0:1, :], marks[1:2, :]], axis=1)
-    plane = jnp.where(where > 0, (where - 1) >> 5, -1)
+    plane = jnp.where(where > 0, plane_place((where - 1) >> 5), -1)
+    where = jnp.where(where > 0, plane * 32 + ((where - 1) & 31) + 1, 0)
     bound = iota((16, 2 * LANES), 0) == plane
     ahead = iota((2 * LANES, 2 * LANES), 0) < iota((2 * LANES, 2 * LANES), 1)
     seen = dot(ones(bound), ones(ahead))
@@ -255,7 +256,7 @@
     total = picked(picker, in_ref[...])
     for rest_ref in rest_and_out[:-1]:
         total = total + jnp.sum(rest_ref[...], axis=0)
-    mine = plane_place(lax.axis_index("z")) * per_plane
+    mine = lax.axis_index("z") * per_plane
     row = iota((per_plane, owner_ref.shape[1]), 0) + mine
     length = jnp.sum(
         jnp.where(row == plane_row(owner_ref[...]), length_ref[...], 0).astype(jnp.float32),
@@ -317,11 +318,11 @@
     slots = swap(sums.reshape(-1, 4, LANES), ("x", "c"), CHUNK_GROUP).reshape(sums.shape)
     placed, ready = place(slots, planes)
     over = crowded(ready, owner_slot, lengths, hidden.shape[0])
-    rows = swap(placed.reshape(-1, 4, LANES), "z", PLANE_GROUP).reshape(placed.shape)
+    rows = swap(placed.reshape(-1, 4, LANES), ("z", "c"), PLANE_GROUP).reshape(placed.shape)
     args = (owner_slot, lengths, pool_bias, chunks, slices)
 
     def with_rest(rows, kept):
-        rest = swap(place_rest(kept, planes, per_plane), "z", PLANE_GROUP)
+        rest = swap(place_rest(kept, planes, per_plane), ("z", "c"), PLANE_GROUP)
         return averages_for_owners(rows, *args, rest)
 
     def alone(rows, kept):

time: 49.5 us -> 49.6 us (level)
  blocking collectives: 26.8 us -> 25.8 us
  starting transfers between devices: 11.8 us -> 12.7 us
    all_to_all x2, blocking collectives: 26.8 us -> 25.8 us  [swap(): lax.all_to_all(array, axes, split_axis=0, concat_axis=0, tiled=True, axis...]
    all_to_all x1, starting transfers between devices: 11.8 us -> 12.7 us  [swap(): lax.all_to_all(array, axes, split_axis=0, concat_axis=0, tiled=True, axis...]
where the time goes in v15:
time: 49.6 us; the launch traced here: 49.3 us
  blocking collectives  25.8 us (52%)
  starting transfers between devices  12.7 us (26%)
  Pallas kernels  5.08 us (10%)
  waiting for transfers between devices  5 us (10%)
  between operations  0.69 us (1%)
    all_to_all x2, blocking collectives, swap(): lax.all_to_all(array, axes, split_axis=0, concat_axis=0, tiled=True, axis...  25.8 us
    all_to_all x1, starting transfers between devices, swap(): lax.all_to_all(array, axes, split_axis=0, concat_axis=0, tiled=True, axis...  12.7 us
    all_to_all x1, waiting for transfers between devices, swap(): lax.all_to_all(array, axes, split_axis=0, concat_axis=0, tiled=True, axis...  5 us
    pallas_call x1, Pallas kernels, local_sums(): pl.pallas_call(functools.partial(sums_kernel, pieces), in_specs=[pl.Block...  2.1 us
    pallas_call x1, Pallas kernels, crowded(): pl.pallas_call(functools.partial(crowded_kernel, tokens), out_specs=pl.Bl...  1.02 us
  transfers between devices with their start and end apart: 1, of which 1 were waited for; matrix products, arithmetic and copies ran while one was open for 0% of the time, Pallas kernels for 2%

profile of v15, /device:TPU:1, one launch (start us, length us, event | category | flops | bytes accessed | tf_op | source)
XLA Modules:
  0.0 49.3 jit_solution(122422189102836938)
XLA Ops:
  0.0 0.0 copy-start
  0.0 0.0 copy-start.2
  0.0 0.0 copy-start.1
  0.0 2.1 %local_sums.1 = f32[160,128]{1,0:T(8,128)S(1)} custom-call(s32[1,1024]{1,0:T(1,128)} %bitcast.32, s32[1,512]{1,0:T(1,128)} %bitcast.23, bf16[1024,1024]{1,0:T(8,128)(2,1)} %hidden_hbm.1), custom_call_target="tpu_custom_call" | custom-call | tf_op jit(solution)/shard_map/local_sums/pallas_call | solution.py:139
  2.1 13.3 %all_to_all.20 = f32[40,4,128]{2,1,0:T(4,128)S(1)} all-to-all(f32[40,4,128]{2,1,0:T(4,128)S(1)} %bitcast.16), channel_id=1, replica_groups={{260,256,388,384,4,0,132,128},{261,257,389,385,5,1,133,129},{262,258,39..., dimensions={0} | all-to-all | bytes 163840 | tf_op jit(solution)/shard_map/all_to_all | solution.py:307
  15.5 1.0 %place.1 = (f32[192,128]{1,0:T(8,128)}, s32[8,128]{1,0:T(8,128)S(1)}) custom-call(f32[160,128]{1,0:T(8,128)S(1)} %bitcast.20), custom_call_target="tpu_custom_call" | custom-call | tf_op jit(solution)/shard_map/place/pallas_call | solution.py:187
  16.4 12.7 %all-to-all-start.2 = ((f32[48,4,128]{2,1,0:T(4,128)}), f32[48,4,128]{2,1,0:T(4,128)S(1)}, u32[]{:S(2)}, u32[]{:S(2)}) async-start(f32[48,4,128]{2,1,0:T(4,128)} %bitcast.12), calls=%async_computation.2 | async-start | bytes 196608 | tf_op jit(solution)/shard_map/all_to_all | solution.py:307
  29.2 0.0 copy-done
  29.2 0.0 copy-done.2
  29.2 1.0 %crowded.1 = s32[1]{0:T(128)} custom-call(s32[8,128]{1,0:T(8,128)S(1)} %get-tuple-element.37.ready_ref, s32[1,512]{1,0:T(1,128)S(1)} %bitcast.24, s32[1,512]{1,0:T(1,128)S(1)} %bitcast.29), custom_call_target="tpu_custom_call" | custom-call | flops 16777216 | bytes 4096 | tf_op jit(solution)/shard_map/crowded/pallas_call | solution.py:209
  30.9 5.0 %all-to-all-done.2 = f32[48,4,128]{2,1,0:T(4,128)S(1)} async-done(((f32[48,4,128]{2,1,0:T(4,128)}), f32[48,4,128]{2,1,0:T(4,128)S(1)}, u32[]{:S(2)}, u32[]{:S(2)}) %all-to-all-start.2) | async-done | bytes 98336 | tf_op jit(solution)/shard_map/all_to_all | solution.py:307
  35.9 0.0 copy-done.1
  35.9 0.3 conditional.1
  35.9 0.3 average.2
  36.2 12.4 %all_to_all.21 = f32[32,4,128]{2,1,0:T(4,128)S(1)} all-to-all(f32[32,4,128]{2,1,0:T(4,128)S(1)} %bitcast.22), channel_id=1, replica_groups={{6,7,4,5,2,3,0,1,134,135,132,133,130,131,128,129,262,263,260,261,258,25..., dimensions={0} | all-to-all | bytes 131072 | tf_op jit(solution)/shard_map/all_to_all | solution.py:307
  48.6 0.7 %norm.1 = bf16[4,1024]{1,0:T(4,128)(2,1)} custom-call(f32[8,4,4,128]{3,2,1,0:T(4,128)S(1)} %bitcast.17), custom_call_target="tpu_custom_call" | custom-call | tf_op jit(solution)/shard_map/norm/pallas_call | solution.py:298
Async XLA Ops:
  0.0 29.2 %copy-start = (s32[512]{0:T(512)S(1)}, s32[512]{0:T(512)}, u32[]{:S(2)}) copy-start(s32[512]{0:T(512)} %param.10) | copy-start | bytes 6148
  0.0 29.2 %copy-start.2 = (s32[512]{0:T(512)S(1)}, s32[512]{0:T(512)}, u32[]{:S(2)}) copy-start(s32[512]{0:T(512)} %param.9) | copy-start | bytes 6148
  0.0 35.9 %copy-start.1 = (f32[1024]{0:T(1024)S(1)}, f32[1024]{0:T(1024)}, u32[]{:S(2)}) copy-start(f32[1024]{0:T(1024)} %param.11) | copy-start | bytes 12292
  16.4 19.4 %all-to-all-start.2 = ((f32[48,4,128]{2,1,0:T(4,128)}), f32[48,4,128]{2,1,0:T(4,128)S(1)}, u32[]{:S(2)}, u32[]{:S(2)}) async-start(f32[48,4,128]{2,1,0:T(4,128)} %bitcast.12), calls=%async_computation.2 | async-start | bytes 196608 | tf_op jit(solution)/shard_map/all_to_all | solution.py:307

commit v16 on v15

--- a/solution.py
+++ b/solution.py
@@ -23,7 +23,7 @@
 
 
 def plane_place(z):
-    return (z + 6 + lax.axis_index("c")) & 15
+    return (z + 5 + lax.axis_index("c")) & 15
 
 
 def slice_place():
@@ -31,7 +31,7 @@
 
 
 CHUNK_GROUP = [[(((j >> 1) + 2) & 3) * 2 + (j & 1) ^ 1 for j in range(8)]]
-PLANE_GROUP = [[((j + 10 - c) & 15) * 2 + c for j in range(16)] for c in range(2)]
+PLANE_GROUP = [[((j + 11 - c) & 15) * 2 + c for j in range(16)] for c in range(2)]
 OWNER_GROUP = [[((j & ~3) ^ 4) + ((j + 2) & 3) for j in range(32)]]
 
 

time: 49.6 us -> 49.5 us (level)
  blocking collectives: 25.8 us -> 26.9 us
  starting transfers between devices: 12.7 us -> 11.8 us
    all_to_all x2, blocking collectives: 25.8 us -> 26.9 us  [swap(): lax.all_to_all(array, axes, split_axis=0, concat_axis=0, tiled=True, axis...]
    all_to_all x1, starting transfers between devices: 12.7 us -> 11.8 us  [swap(): lax.all_to_all(array, axes, split_axis=0, concat_axis=0, tiled=True, axis...]
where the time goes in v16:
time: 49.5 us; the launch traced here: 49.2 us
  blocking collectives  26.9 us (54%)
  starting transfers between devices  11.8 us (24%)
  Pallas kernels  5.08 us (10%)
  waiting for transfers between devices  4.74 us (10%)
  between operations  0.69 us (1%)
    all_to_all x2, blocking collectives, swap(): lax.all_to_all(array, axes, split_axis=0, concat_axis=0, tiled=True, axis...  26.9 us
    all_to_all x1, starting transfers between devices, swap(): lax.all_to_all(array, axes, split_axis=0, concat_axis=0, tiled=True, axis...  11.8 us
    all_to_all x1, waiting for transfers between devices, swap(): lax.all_to_all(array, axes, split_axis=0, concat_axis=0, tiled=True, axis...  4.74 us
    pallas_call x1, Pallas kernels, local_sums(): pl.pallas_call(functools.partial(sums_kernel, pieces), in_specs=[pl.Block...  2.1 us
    pallas_call x1, Pallas kernels, crowded(): pl.pallas_call(functools.partial(crowded_kernel, tokens), out_specs=pl.Bl...  1.02 us
  transfers between devices with their start and end apart: 1, of which 1 were waited for; matrix products, arithmetic and copies ran while one was open for 0% of the time, Pallas kernels for 2%

profile of v16, /device:TPU:1, one launch (start us, length us, event | category | flops | bytes accessed | tf_op | source)
XLA Modules:
  0.0 49.2 jit_solution(15107811469843069857)
XLA Ops:
  0.0 0.0 copy-start
  0.0 0.0 copy-start.2
  0.0 0.0 copy-start.1
  0.0 2.1 %local_sums.1 = f32[160,128]{1,0:T(8,128)S(1)} custom-call(s32[1,1024]{1,0:T(1,128)} %bitcast.32, s32[1,512]{1,0:T(1,128)} %bitcast.23, bf16[1024,1024]{1,0:T(8,128)(2,1)} %hidden_hbm.1), custom_call_target="tpu_custom_call" | custom-call | tf_op jit(solution)/shard_map/local_sums/pallas_call | solution.py:139
  2.1 13.3 %all_to_all.20 = f32[40,4,128]{2,1,0:T(4,128)S(1)} all-to-all(f32[40,4,128]{2,1,0:T(4,128)S(1)} %bitcast.16), channel_id=1, replica_groups={{260,256,388,384,4,0,132,128},{261,257,389,385,5,1,133,129},{262,258,39..., dimensions={0} | all-to-all | bytes 163840 | tf_op jit(solution)/shard_map/all_to_all | solution.py:307
  15.5 1.0 %place.1 = (f32[192,128]{1,0:T(8,128)}, s32[8,128]{1,0:T(8,128)S(1)}) custom-call(f32[160,128]{1,0:T(8,128)S(1)} %bitcast.20), custom_call_target="tpu_custom_call" | custom-call | tf_op jit(solution)/shard_map/place/pallas_call | solution.py:187
  16.4 11.8 %all-to-all-start.2 = ((f32[48,4,128]{2,1,0:T(4,128)}), f32[48,4,128]{2,1,0:T(4,128)S(1)}, u32[]{:S(2)}, u32[]{:S(2)}) async-start(f32[48,4,128]{2,1,0:T(4,128)} %bitcast.12), calls=%async_computation.2 | async-start | bytes 196608 | tf_op jit(solution)/shard_map/all_to_all | solution.py:307
  28.3 0.0 copy-done
  28.3 0.0 copy-done.2
  28.3 1.0 %crowded.1 = s32[1]{0:T(128)} custom-call(s32[8,128]{1,0:T(8,128)S(1)} %get-tuple-element.37.ready_ref, s32[1,512]{1,0:T(1,128)S(1)} %bitcast.24, s32[1,512]{1,0:T(1,128)S(1)} %bitcast.29), custom_call_target="tpu_custom_call" | custom-call | flops 16777216 | bytes 4096 | tf_op jit(solution)/shard_map/crowded/pallas_call | solution.py:209
  30.0 4.7 %all-to-all-done.2 = f32[48,4,128]{2,1,0:T(4,128)S(1)} async-done(((f32[48,4,128]{2,1,0:T(4,128)}), f32[48,4,128]{2,1,0:T(4,128)S(1)}, u32[]{:S(2)}, u32[]{:S(2)}) %all-to-all-start.2) | async-done | bytes 98336 | tf_op jit(solution)/shard_map/all_to_all | solution.py:307
  34.7 0.0 copy-done.1
  34.7 0.3 conditional.1
  34.7 0.3 average.2
  35.0 13.5 %all_to_all.21 = f32[32,4,128]{2,1,0:T(4,128)S(1)} all-to-all(f32[32,4,128]{2,1,0:T(4,128)S(1)} %bitcast.22), channel_id=1, replica_groups={{6,7,4,5,2,3,0,1,134,135,132,133,130,131,128,129,262,263,260,261,258,25..., dimensions={0} | all-to-all | bytes 131072 | tf_op jit(solution)/shard_map/all_to_all | solution.py:307
  48.5 0.7 %norm.1 = bf16[4,1024]{1,0:T(4,128)(2,1)} custom-call(f32[8,4,4,128]{3,2,1,0:T(4,128)S(1)} %bitcast.17), custom_call_target="tpu_custom_call" | custom-call | tf_op jit(solution)/shard_map/norm/pallas_call | solution.py:298
Async XLA Ops:
  0.0 28.3 %copy-start = (s32[512]{0:T(512)S(1)}, s32[512]{0:T(512)}, u32[]{:S(2)}) copy-start(s32[512]{0:T(512)} %param.10) | copy-start | bytes 6148
  0.0 28.3 %copy-start.2 = (s32[512]{0:T(512)S(1)}, s32[512]{0:T(512)}, u32[]{:S(2)}) copy-start(s32[512]{0:T(512)} %param.9) | copy-start | bytes 6148
  0.0 34.7 %copy-start.1 = (f32[1024]{0:T(1024)S(1)}, f32[1024]{0:T(1024)}, u32[]{:S(2)}) copy-start(f32[1024]{0:T(1024)} %param.11) | copy-start | bytes 12292
  16.4 18.3 %all-to-all-start.2 = ((f32[48,4,128]{2,1,0:T(4,128)}), f32[48,4,128]{2,1,0:T(4,128)S(1)}, u32[]{:S(2)}, u32[]{:S(2)}) async-start(f32[48,4,128]{2,1,0:T(4,128)} %bitcast.12), calls=%async_computation.2 | async-start | bytes 196608 | tf_op jit(solution)/shard_map/all_to_all | solution.py:307

commit v17 on v14

--- a/solution.py
+++ b/solution.py
@@ -154,19 +154,17 @@
 
 def slots_of(in_ref):
     count = in_ref.shape[0]
-    values = in_ref[...]
-    empty = jnp.zeros((2 * LANES - count, LANES), jnp.float32)
     marks = in_ref[SLOTS - 2 : SLOTS, :]
     for row in range(2 * SLOTS, count + SLOTS, SLOTS):
         marks = marks + in_ref[row - 2 : row, :]
     marks = marks.astype(jnp.int32)
-    where = jnp.concatenate([marks[0:1, :], marks[1:2, :]], axis=1)
+    where = jnp.concatenate([marks[0:1, :], marks[1:2, : count - LANES]], axis=1)
     plane = jnp.where(where > 0, (where - 1) >> 5, -1)
-    bound = iota((16, 2 * LANES), 0) == plane
-    ahead = iota((2 * LANES, 2 * LANES), 0) < iota((2 * LANES, 2 * LANES), 1)
+    bound = iota((16, count), 0) == plane
+    ahead = iota((count, count), 0) < iota((count, count), 1)
     seen = dot(ones(bound), ones(ahead))
     rank = jnp.sum(jnp.where(bound, seen, 0.0), axis=0, keepdims=True).astype(jnp.int32)
-    return jnp.concatenate([values, empty], axis=0), where, plane, bound, rank
+    return in_ref[...], where, plane, bound, rank
 
 
 def place_kernel(in_ref, out_ref, ready_ref):
@@ -174,9 +172,9 @@
     ready_ref[...] = jnp.zeros_like(ready_ref)
     values, where, plane, bound, rank = slots_of(in_ref)
     target = jnp.where((where > 0) & (rank < FIT), plane * ROWS + rank, -1)
-    out_ref[...] = picked(ones(iota((planes * ROWS, 2 * LANES), 0) == target), values)
+    out_ref[...] = picked(ones(iota((planes * ROWS, where.shape[1]), 0) == target), values)
     number = (((where - 1) & 31) + 1) * jnp.where((rank & 1) == 1, 64, 1)
-    lane = iota((LANES, 2 * LANES), 0) - plane_place(lax.axis_index("z")) * PAIRS
+    lane = iota((LANES, where.shape[1]), 0) - plane_place(lax.axis_index("z")) * PAIRS
     numbers = dot_rows(small(jnp.where(bound, number, 0)), ones((lane == rank >> 1) & (rank < FIT)))
     for p in range(planes):
         out_ref[p * ROWS + FIT : (p + 1) * ROWS, :] = numbers[p : p + 1, :]
@@ -220,7 +218,7 @@
 def place_rest_kernel(in_ref, out_ref):
     planes, per_plane, _ = out_ref.shape
     values, where, _, _, rank = slots_of(in_ref)
-    row = iota((planes * per_plane, 2 * LANES), 0) + 1
+    row = iota((planes * per_plane, where.shape[1]), 0) + 1
     out_ref[...] = picked(ones((row == where) & (rank >= FIT)), values).reshape(out_ref.shape)
 
 

time: 49.5 us -> 49.5 us (level)
  no operation moved by 1% of the time
where the time goes in v17:
time: 49.5 us; the launch traced here: 49.2 us
  blocking collectives  26.8 us (54%)
  starting transfers between devices  11.8 us (24%)
  Pallas kernels  5.07 us (10%)
  waiting for transfers between devices  4.8 us (10%)
  between operations  0.69 us (1%)
    all_to_all x2, blocking collectives, swap(): lax.all_to_all(array, axes, split_axis=0, concat_axis=0, tiled=True, axis...  26.8 us
    all_to_all x1, starting transfers between devices, swap(): lax.all_to_all(array, axes, split_axis=0, concat_axis=0, tiled=True, axis...  11.8 us
    all_to_all x1, waiting for transfers between devices, swap(): lax.all_to_all(array, axes, split_axis=0, concat_axis=0, tiled=True, axis...  4.8 us
    pallas_call x1, Pallas kernels, local_sums(): pl.pallas_call(functools.partial(sums_kernel, pieces), in_specs=[pl.Block...  2.1 us
    pallas_call x1, Pallas kernels, crowded(): pl.pallas_call(functools.partial(crowded_kernel, tokens), out_specs=pl.Bl...  1.02 us
  transfers between devices with their start and end apart: 1, of which 1 were waited for; matrix products, arithmetic and copies ran while one was open for 0% of the time, Pallas kernels for 2%

profile of v17, /device:TPU:1, one launch (start us, length us, event | category | flops | bytes accessed | tf_op | source)
XLA Modules:
  0.0 49.2 jit_solution(8208218225911781288)
XLA Ops:
  0.0 0.0 copy-start
  0.0 0.0 copy-start.2
  0.0 0.0 copy-start.1
  0.0 2.1 %local_sums.1 = f32[160,128]{1,0:T(8,128)S(1)} custom-call(s32[1,1024]{1,0:T(1,128)} %bitcast.32, s32[1,512]{1,0:T(1,128)} %bitcast.23, bf16[1024,1024]{1,0:T(8,128)(2,1)} %hidden_hbm.1), custom_call_target="tpu_custom_call" | custom-call | tf_op jit(solution)/shard_map/local_sums/pallas_call | solution.py:139
  2.1 13.3 %all_to_all.20 = f32[40,4,128]{2,1,0:T(4,128)S(1)} all-to-all(f32[40,4,128]{2,1,0:T(4,128)S(1)} %bitcast.16), channel_id=1, replica_groups={{260,256,388,384,4,0,132,128},{261,257,389,385,5,1,133,129},{262,258,39..., dimensions={0} | all-to-all | bytes 163840 | tf_op jit(solution)/shard_map/all_to_all | solution.py:304
  15.5 1.0 %place.1 = (f32[192,128]{1,0:T(8,128)}, s32[8,128]{1,0:T(8,128)S(1)}) custom-call(f32[160,128]{1,0:T(8,128)S(1)} %bitcast.20), custom_call_target="tpu_custom_call" | custom-call | tf_op jit(solution)/shard_map/place/pallas_call | solution.py:184
  16.4 11.8 %all-to-all-start.2 = ((f32[48,4,128]{2,1,0:T(4,128)}), f32[48,4,128]{2,1,0:T(4,128)S(1)}, u32[]{:S(2)}, u32[]{:S(2)}) async-start(f32[48,4,128]{2,1,0:T(4,128)} %bitcast.12), calls=%async_computation.2 | async-start | bytes 196608 | tf_op jit(solution)/shard_map/all_to_all | solution.py:304
  28.3 0.0 copy-done
  28.3 0.0 copy-done.2
  28.3 1.0 %crowded.1 = s32[1]{0:T(128)} custom-call(s32[8,128]{1,0:T(8,128)S(1)} %get-tuple-element.37.ready_ref, s32[1,512]{1,0:T(1,128)S(1)} %bitcast.24, s32[1,512]{1,0:T(1,128)S(1)} %bitcast.29), custom_call_target="tpu_custom_call" | custom-call | flops 16777216 | bytes 4096 | tf_op jit(solution)/shard_map/crowded/pallas_call | solution.py:206
  30.0 4.8 %all-to-all-done.2 = f32[48,4,128]{2,1,0:T(4,128)S(1)} async-done(((f32[48,4,128]{2,1,0:T(4,128)}), f32[48,4,128]{2,1,0:T(4,128)S(1)}, u32[]{:S(2)}, u32[]{:S(2)}) %all-to-all-start.2) | async-done | bytes 98336 | tf_op jit(solution)/shard_map/all_to_all | solution.py:304
  34.8 0.0 copy-done.1
  34.8 0.3 conditional.1
  34.8 0.3 average.2
  35.0 13.5 %all_to_all.21 = f32[32,4,128]{2,1,0:T(4,128)S(1)} all-to-all(f32[32,4,128]{2,1,0:T(4,128)S(1)} %bitcast.22), channel_id=1, replica_groups={{6,7,4,5,2,3,0,1,134,135,132,133,130,131,128,129,262,263,260,261,258,25..., dimensions={0} | all-to-all | bytes 131072 | tf_op jit(solution)/shard_map/all_to_all | solution.py:304
  48.5 0.7 %norm.1 = bf16[4,1024]{1,0:T(4,128)(2,1)} custom-call(f32[8,4,4,128]{3,2,1,0:T(4,128)S(1)} %bitcast.17), custom_call_target="tpu_custom_call" | custom-call | tf_op jit(solution)/shard_map/norm/pallas_call | solution.py:295
Async XLA Ops:
  0.0 28.3 %copy-start = (s32[512]{0:T(512)S(1)}, s32[512]{0:T(512)}, u32[]{:S(2)}) copy-start(s32[512]{0:T(512)} %param.10) | copy-start | bytes 6148
  0.0 28.3 %copy-start.2 = (s32[512]{0:T(512)S(1)}, s32[512]{0:T(512)}, u32[]{:S(2)}) copy-start(s32[512]{0:T(512)} %param.9) | copy-start | bytes 6148
  0.0 34.8 %copy-start.1 = (f32[1024]{0:T(1024)S(1)}, f32[1024]{0:T(1024)}, u32[]{:S(2)}) copy-start(f32[1024]{0:T(1024)} %param.11) | copy-start | bytes 12292
  16.4 18.3 %all-to-all-start.2 = ((f32[48,4,128]{2,1,0:T(4,128)}), f32[48,4,128]{2,1,0:T(4,128)S(1)}, u32[]{:S(2)}, u32[]{:S(2)}) async-start(f32[48,4,128]{2,1,0:T(4,128)} %bitcast.12), calls=%async_computation.2 | async-start | bytes 196608 | tf_op jit(solution)/shard_map/all_to_all | solution.py:304

commit v18 on v17

--- a/solution.py
+++ b/solution.py
@@ -32,7 +32,7 @@
 
 CHUNK_GROUP = [[(((j >> 1) + 2) & 3) * 2 + (j & 1) ^ 1 for j in range(8)]]
 PLANE_GROUP = [[(j + 10) & 15 for j in range(16)]]
-OWNER_GROUP = [[((j & ~3) ^ 4) + ((j + 2) & 3) for j in range(32)]]
+OWNER_GROUP = [[(j & ~3) + ((j + 2) & 3) for j in range(32)]]
 
 
 def plane_row(owner):
@@ -265,7 +265,7 @@
     owners, copies, rows, _ = out_ref.shape
     for o in range(owners):
         for y in range(copies):
-            out_ref[o ^ 1, y] = average[o * rows : (o + 1) * rows, :]
+            out_ref[o, y] = average[o * rows : (o + 1) * rows, :]
 
 
 def averages_for_owners(arrived, owner_slot, lengths, pool_bias, owners, copies, *rest):
@@ -286,7 +286,7 @@
     scale = lax.rsqrt(energy + 1e-06)
     mine = slice_place()
     for c, device in enumerate(CHUNK_GROUP[0]):
-        values = in_ref[device ^ 1, mine] * scale
+        values = in_ref[device, mine] * scale
         out_ref[:, c * LANES : (c + 1) * LANES] = values.astype(jnp.bfloat16)
 
 

time: 49.5 us -> 49.7 us (level)
  no operation moved by 1% of the time
where the time goes in v18:
time: 49.7 us; the launch traced here: 49.5 us
  blocking collectives  27.1 us (55%)
  starting transfers between devices  11.8 us (24%)
  Pallas kernels  5.07 us (10%)
  waiting for transfers between devices  4.8 us (10%)
  between operations  0.69 us (1%)
    all_to_all x2, blocking collectives, swap(): lax.all_to_all(array, axes, split_axis=0, concat_axis=0, tiled=True, axis...  27.1 us
    all_to_all x1, starting transfers between devices, swap(): lax.all_to_all(array, axes, split_axis=0, concat_axis=0, tiled=True, axis...  11.8 us
    all_to_all x1, waiting for transfers between devices, swap(): lax.all_to_all(array, axes, split_axis=0, concat_axis=0, tiled=True, axis...  4.8 us
    pallas_call x1, Pallas kernels, local_sums(): pl.pallas_call(functools.partial(sums_kernel, pieces), in_specs=[pl.Block...  2.1 us
    pallas_call x1, Pallas kernels, crowded(): pl.pallas_call(functools.partial(crowded_kernel, tokens), out_specs=pl.Bl...  1.02 us
  transfers between devices with their start and end apart: 1, of which 1 were waited for; matrix products, arithmetic and copies ran while one was open for 0% of the time, Pallas kernels for 2%

profile of v18, /device:TPU:1, one launch (start us, length us, event | category | flops | bytes accessed | tf_op | source)
XLA Modules:
  0.0 49.5 jit_solution(13337511574703588722)
XLA Ops:
  0.0 0.0 copy-start
  0.0 0.0 copy-start.2
  0.0 0.0 copy-start.1
  0.0 2.1 %local_sums.1 = f32[160,128]{1,0:T(8,128)S(1)} custom-call(s32[1,1024]{1,0:T(1,128)} %bitcast.32, s32[1,512]{1,0:T(1,128)} %bitcast.23, bf16[1024,1024]{1,0:T(8,128)(2,1)} %hidden_hbm.1), custom_call_target="tpu_custom_call" | custom-call | tf_op jit(solution)/shard_map/local_sums/pallas_call | solution.py:139
  2.1 13.3 %all_to_all.20 = f32[40,4,128]{2,1,0:T(4,128)S(1)} all-to-all(f32[40,4,128]{2,1,0:T(4,128)S(1)} %bitcast.16), channel_id=1, replica_groups={{260,256,388,384,4,0,132,128},{261,257,389,385,5,1,133,129},{262,258,39..., dimensions={0} | all-to-all | bytes 163840 | tf_op jit(solution)/shard_map/all_to_all | solution.py:304
  15.5 1.0 %place.1 = (f32[192,128]{1,0:T(8,128)}, s32[8,128]{1,0:T(8,128)S(1)}) custom-call(f32[160,128]{1,0:T(8,128)S(1)} %bitcast.20), custom_call_target="tpu_custom_call" | custom-call | tf_op jit(solution)/shard_map/place/pallas_call | solution.py:184
  16.4 11.8 %all-to-all-start.2 = ((f32[48,4,128]{2,1,0:T(4,128)}), f32[48,4,128]{2,1,0:T(4,128)S(1)}, u32[]{:S(2)}, u32[]{:S(2)}) async-start(f32[48,4,128]{2,1,0:T(4,128)} %bitcast.12), calls=%async_computation.2 | async-start | bytes 196608 | tf_op jit(solution)/shard_map/all_to_all | solution.py:304
  28.3 0.0 copy-done
  28.3 0.0 copy-done.2
  28.3 1.0 %crowded.1 = s32[1]{0:T(128)} custom-call(s32[8,128]{1,0:T(8,128)S(1)} %get-tuple-element.37.ready_ref, s32[1,512]{1,0:T(1,128)S(1)} %bitcast.24, s32[1,512]{1,0:T(1,128)S(1)} %bitcast.29), custom_call_target="tpu_custom_call" | custom-call | flops 16777216 | bytes 4096 | tf_op jit(solution)/shard_map/crowded/pallas_call | solution.py:206
  30.0 4.8 %all-to-all-done.2 = f32[48,4,128]{2,1,0:T(4,128)S(1)} async-done(((f32[48,4,128]{2,1,0:T(4,128)}), f32[48,4,128]{2,1,0:T(4,128)S(1)}, u32[]{:S(2)}, u32[]{:S(2)}) %all-to-all-start.2) | async-done | bytes 98336 | tf_op jit(solution)/shard_map/all_to_all | solution.py:304
  34.8 0.0 copy-done.1
  34.8 0.3 conditional.1
  34.8 0.3 average.2
  35.0 13.7 %all_to_all.21 = f32[32,4,128]{2,1,0:T(4,128)S(1)} all-to-all(f32[32,4,128]{2,1,0:T(4,128)S(1)} %bitcast.22), channel_id=1, replica_groups={{2,3,0,1,6,7,4,5,130,131,128,129,134,135,132,133,258,259,256,257,262,26..., dimensions={0} | all-to-all | bytes 131072 | tf_op jit(solution)/shard_map/all_to_all | solution.py:304
  48.8 0.7 %norm.1 = bf16[4,1024]{1,0:T(4,128)(2,1)} custom-call(f32[8,4,4,128]{3,2,1,0:T(4,128)S(1)} %bitcast.17), custom_call_target="tpu_custom_call" | custom-call | tf_op jit(solution)/shard_map/norm/pallas_call | solution.py:295
Async XLA Ops:
  0.0 28.3 %copy-start = (s32[512]{0:T(512)S(1)}, s32[512]{0:T(512)}, u32[]{:S(2)}) copy-start(s32[512]{0:T(512)} %param.10) | copy-start | bytes 6148
  0.0 28.3 %copy-start.2 = (s32[512]{0:T(512)S(1)}, s32[512]{0:T(512)}, u32[]{:S(2)}) copy-start(s32[512]{0:T(512)} %param.9) | copy-start | bytes 6148
  0.0 34.8 %copy-start.1 = (f32[1024]{0:T(1024)S(1)}, f32[1024]{0:T(1024)}, u32[]{:S(2)}) copy-start(f32[1024]{0:T(1024)} %param.11) | copy-start | bytes 12292
  16.4 18.3 %all-to-all-start.2 = ((f32[48,4,128]{2,1,0:T(4,128)}), f32[48,4,128]{2,1,0:T(4,128)S(1)}, u32[]{:S(2)}, u32[]{:S(2)}) async-start(f32[48,4,128]{2,1,0:T(4,128)} %bitcast.12), calls=%async_computation.2 | async-start | bytes 196608 | tf_op jit(solution)/shard_map/all_to_all | solution.py:304

commit v19 on v18

--- a/solution.py
+++ b/solution.py
@@ -27,12 +27,12 @@
 
 
 def slice_place():
-    return (lax.axis_index("y") + 2) & 3
+    return lax.axis_index("y")
 
 
 CHUNK_GROUP = [[(((j >> 1) + 2) & 3) * 2 + (j & 1) ^ 1 for j in range(8)]]
 PLANE_GROUP = [[(j + 10) & 15 for j in range(16)]]
-OWNER_GROUP = [[(j & ~3) + ((j + 2) & 3) for j in range(32)]]
+OWNER_GROUP = [[j ^ 20 for j in range(32)]]
 
 
 def plane_row(owner):
@@ -265,7 +265,7 @@
     owners, copies, rows, _ = out_ref.shape
     for o in range(owners):
         for y in range(copies):
-            out_ref[o, y] = average[o * rows : (o + 1) * rows, :]
+            out_ref[o ^ 5, y] = average[o * rows : (o + 1) * rows, :]
 
 
 def averages_for_owners(arrived, owner_slot, lengths, pool_bias, owners, copies, *rest):
@@ -286,7 +286,7 @@
     scale = lax.rsqrt(energy + 1e-06)
     mine = slice_place()
     for c, device in enumerate(CHUNK_GROUP[0]):
-        values = in_ref[device, mine] * scale
+        values = in_ref[device ^ 5, mine] * scale
         out_ref[:, c * LANES : (c + 1) * LANES] = values.astype(jnp.bfloat16)
 
 

time: 49.7 us -> 49.6 us (level)
  no operation moved by 1% of the time
where the time goes in v19:
time: 49.6 us; the launch traced here: 49.3 us
  blocking collectives  26.9 us (54%)
  starting transfers between devices  11.8 us (24%)
  Pallas kernels  5.07 us (10%)
  waiting for transfers between devices  4.8 us (10%)
  between operations  0.69 us (1%)
    all_to_all x2, blocking collectives, swap(): lax.all_to_all(array, axes, split_axis=0, concat_axis=0, tiled=True, axis...  26.9 us
    all_to_all x1, starting transfers between devices, swap(): lax.all_to_all(array, axes, split_axis=0, concat_axis=0, tiled=True, axis...  11.8 us
    all_to_all x1, waiting for transfers between devices, swap(): lax.all_to_all(array, axes, split_axis=0, concat_axis=0, tiled=True, axis...  4.8 us
    pallas_call x1, Pallas kernels, local_sums(): pl.pallas_call(functools.partial(sums_kernel, pieces), in_specs=[pl.Block...  2.1 us
    pallas_call x1, Pallas kernels, crowded(): pl.pallas_call(functools.partial(crowded_kernel, tokens), out_specs=pl.Bl...  1.02 us
  transfers between devices with their start and end apart: 1, of which 1 were waited for; matrix products, arithmetic and copies ran while one was open for 0% of the time, Pallas kernels for 2%

profile of v19, /device:TPU:1, one launch (start us, length us, event | category | flops | bytes accessed | tf_op | source)
XLA Modules:
  0.0 49.3 jit_solution(6777383639622031411)
XLA Ops:
  0.0 0.0 copy-start
  0.0 0.0 copy-start.2
  0.0 0.0 copy-start.1
  0.0 2.1 %local_sums.1 = f32[160,128]{1,0:T(8,128)S(1)} custom-call(s32[1,1024]{1,0:T(1,128)} %bitcast.32, s32[1,512]{1,0:T(1,128)} %bitcast.23, bf16[1024,1024]{1,0:T(8,128)(2,1)} %hidden_hbm.1), custom_call_target="tpu_custom_call" | custom-call | tf_op jit(solution)/shard_map/local_sums/pallas_call | solution.py:139
  2.1 13.3 %all_to_all.20 = f32[40,4,128]{2,1,0:T(4,128)S(1)} all-to-all(f32[40,4,128]{2,1,0:T(4,128)S(1)} %bitcast.16), channel_id=1, replica_groups={{260,256,388,384,4,0,132,128},{261,257,389,385,5,1,133,129},{262,258,39..., dimensions={0} | all-to-all | bytes 163840 | tf_op jit(solution)/shard_map/all_to_all | solution.py:304
  15.5 1.0 %place.1 = (f32[192,128]{1,0:T(8,128)}, s32[8,128]{1,0:T(8,128)S(1)}) custom-call(f32[160,128]{1,0:T(8,128)S(1)} %bitcast.20), custom_call_target="tpu_custom_call" | custom-call | tf_op jit(solution)/shard_map/place/pallas_call | solution.py:184
  16.4 11.8 %all-to-all-start.2 = ((f32[48,4,128]{2,1,0:T(4,128)}), f32[48,4,128]{2,1,0:T(4,128)S(1)}, u32[]{:S(2)}, u32[]{:S(2)}) async-start(f32[48,4,128]{2,1,0:T(4,128)} %bitcast.12), calls=%async_computation.2 | async-start | bytes 196608 | tf_op jit(solution)/shard_map/all_to_all | solution.py:304
  28.3 0.0 copy-done
  28.3 0.0 copy-done.2
  28.3 1.0 %crowded.1 = s32[1]{0:T(128)} custom-call(s32[8,128]{1,0:T(8,128)S(1)} %get-tuple-element.37.ready_ref, s32[1,512]{1,0:T(1,128)S(1)} %bitcast.24, s32[1,512]{1,0:T(1,128)S(1)} %bitcast.29), custom_call_target="tpu_custom_call" | custom-call | flops 16777216 | bytes 4096 | tf_op jit(solution)/shard_map/crowded/pallas_call | solution.py:206
  30.0 4.8 %all-to-all-done.2 = f32[48,4,128]{2,1,0:T(4,128)S(1)} async-done(((f32[48,4,128]{2,1,0:T(4,128)}), f32[48,4,128]{2,1,0:T(4,128)S(1)}, u32[]{:S(2)}, u32[]{:S(2)}) %all-to-all-start.2) | async-done | bytes 98336 | tf_op jit(solution)/shard_map/all_to_all | solution.py:304
  34.8 0.0 copy-done.1
  34.8 0.3 conditional.1
  34.8 0.3 average.2
  35.0 13.5 %all_to_all.21 = f32[32,4,128]{2,1,0:T(4,128)S(1)} all-to-all(f32[32,4,128]{2,1,0:T(4,128)S(1)} %bitcast.22), channel_id=1, replica_groups={{260,261,262,263,256,257,258,259,388,389,390,391,384,385,386,387,4,5,6,..., dimensions={0} | all-to-all | bytes 131072 | tf_op jit(solution)/shard_map/all_to_all | solution.py:304
  48.6 0.7 %norm.1 = bf16[4,1024]{1,0:T(4,128)(2,1)} custom-call(f32[8,4,4,128]{3,2,1,0:T(4,128)S(1)} %bitcast.17), custom_call_target="tpu_custom_call" | custom-call | tf_op jit(solution)/shard_map/norm/pallas_call | solution.py:295
Async XLA Ops:
  0.0 28.3 %copy-start = (s32[512]{0:T(512)S(1)}, s32[512]{0:T(512)}, u32[]{:S(2)}) copy-start(s32[512]{0:T(512)} %param.10) | copy-start | bytes 6148
  0.0 28.3 %copy-start.2 = (s32[512]{0:T(512)S(1)}, s32[512]{0:T(512)}, u32[]{:S(2)}) copy-start(s32[512]{0:T(512)} %param.9) | copy-start | bytes 6148
  0.0 34.8 %copy-start.1 = (f32[1024]{0:T(1024)S(1)}, f32[1024]{0:T(1024)}, u32[]{:S(2)}) copy-start(f32[1024]{0:T(1024)} %param.11) | copy-start | bytes 12292
  16.4 18.3 %all-to-all-start.2 = ((f32[48,4,128]{2,1,0:T(4,128)}), f32[48,4,128]{2,1,0:T(4,128)S(1)}, u32[]{:S(2)}, u32[]{:S(2)}) async-start(f32[48,4,128]{2,1,0:T(4,128)} %bitcast.12), calls=%async_computation.2 | async-start | bytes 196608 | tf_op jit(solution)/shard_map/all_to_all | solution.py:304
